TPU v7x, 32 devices: a whole 2x2x4 slice. The times are simulated.
32 devices in a mesh: fsdp: 2 (over y), ctx: 4 (over x, core), tp: 4 (over z).
Axes of the slice: x: 2, y: 2, z: 4, core: 2. Of those that a mesh axis runs over, the one named last changes fastest.
Arguments:
- block_input: bfloat16 [4, 2048, 1024], P('fsdp', 'ctx'), may hold values from -6 to 6
- positions: int32 [3, 4, 2048], P(None, 'fsdp', 'ctx'), may hold values from 0 to 15
- w_qkv: bfloat16 [3, 1024, 1024], P(None, 'fsdp', 'tp'), may hold values from -0.1875 to 0.1875
- b_qkv: float32 [3, 1024], P(None, 'tp'), may hold values from -3 to 3
- w_proj: bfloat16 [1024, 1024], P('tp', 'fsdp'), may hold values from -1 to 1
- w_up: bfloat16 [1024, 4096], P('fsdp', 'tp'), may hold values from -0.1875 to 0.1875
- b_up: float32 [4096], P('tp'), may hold values from -3 to 3
- w_down: bfloat16 [4096, 1024], P('tp', 'fsdp'), may hold values from -0.09375 to 0.09375
- norm_gains: float32 [2, 1024], replicated, may hold values from 0.5 to 1.5
- norm_shifts: float32 [2, 1024], replicated, may hold values from -2 to 2
- out_shifts: float32 [2, 1024], replicated, may hold values from -2 to 2
- grad_out: bfloat16 [4, 2048, 1024], P('fsdp', 'ctx'), may hold values from -6 to 6
Outputs:
- block_output: bfloat16 [4, 2048, 1024], P('fsdp', 'ctx')
- grad_input: float32 [4, 2048, 1024], P('fsdp', 'ctx')
- grad_w_qkv: float32 [3, 1024, 1024], P(None, 'fsdp', 'tp')
- grad_b_qkv: float32 [3, 1024], P(None, 'tp')
- grad_w_proj: float32 [1024, 1024], P('tp', 'fsdp')
- grad_w_up: float32 [1024, 4096], P('fsdp', 'tp')
- grad_b_up: float32 [4096], P('tp')
- grad_w_down: float32 [4096, 1024], P('tp', 'fsdp')
- grad_gains: float32 [2, 1024], replicated
- grad_shifts: float32 [2, 1024], replicated
- grad_out_shifts: float32 [2, 1024], replicated
Inputs may be any that keep to these rules, and one draw needn't show every extreme that they name: `positions`: each token's time, height and width index in its clip.
All inputs are finite; a program needn't handle non-finite values.
Results may differ from a plain program's by a relative error of at most 0.02.
Values may be sent and summed in bfloat16 or wider, within the bound.
A program may use at most 128 MiB of HBM per device.

v0:
```python
from functools import partial

import jax
import jax.numpy as jnp
from jax import lax
from jax.sharding import PartitionSpec as P

HD = 64
LEN = 2048
ROT = 20
QBLK = 512


EPSILON = 1e-06


def layer_norm(values, gain_vec, shift_vec):
    center = values - jnp.mean(values, axis=-1, keepdims=True)
    spread = jnp.mean(center * center, axis=-1, keepdims=True)
    return center * lax.rsqrt(spread + EPSILON) * gain_vec + shift_vec


def rotary_tables(position_rows):
    half_rot = ROT // 2
    freqs = 10000.0 ** (-2.0 * jnp.arange(half_rot, dtype=jnp.float32) / ROT)
    angles = position_rows.astype(jnp.float32)[:, :, None] * freqs[None, None, :]
    return (jnp.cos(angles), jnp.sin(angles))


def rotary(values, cos_table, sin_table):
    half_rot = ROT // 2
    pieces = []
    for dim_index in range(3):
        offset_at = dim_index * ROT
        first_half = values[..., offset_at : offset_at + half_rot]
        second_half = values[..., offset_at + half_rot : offset_at + ROT]
        cos_part = cos_table[dim_index][:, None, :]
        sin_part = sin_table[dim_index][:, None, :]
        pieces.append(first_half * cos_part - second_half * sin_part)
        pieces.append(second_half * cos_part + first_half * sin_part)
    pieces.append(values[..., 3 * ROT :])
    return jnp.concatenate(pieces, axis=-1)


def contract_rows(left_mat, right_mat):
    return lax.dot_general(
        left_mat, right_mat, (((0,), (0,)), ((), ())), preferred_element_type=jnp.float32
    )


def contract_cols(left_mat, right_mat):
    return lax.dot_general(
        left_mat, right_mat, (((1,), (1,)), ((), ())), preferred_element_type=jnp.float32
    )


def tp_whole(partial_sum):
    return lax.psum(partial_sum.astype(jnp.bfloat16), "tp").astype(jnp.float32)


def attend_group(operands):
    queries, keys_all, values_all = operands
    score_factor = HD ** (-0.5)

    def attend_block(query_block):
        scores = (
            jnp.einsum("qe,ke->qk", query_block, keys_all, preferred_element_type=jnp.float32)
            * score_factor
        )
        largest = jnp.max(scores, axis=-1, keepdims=True)
        expon = jnp.exp(scores - largest)
        totals = jnp.sum(expon, axis=-1, keepdims=True)
        probs = expon / totals
        block_out = jnp.dot(
            probs.astype(jnp.bfloat16), values_all, preferred_element_type=jnp.float32
        )
        return (block_out.astype(jnp.bfloat16), (largest + jnp.log(totals))[:, 0])

    return lax.map(attend_block, queries.reshape(LEN // QBLK, QBLK, HD))


def backward_group(operands):
    queries, keys_all, values_all, grad_attended, log_totals = operands
    score_factor = HD ** (-0.5)

    def back_block(carry, block_items):
        grad_keys, grad_values = carry
        query_block, grad_block, log_block = block_items
        scores = (
            jnp.einsum("qe,ke->qk", query_block, keys_all, preferred_element_type=jnp.float32)
            * score_factor
        )
        probs = jnp.exp(scores - log_block[:, None])
        probs_low = probs.astype(jnp.bfloat16)
        grad_probs = jnp.einsum(
            "qe,ke->qk", grad_block, values_all, preferred_element_type=jnp.float32
        )
        inner = jnp.sum(probs * grad_probs, axis=-1, keepdims=True)
        grad_scores = (probs * (grad_probs - inner)).astype(jnp.bfloat16)
        grad_query = (
            jnp.dot(grad_scores, keys_all, preferred_element_type=jnp.float32) * score_factor
        )
        grad_keys = grad_keys + contract_rows(grad_scores, query_block) * score_factor
        grad_values = grad_values + contract_rows(probs_low, grad_block)
        return ((grad_keys, grad_values), grad_query)

    zeros_kv = jnp.zeros((LEN, HD), jnp.float32)
    block_count = LEN // QBLK
    items = (
        queries.reshape(block_count, QBLK, HD),
        grad_attended.reshape(block_count, QBLK, HD),
        log_totals,
    )
    (grad_keys, grad_values), grad_queries = lax.scan(back_block, (zeros_kv, zeros_kv), items)
    return (grad_queries.reshape(LEN, HD), grad_keys, grad_values)


def shards(
    block_input,
    positions,
    w_qkv,
    b_qkv,
    w_proj,
    w_up,
    b_up,
    w_down,
    norm_gains,
    norm_shifts,
    out_shifts,
    grad_out,
):
    clip_count, local_len, width = block_input.shape
    row_count = clip_count * local_len
    ctx_count = lax.axis_size("ctx")
    local_width = w_qkv.shape[2]
    group_heads = local_width // ctx_count // HD
    group_count = clip_count * group_heads
    inputs = block_input.reshape(row_count, width).astype(jnp.float32)
    full_qkv, full_proj, full_up, full_down = (
        lax.all_gather(w_qkv, "fsdp", axis=1, tiled=True),
        lax.all_gather(w_proj, "fsdp", axis=1, tiled=True),
        lax.all_gather(w_up, "fsdp", axis=0, tiled=True),
        lax.all_gather(w_down, "fsdp", axis=1, tiled=True),
    )
    cos_table, sin_table = rotary_tables(positions.reshape(3, row_count))
    normed_one = layer_norm(inputs, norm_gains[0], norm_shifts[0])
    normed_one_low = normed_one.astype(jnp.bfloat16)
    projected = (
        jnp.einsum("rd,cde->cre", normed_one_low, full_qkv, preferred_element_type=jnp.float32)
        + b_qkv[:, None, :]
    )
    head_shape = (row_count, local_width // HD, HD)
    queries_rot = rotary(projected[0].reshape(head_shape), cos_table, sin_table).reshape(
        row_count, local_width
    )
    keys_rot = rotary(projected[1].reshape(head_shape), cos_table, sin_table).reshape(
        row_count, local_width
    )
    token_qkv = (
        jnp.stack([queries_rot, keys_rot, projected[2]])
        .astype(jnp.bfloat16)
        .reshape(3, clip_count, local_len, local_width)
    )
    head_qkv = lax.all_to_all(token_qkv, "ctx", split_axis=3, concat_axis=2, tiled=True)
    full_len = head_qkv.shape[2]
    grouped = (
        head_qkv.reshape(3, clip_count, full_len, group_heads, HD)
        .transpose(0, 1, 3, 2, 4)
        .reshape(3, group_count, full_len, HD)
    )
    attended, log_totals = lax.map(attend_group, (grouped[0], grouped[1], grouped[2]))
    attended = (
        attended.reshape(clip_count, group_heads, full_len, HD)
        .transpose(0, 2, 1, 3)
        .reshape(clip_count, full_len, group_heads * HD)
    )
    token_attended = lax.all_to_all(
        attended, "ctx", split_axis=1, concat_axis=2, tiled=True
    ).reshape(row_count, local_width)
    attn_part = jnp.dot(token_attended, full_proj, preferred_element_type=jnp.float32)
    residual = inputs + tp_whole(attn_part) + out_shifts[0]
    normed_two_low = layer_norm(residual, norm_gains[1], norm_shifts[1]).astype(jnp.bfloat16)
    pre_act = jnp.dot(normed_two_low, full_up, preferred_element_type=jnp.float32) + b_up
    act_low = jax.nn.gelu(pre_act, approximate=False).astype(jnp.bfloat16)
    mlp_part = jnp.dot(act_low, full_down, preferred_element_type=jnp.float32)
    result = residual + tp_whole(mlp_part) + out_shifts[1]
    block_rows = result.astype(jnp.bfloat16)
    full_qkv, full_proj, full_up, full_down = (
        lax.all_gather(w_qkv, "fsdp", axis=1, tiled=True),
        lax.all_gather(w_proj, "fsdp", axis=1, tiled=True),
        lax.all_gather(w_up, "fsdp", axis=0, tiled=True),
        lax.all_gather(w_down, "fsdp", axis=1, tiled=True),
    )
    upstream = grad_out.reshape(row_count, width).astype(jnp.float32)
    upstream_low = upstream.astype(jnp.bfloat16)
    grad_down = contract_rows(act_low, upstream_low)
    grad_act = contract_cols(upstream_low, full_down)
    _, gelu_pull = jax.vjp(partial(jax.nn.gelu, approximate=False), pre_act)
    grad_pre = gelu_pull(grad_act)[0].astype(jnp.bfloat16)
    grad_b_up = jnp.sum(grad_pre.astype(jnp.float32), axis=0)
    grad_up = contract_rows(normed_two_low, grad_pre)
    back_part_two = contract_cols(grad_pre, full_up)
    grad_normed_two = tp_whole(back_part_two)
    _, norm_pull_two = jax.vjp(layer_norm, residual, norm_gains[1], norm_shifts[1])
    grad_res_norm, grad_gain_two, grad_shift_two = norm_pull_two(grad_normed_two)
    grad_residual = upstream + grad_res_norm
    grad_residual_low = grad_residual.astype(jnp.bfloat16)
    grad_proj = contract_rows(token_attended, grad_residual_low)
    grad_token_att = (
        contract_cols(grad_residual_low, full_proj)
        .astype(jnp.bfloat16)
        .reshape(clip_count, local_len, local_width)
    )
    grad_head_att = lax.all_to_all(grad_token_att, "ctx", split_axis=2, concat_axis=1, tiled=True)
    grad_grouped = (
        grad_head_att.reshape(clip_count, full_len, group_heads, HD)
        .transpose(0, 2, 1, 3)
        .reshape(group_count, full_len, HD)
    )
    grad_q, grad_k, grad_v = lax.map(
        backward_group, (grouped[0], grouped[1], grouped[2], grad_grouped, log_totals)
    )
    grad_heads = jnp.stack([grad_q, grad_k, grad_v]).astype(jnp.bfloat16)
    grad_heads = (
        grad_heads.reshape(3, clip_count, group_heads, full_len, HD)
        .transpose(0, 1, 3, 2, 4)
        .reshape(3, clip_count, full_len, group_heads * HD)
    )
    grad_tokens = (
        lax.all_to_all(grad_heads, "ctx", split_axis=2, concat_axis=3, tiled=True)
        .reshape(3, row_count, local_width)
        .astype(jnp.float32)
    )

    def rotate_rows(moved):
        return rotary(moved, cos_table, sin_table)

    _, rotary_pull = jax.vjp(rotate_rows, jnp.zeros(head_shape, jnp.float32))
    grad_q_pre = rotary_pull(grad_tokens[0].reshape(head_shape))[0].reshape(row_count, local_width)
    grad_k_pre = rotary_pull(grad_tokens[1].reshape(head_shape))[0].reshape(row_count, local_width)
    grad_qkv_low = jnp.stack([grad_q_pre, grad_k_pre, grad_tokens[2]]).astype(jnp.bfloat16)
    grad_b_qkv = jnp.sum(grad_qkv_low.astype(jnp.float32), axis=1)
    grad_qkv = jnp.einsum(
        "rd,cre->cde", normed_one_low, grad_qkv_low, preferred_element_type=jnp.float32
    )
    back_part_one = jnp.einsum(
        "cre,cde->rd", grad_qkv_low, full_qkv, preferred_element_type=jnp.float32
    )
    grad_normed_one = tp_whole(back_part_one)
    _, norm_pull_one = jax.vjp(layer_norm, inputs, norm_gains[0], norm_shifts[0])
    grad_in_norm, grad_gain_one, grad_shift_one = norm_pull_one(grad_normed_one)
    grad_input_rows = grad_residual + grad_in_norm
    norm_vectors = jnp.stack(
        [
            grad_gain_one,
            grad_gain_two,
            grad_shift_one,
            grad_shift_two,
            jnp.sum(grad_residual, axis=0),
            jnp.sum(upstream, axis=0),
        ]
    )
    block_output = block_rows.reshape(clip_count, local_len, width)
    grad_input = grad_input_rows.reshape(clip_count, local_len, width)
    shard_qkv, shard_proj, shard_up, shard_down = (
        lax.psum_scatter(
            grad_qkv.astype(jnp.bfloat16), "fsdp", scatter_dimension=1, tiled=True
        ).astype(jnp.float32),
        lax.psum_scatter(
            grad_proj.astype(jnp.bfloat16), "fsdp", scatter_dimension=1, tiled=True
        ).astype(jnp.float32),
        lax.psum_scatter(
            grad_up.astype(jnp.bfloat16), "fsdp", scatter_dimension=0, tiled=True
        ).astype(jnp.float32),
        lax.psum_scatter(
            grad_down.astype(jnp.bfloat16), "fsdp", scatter_dimension=1, tiled=True
        ).astype(jnp.float32),
    )
    shard_qkv, shard_proj, shard_up, shard_down = (
        lax.psum(shard_qkv.astype(jnp.bfloat16), "ctx").astype(jnp.float32),
        lax.psum(shard_proj.astype(jnp.bfloat16), "ctx").astype(jnp.float32),
        lax.psum(shard_up.astype(jnp.bfloat16), "ctx").astype(jnp.float32),
        lax.psum(shard_down.astype(jnp.bfloat16), "ctx").astype(jnp.float32),
    )
    gains_sum, shifts_sum, outs_sum, bqkv_sum, bup_sum = lax.psum(
        (norm_vectors[0:2], norm_vectors[2:4], norm_vectors[4:6], grad_b_qkv, grad_b_up),
        ("fsdp", "ctx"),
    )
    return (
        block_output,
        grad_input,
        shard_qkv,
        bqkv_sum,
        shard_proj,
        shard_up,
        bup_sum,
        shard_down,
        gains_sum,
        shifts_sum,
        outs_sum,
    )


def solution(mesh):
    in_specs = (
        P("fsdp", "ctx", None),
        P(None, "fsdp", "ctx"),
        P(None, "fsdp", "tp"),
        P(None, "tp"),
        P("tp", "fsdp"),
        P("fsdp", "tp"),
        P("tp"),
        P("tp", "fsdp"),
        P(),
        P(),
        P(),
        P("fsdp", "ctx", None),
    )
    out_specs = (
        P("fsdp", "ctx", None),
        P("fsdp", "ctx", None),
        P(None, "fsdp", "tp"),
        P(None, "tp"),
        P("tp", "fsdp"),
        P("fsdp", "tp"),
        P("tp"),
        P("tp", "fsdp"),
        P(),
        P(),
        P(),
    )
    return jax.shard_map(shards, mesh=mesh, in_specs=in_specs, out_specs=out_specs, check_vma=False)
```

profile of v0, /device:TPU:0, one launch (start us, length us, event | category | flops | bytes accessed | tf_op | source)
XLA Modules:
  0.0 875.1 jit_solution(13437522062420596701)
XLA Ops:
  7.3 2.4 copy.73
  9.7 1.9 convert_reduce_fusion.2
  15.1 2.1 fusion.40
  17.3 22.8 %all-gather.4.cloned.1.call-done = bf16[3,1024,256]{1,2,0:T(8,128)(2,1)} async-done(((bf16[3,512,256]{1,2,0:T(8,128)(2,1)}), bf16[3,1024,256]{1,2,0:T(8,128)(2,1)}) %all-gather.4.cloned.1.call-update) | async-done | bytes 1572880 | tf_op jit(solution)/shard_map/all_gather | solution.py:140
  40.1 3.9 add_bitcast_fusion
  46.6 2.1 concatenate.14
  49.0 2.1 concatenate.13
  51.5 3.1 pad_maximum_fusion.1
  54.5 3.8 all-to-all-start
  58.3 20.0 %all-to-all-done = bf16[3,2,512,256]{2,1,0,3:T(2,128)(2,1)S(1)} async-done(((bf16[3,2,512,256]{2,1,0,3:T(2,128)(2,1)}), bf16[3,2,512,256]{2,1,0,3:T(2,128)(2,1)S(1)}, u32[]{:S(2)}, u32[]{:S(2)}) %all-to-all-start) | async-done | bytes 1572896 | tf_op jit(solution)/shard_map/all_to_all | solution.py:164
  83.0 27.2 %while.54 = (s32[]{:T(128)}, bf16[2,4,512,64]{2,3,1,0:T(8,128)(2,1)}, f32[2,4,512]{2,1,0:T(4,128)S(1)}, bf16[2,2048,64]{2,1,0:T(8,128)(2,1)S(1)}, bf16[2,2048,64...) while((s32[]{:T(128)}, ...), condition=%wide.region_7.8_spmd, body=%wide.region_2.7_spmd.sunk | while | flops 277904896 | bytes 20156772 | solution.py:171
  84.4 11.4 %while.57 = (s32[]{:T(128)}, bf16[4,512,64]{1,2,0:T(8,128)(2,1)S(1)}, f32[4,512]{1,0:T(4,128)S(1)}, bf16[4,512,64]{2,1,0:T(8,128)(2,1)S(1)}, bf16[2048,64]{1,0:T...) while((s32[]{:T(128)}, bf16[4,512,64]{1,2,0:T(8,128)(2,1)S(1)}, ...), condition=%wide.region_6.6_spmd, body=%wide.region_3.5_spmd.sunk | while | flops 277904896 | bytes 13848681 | solution.py:79
  98.0 11.4 %while.57 = (s32[]{:T(128)}, bf16[4,512,64]{1,2,0:T(8,128)(2,1)S(1)}, f32[4,512]{1,0:T(4,128)S(1)}, bf16[4,512,64]{2,1,0:T(8,128)(2,1)S(1)}, bf16[2048,64]{1,0:T...) while((s32[]{:T(128)}, bf16[4,512,64]{1,2,0:T(8,128)(2,1)S(1)}, ...), condition=%wide.region_6.6_spmd, body=%wide.region_3.5_spmd.sunk | while | flops 277904896 | bytes 13848681 | solution.py:79
  110.3 2.6 copy.101
  114.4 3.5 all-to-all-start.1
  117.9 9.3 %all_gather.17 = bf16[256,1024]{1,0:T(8,128)(2,1)S(1)} all-gather(bf16[256,512]{1,0:T(8,128)(2,1)S(1)} %copy-done.30), channel_id=1, replica_groups=mesh['fsdp'=2,'ctx'=4,'tp'=4] {'fsdp'}, dimensions={1}, use_global_device_ids=true | all-gather | bytes 786432 | tf_op jit(solution)/shard_map/all_gather | solution.py:141
  128.0 1.9 copy.82
  131.1 2.1 convolution_convert_fusion.4
  135.5 84.2 %all-reduce.22.cloned.1.call-done = bf16[1024,1024]{1,0:T(8,128)(2,1)} async-done(((bf16[1024,1024]{1,0:T(8,128)(2,1)}), bf16[1024,1024]{1,0:T(8,128)(2,1)}) %all-reduce.22.cloned.1.call-update) | async-done | bytes 2097168 | tf_op jit(solution)/shard_map/psum | solution.py:58
  219.7 2.5 fusion.50
  222.2 3.0 multiply_reduce_fusion.2
  225.3 28.2 %all-gather.6.cloned.1.call-done = bf16[1024,1024]{1,0:T(8,128)(2,1)} async-done(((bf16[512,1024]{1,0:T(8,128)(2,1)}), bf16[1024,1024]{1,0:T(8,128)(2,1)}) %all-gather.6.cloned.1.call-update) | async-done | bytes 2097168 | tf_op jit(solution)/shard_map/all_gather | solution.py:142
  253.4 7.4 fusion.69
  260.8 27.1 %all-gather.8.cloned.1.call-done = bf16[1024,1024]{1,0:T(8,128)(2,1)} async-done(((bf16[1024,512]{1,0:T(8,128)(2,1)}), bf16[1024,1024]{1,0:T(8,128)(2,1)}) %all-gather.8.cloned.1.call-update) | async-done | bytes 2097168 | tf_op jit(solution)/shard_map/all_gather | solution.py:143
  287.9 16.0 %convert_reduce_fusion.4 = (f32[1024]{0:T(1024)}, bf16[1024,1024]{1,0:T(8,128)(2,1)S(1)}, f32[1024,1024]{1,0:T(8,128)}) fusion(f32[1024,1024]{1,0:T(8,128)} %fusion.69, f32[1024]{0:T(1024)S(1)} %copy-done.50, bf16[1024,1024]{1,0:T(8,128)(2,1)S(1)} %bitcast.274, bf16[1024,1024]{1,0:T(8,128)(2,1)} %all-gather.8.cloned.1.call-done), kind=kOutput, calls=%fused_computation.82 | convolution fusion | flops 2226125824 | bytes 14688256 | tf_op jit(solution)/shard_map/dot_general | solution.py:52
  305.2 3.7 convolution_convert_fusion.2
  308.9 12.1 %reduce-scatter.7.cloned.1.call-start = ((), (), s32[]{:S(2)}) async-start(), calls=%async_computation.14 | async-start | bytes 786432 | tf_op jit(solution)/shard_map/reduce_scatter | solution.py:269
  321.1 74.2 %all-reduce.24.cloned.1.call-done = bf16[1024,1024]{1,0:T(8,128)(2,1)} async-done(((bf16[1024,1024]{1,0:T(8,128)(2,1)}), bf16[1024,1024]{1,0:T(8,128)(2,1)}) %all-reduce.24.cloned.1.call-update) | async-done | bytes 2097168 | tf_op jit(solution)/shard_map/psum | solution.py:58
  395.3 4.5 convert_reduce_fusion.1
  400.0 2.7 fusion.34
  402.7 2.4 fusion.70
  405.0 2.0 copy-done.3
  408.6 4.6 multiply_convert_fusion.1
  414.5 3.8 convolution_convert_fusion
  418.3 3.0 convolution_convert_fusion.6
  422.5 3.5 all-to-all-start.2
  426.0 6.9 convolution_convert_fusion.1
  433.0 1.8 all-to-all-done.2
  436.1 103.6 %while.56 = (s32[]{:T(128)}, bf16[2,2048,64]{2,0,1:T(2,128)(2,1)}, bf16[2,2048,64]{1,2,0:T(8,128)(2,1)}, bf16[2,2048,64]{1,2,0:T(8,128)(2,1)}, bf16[2,2048,64]{2...) while((s32[]{:T(128)}, bf16[2,2048,64]{2,0,1:T(2,128)(2,1)}, ...), condition=%wide.region_19.20_spmd, body=%wide.region_15.19_spmd.sunk | while | flops 680164864 | bytes 41838996 | solution.py:220
  440.5 20.1 %while.58 = (s32[]{:T(128)}, f32[2048,64]{0,1:T(8,128)S(1)}, f32[2048,64]{0,1:T(8,128)S(1)}, f32[4,512,64]{1,2,0:T(8,128)}, bf16[4,512,64]{2,1,0:T(8,128)(2,1)S(...) while((s32[]{:T(128)}, f32[2048,64]{0,1:T(8,128)S(1)}, ...), condition=%wide.region_18.18_spmd.clone, body=%wide.region_16.17_spmd.clone.sunk | while | flops 680164864 | bytes 35530900 | solution.py:114
  462.0 25.1 %dynamic_update_slice.47 = bf16[2,2048,64]{2,0,1:T(2,128)(2,1)} dynamic-update-slice(bf16[2,2048,64]{2,0,1:T(2,128)(2,1)} %get-tuple-element.795, f32[1,2048,64]{2,0,1:T(1,128)S(1)} %bitcast.268, s32[]{:T(128)S(6)} %copy.189, s32[]{:T(128)} %constant.78.clone.1..sunk.2, s32[]{:T(128)} %constant.78.clone.1..sunk.2) | dynamic-update-slice | bytes 1048580 | tf_op jit(solution)/shard_map/while/body/jit(dynamic_update_index_in_dim)/dynamic_update_slice | solution.py:220
  492.3 20.1 %while.58 = (s32[]{:T(128)}, f32[2048,64]{0,1:T(8,128)S(1)}, f32[2048,64]{0,1:T(8,128)S(1)}, f32[4,512,64]{1,2,0:T(8,128)}, bf16[4,512,64]{2,1,0:T(8,128)(2,1)S(...) while((s32[]{:T(128)}, f32[2048,64]{0,1:T(8,128)S(1)}, ...), condition=%wide.region_18.18_spmd.clone, body=%wide.region_16.17_spmd.clone.sunk | while | flops 680164864 | bytes 35530900 | solution.py:114
  513.8 25.1 %dynamic_update_slice.47 = bf16[2,2048,64]{2,0,1:T(2,128)(2,1)} dynamic-update-slice(bf16[2,2048,64]{2,0,1:T(2,128)(2,1)} %get-tuple-element.795, f32[1,2048,64]{2,0,1:T(1,128)S(1)} %bitcast.268, s32[]{:T(128)S(6)} %copy.189, s32[]{:T(128)} %constant.78.clone.1..sunk.2, s32[]{:T(128)} %constant.78.clone.1..sunk.2) | dynamic-update-slice | bytes 1048580 | tf_op jit(solution)/shard_map/while/body/jit(dynamic_update_index_in_dim)/dynamic_update_slice | solution.py:220
  539.7 3.6 copy.142
  543.3 3.6 copy.141
  546.8 7.2 fusion.79
  554.0 3.3 reshape.228
  557.3 24.7 %all_to_all.57 = bf16[4,2,98304]{2,1,0:T(2,128)(2,1)} all-to-all(bf16[4,2,98304]{2,1,0:T(2,128)(2,1)} %reshape.228), channel_id=1, replica_groups=mesh['fsdp'=2,'ctx'=4,'tp'=4] {'ctx'}, dimensions={0} | all-to-all | bytes 3145728 | tf_op jit(solution)/shard_map/all_to_all | solution.py:230
  582.0 3.8 reshape.229
  585.8 6.4 copy.92
  601.3 4.9 fusion.61
  606.3 5.4 convolution_convert_fusion.3
  611.7 3.1 bitcast_convert_fusion
  615.2 2.1 convert_reduce_fusion.3
  618.7 11.9 %reduce-scatter.5.cloned.1.call-done = bf16[3,512,256]{1,2,0:T(8,128)(2,1)} async-done(((bf16[3,1024,256]{1,2,0:T(8,128)(2,1)}), bf16[3,512,256]{1,2,0:T(8,128)(2,1)}) %reduce-scatter.5.cloned.1.call-update) | async-done | bytes 786448 | tf_op jit(solution)/shard_map/reduce_scatter | solution.py:266
  630.7 157.9 %all-reduce.26.cloned.1.call-done = (bf16[1024,1024]{1,0:T(8,128)(2,1)}, bf16[1024,1024]{1,0:T(8,128)(2,1)}) async-done(((bf16[1024,1024]{1,0:T(8,128)(2,1)}, bf16[1024,1024]{1,0:T(8,128)(2,1)}), (bf16[1024,1024]{1,0:T(8,128)(2,1)}, bf16[1024,1024]{1,0:T(8,128)(2,1)})) %all-reduce.26.cloned.1.call-update) | async-done | bytes 4194320 | tf_op jit(solution)/shard_map/psum | solution.py:58
  788.6 3.1 convert_reduce_fusion
  791.7 2.7 fusion.35
  794.5 26.2 %all-reduce.14 = (f32[3,256]{1,0:T(4,128)}, f32[1024]{0:T(1024)}, f32[2,1024]{1,0:T(2,128)}, f32[2,1024]{1,0:T(2,128)}, f32[2,1024]{1,0:T(2,128)}) all-reduce(f32[3,256]{1,0:T(4,128)S(1)} %convert_reduce_fusion.5, f32[1024]{0:T(1024)S(1)} %copy-done.52, ...), channel_id=1, replica_groups=mesh['fsdp'=2,'ctx'=4,'tp'=4] {'fsdp','ctx'}, use_global_device_ids=true, to_apply=%region_26.27 | all-reduce | flops 7936 | bytes 63488 | tf_op jit(solution)/shard_map/psum | solution.py:285
  820.7 7.1 add_add_fusion.2
  827.9 31.4 %all-reduce.28.cloned.1.call-done = (bf16[3,512,256]{1,2,0:T(8,128)(2,1)}, bf16[256,512]{1,0:T(8,128)(2,1)}, bf16[512,1024]{1,0:T(8,128)(2,1)}, bf16[1024,512]{1,0:T(8,128)(2,1)}) async-done(((bf16[3,512,256]{1,2,0:T(8,128)(2,1)}, bf16[256,512]{1,0:T(8,128)(2,1)}, bf16[512,1024]{1,0:T(8,128)(2,1)}, bf16[1024,512]{1,0:T(8,128)(2,1)}), (bf16[3,512,256]{1,2,0:T(8,128)(2,1)}, bf16[256,512]{1,0:T(8,128)(2,1)}, ...) | async-done | bytes 3145744 | tf_op jit(solution)/shard_map/psum | solution.py:280
  859.2 1.9 convert_element_type.168
  861.1 2.5 copy.98
  863.7 2.8 convert_element_type.170
  (335 shorter events, 116.5 us)
Async XLA Ops:
  7.2 4.5 copy-start
  7.2 5.3 copy-start.46
  7.2 5.8 copy-start.47
  7.2 6.4 copy-start.48
  7.2 32.9 %all-gather.4.cloned.1.call-start = ((), (), s32[]{:S(2)}) async-start(), calls=%async_computation.8 | async-start | bytes 2359296 | tf_op jit(solution)/shard_map/all_gather | solution.py:140
  11.7 28.4 %copy-start.55 = (f32[3,256]{1,0:T(4,128)S(1)}, f32[3,256]{1,0:T(4,128)}, u32[]{:S(2)}) copy-start(f32[3,256]{1,0:T(4,128)} %param.23) | copy-start | bytes 9220
  11.7 3.4 copy-start.31
  12.5 2.6 copy-start.38
  15.0 30.8 %copy-start.15 = (f32[1024,10]{0,1:T(8,128)}, f32[1024,10]{0,1:T(8,128)S(1)}, u32[]{:S(2)}) copy-start(f32[1024,10]{0,1:T(8,128)S(1)} %get-tuple-element.436) | copy-start | bytes 122884
  15.0 30.8 %copy-start.17 = (f32[1024,10]{0,1:T(8,128)}, f32[1024,10]{0,1:T(8,128)S(1)}, u32[]{:S(2)}) copy-start(f32[1024,10]{0,1:T(8,128)S(1)} %get-tuple-element.437) | copy-start | bytes 122884
  15.0 30.8 %copy-start.19 = (f32[1024,10]{0,1:T(8,128)}, f32[1024,10]{0,1:T(8,128)S(1)}, u32[]{:S(2)}) copy-start(f32[1024,10]{0,1:T(8,128)S(1)} %get-tuple-element.438) | copy-start | bytes 122884
  15.1 30.8 %copy-start.21 = (f32[1024,10]{0,1:T(8,128)}, f32[1024,10]{0,1:T(8,128)S(1)}, u32[]{:S(2)}) copy-start(f32[1024,10]{0,1:T(8,128)S(1)} %get-tuple-element.449) | copy-start | bytes 122884
  15.1 30.8 %copy-start.23 = (f32[1024,10]{0,1:T(8,128)}, f32[1024,10]{0,1:T(8,128)S(1)}, u32[]{:S(2)}) copy-start(f32[1024,10]{0,1:T(8,128)S(1)} %get-tuple-element.450) | copy-start | bytes 122884
  15.1 30.8 %copy-start.25 = (f32[1024,10]{0,1:T(8,128)}, f32[1024,10]{0,1:T(8,128)S(1)}, u32[]{:S(2)}) copy-start(f32[1024,10]{0,1:T(8,128)S(1)} %get-tuple-element.451) | copy-start | bytes 122884
  54.5 23.8 %all-to-all-start = ((bf16[3,2,512,256]{2,1,0,3:T(2,128)(2,1)}), bf16[3,2,512,256]{2,1,0,3:T(2,128)(2,1)S(1)}, u32[]{:S(2)}, u32[]{:S(2)}) async-start(bf16[3,2,512,256]{2,1,0,3:T(2,128)(2,1)} %pad_maximum_fusion.1), calls=%async_computation | async-start | bytes 3145728 | tf_op jit(solution)/shard_map/all_to_all | solution.py:164
  84.4 11.4 %copy-start.28 = (bf16[2,4,512,64]{2,3,1,0:T(8,128)(2,1)S(1)}, bf16[2,4,512,64]{2,3,1,0:T(8,128)(2,1)}, u32[]{:S(2)}) copy-start(bf16[2,4,512,64]{2,3,1,0:T(8,128)(2,1)} %get-tuple-element.762) | copy-start | bytes 1572868 | tf_op jit(solution)/shard_map/while
  98.0 11.4 %copy-start.28 = (bf16[2,4,512,64]{2,3,1,0:T(8,128)(2,1)S(1)}, bf16[2,4,512,64]{2,3,1,0:T(8,128)(2,1)}, u32[]{:S(2)}) copy-start(bf16[2,4,512,64]{2,3,1,0:T(8,128)(2,1)} %get-tuple-element.762) | copy-start | bytes 1572868 | tf_op jit(solution)/shard_map/while
  110.2 19.6 %copy-start.5 = (bf16[2,2048,64]{2,1,0:T(8,128)(2,1)}, bf16[2,2048,64]{2,1,0:T(8,128)(2,1)S(1)}, u32[]{:S(2)}) copy-start(bf16[2,2048,64]{2,1,0:T(8,128)(2,1)S(1)} %get-tuple-element.841) | copy-start | bytes 1572868
  110.3 7.7 copy-start.30
  114.4 12.8 %all-to-all-start.1 = ((bf16[4,2,32768]{2,1,0:T(2,128)(2,1)}), bf16[4,2,32768]{2,1,0:T(2,128)(2,1)S(1)}, u32[]{:S(2)}, u32[]{:S(2)}) async-start(bf16[4,2,32768]{2,1,0:T(2,128)(2,1)} %reshape.226), calls=%async_computation.1 | async-start | bytes 1048576 | tf_op jit(solution)/shard_map/all_to_all | solution.py:177
  117.9 101.8 %all-reduce.22.cloned.1.call-start = ((), (), s32[]{:S(2)}) async-start(), calls=%async_computation.9 | async-start | bytes 4194304 | tf_op jit(solution)/shard_map/psum | solution.py:58
  129.9 5.0 copy-start.49
  129.9 89.8 %copy-start.1 = (bf16[2,512,1024]{2,1,0:T(8,128)(2,1)S(1)}, bf16[2,512,1024]{2,1,0:T(8,128)(2,1)}, u32[]{:S(2)}) copy-start(bf16[2,512,1024]{2,1,0:T(8,128)(2,1)} %param.20) | copy-start | bytes 6291460
  133.2 120.2 %all-gather.6.cloned.1.call-start = ((), (), s32[]{:S(2)}) async-start(), calls=%async_computation.10 | async-start | bytes 3145728 | tf_op jit(solution)/shard_map/all_gather | solution.py:142
  134.0 154.0 %all-gather.8.cloned.1.call-start = ((), (), s32[]{:S(2)}) async-start(), calls=%async_computation.11 | async-start | bytes 3145728 | tf_op jit(solution)/shard_map/all_gather | solution.py:143
  134.5 260.7 %all-reduce.24.cloned.1.call-start = ((), (), s32[]{:S(2)}) async-start(), calls=%async_computation.12 | async-start | bytes 4194304 | tf_op jit(solution)/shard_map/psum | solution.py:58
  135.5 89.7 %copy-start.36 = (f32[1,1024]{1,0:T(1,128)}, f32[1,1024]{1,0:T(1,128)S(1)}, u32[]{:S(2)}) copy-start(f32[1,1024]{1,0:T(1,128)S(1)} %get-tuple-element.442) | copy-start | bytes 12292
  219.7 2.5 copy-start.6
  222.2 31.2 %copy-start.35 = (f32[1,1024]{1,0:T(1,128)S(1)}, f32[1,1024]{1,0:T(1,128)}, u32[]{:S(2)}) copy-start(f32[1,1024]{1,0:T(1,128)} %get-tuple-element.443) | copy-start | bytes 12292
  222.2 31.2 %copy-start.51 = (f32[1,1024]{1,0:T(1,128)S(1)}, f32[1,1024]{1,0:T(1,128)}, u32[]{:S(2)}) copy-start(f32[1,1024]{1,0:T(1,128)} %get-tuple-element.445) | copy-start | bytes 12292
  253.4 34.5 %copy-start.10 = (bf16[2,512,1024]{2,1,0:T(8,128)(2,1)S(1)}, bf16[2,512,1024]{2,1,0:T(8,128)(2,1)}, u32[]{:S(2)}) copy-start(bf16[2,512,1024]{2,1,0:T(8,128)(2,1)} %param.31) | copy-start | bytes 6291460
  253.4 34.5 %copy-start.50 = (f32[1024]{0:T(1024)S(1)}, f32[1024]{0:T(1024)}, u32[]{:S(2)}) copy-start(f32[1024]{0:T(1024)} %param.26) | copy-start | bytes 12292
  287.9 17.3 %copy-start.53 = (bf16[1024,1024]{1,0:T(8,128)(2,1)S(1)}, bf16[1024,1024]{1,0:T(8,128)(2,1)}, u32[]{:S(2)}) copy-start(bf16[1024,1024]{1,0:T(8,128)(2,1)} %all-gather.6.cloned.1.call-done) | copy-start | bytes 6291460
  308.9 309.7 %reduce-scatter.7.cloned.1.call-start = ((), (), s32[]{:S(2)}) async-start(), calls=%async_computation.14 | async-start | bytes 786432 | tf_op jit(solution)/shard_map/reduce_scatter | solution.py:269
  395.2 4.5 copy-start.4
  395.3 4.7 copy-start.7
  405.0 2.0 copy-start.3
  408.5 210.2 %reduce-scatter.11.cloned.1.call-start = ((), (), s32[]{:S(2)}) async-start(), calls=%async_computation.16 | async-start | bytes 3145728 | tf_op jit(solution)/shard_map/reduce_scatter | solution.py:275
  422.5 12.3 %all-to-all-start.2 = ((bf16[2,512,256]{1,0,2:T(2,128)(2,1)}), bf16[2,512,256]{1,0,2:T(2,128)(2,1)S(1)}, u32[]{:S(2)}, u32[]{:S(2)}) async-start(bf16[2,512,256]{1,0,2:T(2,128)(2,1)} %copy.83), calls=%async_computation.2 | async-start | bytes 1048576 | tf_op jit(solution)/shard_map/all_to_all | solution.py:214
  426.0 192.7 %reduce-scatter.9.cloned.1.call-start = ((), (), s32[]{:S(2)}) async-start(), calls=%async_computation.15 | async-start | bytes 3145728 | tf_op jit(solution)/shard_map/reduce_scatter | solution.py:272
  432.9 197.7 %reduce-scatter.5.cloned.1.call-start = ((), (), s32[]{:S(2)}) async-start(), calls=%async_computation.13 | async-start | bytes 2359296 | tf_op jit(solution)/shard_map/reduce_scatter | solution.py:266
  592.2 2.9 copy-start.9
  596.4 1.7 copy-start.16
  596.4 1.7 copy-start.18
  596.4 1.7 copy-start.20
  598.9 2.4 copy-start.13
  601.3 5.0 copy-start.12
  606.2 182.3 %all-reduce.26.cloned.1.call-start = ((), (), s32[]{:S(2)}) async-start(), calls=%async_computation.17 | async-start | bytes 8388608 | tf_op jit(solution)/shard_map/psum | solution.py:58
  606.3 5.4 copy-start.14
  606.3 5.4 copy-start.54
  614.8 2.5 copy-start.42
  614.8 173.7 %copy-start.2 = (bf16[2,512,1024]{2,1,0:T(8,128)(2,1)S(1)}, bf16[2,512,1024]{2,1,0:T(8,128)(2,1)}, u32[]{:S(2)}) copy-start(bf16[2,512,1024]{2,1,0:T(8,128)(2,1)} %param.20) | copy-start | bytes 6291460
  614.8 173.7 %copy-start.32 = (f32[1,4,2,128]{3,1,2,0:T(4,128)S(1)}, f32[1,4,2,128]{3,1,2,0:T(4,128)}, u32[]{:S(2)}) copy-start(f32[1,4,2,128]{3,1,2,0:T(4,128)} %copy-done.31) | copy-start | bytes 12292
  614.9 173.7 %copy-start.34 = (f32[1,1024]{1,0:T(1,128)S(1)}, f32[1,1024]{1,0:T(1,128)}, u32[]{:S(2)}) copy-start(f32[1,1024]{1,0:T(1,128)} %copy-done.33) | copy-start | bytes 12292
  614.9 244.4 %all-reduce.28.cloned.1.call-start = ((), (), s32[]{:S(2)}) async-start(), calls=%async_computation.18 | async-start | bytes 6291456 | tf_op jit(solution)/shard_map/psum | solution.py:280
  617.3 174.4 %copy-start.41 = (f32[1,4,2,128]{3,1,2,0:T(4,128)S(1)}, f32[1,4,2,128]{3,1,2,0:T(4,128)}, u32[]{:S(2)}) copy-start(f32[1,4,2,128]{3,1,2,0:T(4,128)} %copy-done.40) | copy-start | bytes 12292
  617.3 174.4 %copy-start.44 = (f32[1024]{0:T(1024)S(1)}, f32[1024]{0:T(1024)}, u32[]{:S(2)}) copy-start(f32[1024]{0:T(1024)} %get-tuple-element.296) | copy-start | bytes 12292
  617.3 174.4 %copy-start.39 = (f32[1024]{0:T(1024)S(1)}, f32[1024]{0:T(1024)}, u32[]{:S(2)}) copy-start(f32[1024]{0:T(1024)} %copy-done.38) | copy-start | bytes 12292
  788.5 3.2 copy-start.8
  788.5 5.9 copy-start.43
  788.5 5.9 copy-start.52
  788.6 32.2 %copy-start.37 = (f32[1,1024]{1,0:T(1,128)S(1)}, f32[1,1024]{1,0:T(1,128)}, u32[]{:S(2)}) copy-start(f32[1,1024]{1,0:T(1,128)} %copy-done.36) | copy-start | bytes 12292
  788.6 32.2 %copy-start.45 = (f32[1,1024]{1,0:T(1,128)S(1)}, f32[1,1024]{1,0:T(1,128)}, u32[]{:S(2)}) copy-start(f32[1,1024]{1,0:T(1,128)} %get-tuple-element.441) | copy-start | bytes 12292
  859.2 7.2 copy-start.27
  (9 other events, 11.5 us)
Sparse Core Ops, SparseCore 0:
  10.1 29.8 all-gather.3
  133.3 86.3 all-reduce.21
  221.2 32.1 all-gather.5
  254.8 33.0 all-gather.7
  309.1 86.1 all-reduce.23
  408.7 13.6 reduce-scatter.6
  424.6 31.8 reduce-scatter.10
  458.8 31.8 reduce-scatter.8
  606.3 24.2 reduce-scatter.4
  633.5 155.0 all-reduce.25
  791.1 68.0 all-reduce.27
where the time goes:
time: 888 us; the launch traced here: 875 us
  waiting for transfers between devices  461 us (52%)
  local copies, waits for them, and re-layouts  130 us (15%)
  matrix products  113 us (13%)
  other arithmetic  71.1 us (8%)
  blocking collectives  60.2 us (7%)
  starting transfers between devices  23.8 us (3%)
  between operations  15.3 us (2%)
    psum x3, waiting for transfers between devices, tp_whole(): return lax.psum(partial_sum.astype(jnp.bfloat16), 'tp').astype(jnp.float32)  316 us
    dynamic_update_slice x4, local copies, waits for them, and re-layouts, shards(): lax.map(backward_group, (grouped[0], grouped[1], grouped[2], grad_grouped...  51.9 us
    psum x1, waiting for transfers between devices, shards(): lax.psum(shard_qkv.astype(jnp.bfloat16), 'ctx').astype(jnp.float32)  31.4 us
    unnamed x122, local copies, waits for them, and re-layouts  28.2 us
    all_gather x1, waiting for transfers between devices, shards(): lax.all_gather(w_up, 'fsdp', axis=0, tiled=True)  28.2 us
    all_gather x1, waiting for transfers between devices, shards(): lax.all_gather(w_down, 'fsdp', axis=1, tiled=True)  27.1 us
    psum x1, blocking collectives, shards(): lax.psum((norm_vectors[0:2], norm_vectors[2:4], norm_vectors[4:6], grad_b...  26.2 us
    all_to_all x1, blocking collectives, shards(): lax.all_to_all(grad_heads, 'ctx', split_axis=2, concat_axis=3, tiled=True)  24.7 us
  transfers between devices with their start and end apart: 14, of which 10 were waited for; matrix products, arithmetic and copies ran while one was open for 24% of the time, Pallas kernels for 0%

commit v1 on v0

v1 whole, which is shorter than its diff:
```python
import functools

import jax
import jax.numpy as jnp
from jax import lax
from jax.experimental import pallas as pl
from jax.experimental.pallas import tpu as pltpu
from jax.sharding import PartitionSpec as P

HD = 64
ROT = 20
EPSILON = 1e-06
SCALE = HD ** (-0.5)
QB = 256
ROWS = 128
MESH = pl.DeviceIdType.MESH
F32, BF16 = jnp.float32, jnp.bfloat16


def mm(left, right, left_dim, right_dim):
    return lax.dot_general(
        left, right, (((left_dim,), (right_dim,)), ((), ())), preferred_element_type=F32
    )


def remote(src, dst, send_sem, recv_sem, axis, peer):
    return pltpu.make_async_remote_copy(
        src_ref=src,
        dst_ref=dst,
        send_sem=send_sem,
        recv_sem=recv_sem,
        device_id={axis: peer},
        device_id_type=MESH,
    )


def greet(*axes):
    barrier = pltpu.get_barrier_semaphore()
    total = 0
    for axis in axes:
        size, me = lax.axis_size(axis), lax.axis_index(axis)
        for step in range(1, size):
            pl.semaphore_signal(
                barrier, inc=1, device_id={axis: lax.rem(me + step, size)}, device_id_type=MESH
            )
            total += 1
    pl.semaphore_wait(barrier, total)


def aligned(start, size):
    return pl.ds(pl.multiple_of(start, size), size)


def norm_parts(values):
    center = values - jnp.mean(values, axis=-1, keepdims=True)
    rstd = lax.rsqrt(jnp.mean(center * center, axis=-1, keepdims=True) + EPSILON)
    return center * rstd, rstd


def norm_pull(hat, rstd, gain, grad):
    scaled = grad * gain
    return rstd * (
        scaled
        - jnp.mean(scaled, axis=-1, keepdims=True)
        - hat * jnp.mean(scaled * hat, axis=-1, keepdims=True)
    )


def turn(values, cos_t, low_t, high_t, sign):
    half = ROT // 2
    up = jnp.concatenate([values[half:], values[:half]], axis=0)
    down = jnp.concatenate([values[-half:], values[:-half]], axis=0)
    if sign > 0:
        return values * cos_t + (up * low_t + down * high_t)
    return values * cos_t - (up * low_t + down * high_t)


def chain_step(step, count, size, half, part, landed, full, sems):
    n, j = lax.axis_size("tp"), lax.axis_index("tp")
    for way in (0, 1):
        pos = (n - 1 - j) if way == 0 else j
        ahead, behind = (j - 1, j + 1) if way == 0 else (j + 1, j - 1)

        def sums(i, rows):
            return remote(
                part.at[rows], landed.at[rows], sems.at[4 * way, i], sems.at[4 * way + 1, i], "tp", ahead
            )

        def totals(i, rows):
            return remote(
                full.at[rows], full.at[rows], sems.at[4 * way + 2, i], sems.at[4 * way + 3, i], "tp", behind
            )

        i = step - pos

        @pl.when((i >= 0) & (i < count))
        def _():
            rows = aligned(way * half + i * size, size)

            @pl.when(pos == 0)
            def _():
                sums(i, rows).start()

            @pl.when((pos > 0) & (pos < n - 1))
            def _():
                sums(i, rows).wait_recv()
                part[rows, :] = (part[rows, :].astype(F32) + landed[rows, :].astype(F32)).astype(BF16)
                sums(i, rows).start()

            @pl.when(pos == n - 1)
            def _():
                sums(i, rows).wait_recv()
                full[rows, :] = (part[rows, :].astype(F32) + landed[rows, :].astype(F32)).astype(BF16)
                totals(i, rows).start()

        k = step - (n - 1) - (n - 1 - pos)

        @pl.when((k >= 0) & (k < count) & (pos < n - 1))
        def _():
            rows = aligned(way * half + k * size, size)
            totals(k, rows).wait_recv()

            @pl.when(pos > 0)
            def _():
                totals(k, rows).start()


def chain_drain(count, size, half, part, landed, full, sems):
    n, j = lax.axis_size("tp"), lax.axis_index("tp")
    for way in (0, 1):
        pos = (n - 1 - j) if way == 0 else j
        ahead, behind = (j - 1, j + 1) if way == 0 else (j + 1, j - 1)

        @pl.loop(0, count)
        def _(i):
            rows = aligned(way * half + i * size, size)

            @pl.when(pos < n - 1)
            def _():
                remote(
                    part.at[rows], landed.at[rows], sems.at[4 * way, i], sems.at[4 * way + 1, i], "tp", ahead
                ).wait_send()

            @pl.when(pos > 0)
            def _():
                remote(
                    full.at[rows], full.at[rows], sems.at[4 * way + 2, i], sems.at[4 * way + 3, i], "tp", behind
                ).wait_send()


def forward_kernel(
    x_ref, w_ref, b_ref, cos_ref, low_ref, high_ref, gain_ref, shift_ref,
    n1_ref, qkv_out, own_ref, lse_ref, att_out,
    send_buf, qkv, keys, back_buf, att, out_sem, in_sem, back_out, back_in,
):
    ctx, me = lax.axis_size("ctx"), lax.axis_index("ctx")
    clips, length = lse_ref.shape[0], lse_ref.shape[2]
    local = length // ctx
    heads = b_ref.shape[2] // HD
    greet("ctx")

    def outgoing(clip, step):
        peer = lax.rem(me + step, ctx)
        return remote(
            send_buf.at[clip, :, aligned(peer * HD, HD), :],
            qkv.at[clip, :, :, aligned(me * local, local)],
            out_sem.at[clip, step],
            in_sem.at[clip, step],
            "ctx",
            peer,
        )

    def returning(clip, step):
        peer = lax.rem(me + step, ctx)
        return remote(
            back_buf.at[clip, :, aligned(peer * local, local)],
            att.at[clip, aligned(me * HD, HD), :],
            back_out.at[clip, step],
            back_in.at[clip, step],
            "ctx",
            peer,
        )

    for clip in range(clips):

        @pl.loop(0, local // ROWS)
        def _(block):
            rows = aligned(clip * local + block * ROWS, ROWS)
            lanes = aligned(block * ROWS, ROWS)
            hat, _ = norm_parts(x_ref[rows, :].astype(F32))
            normed = (hat * gain_ref[0:1, :] + shift_ref[0:1, :]).astype(BF16)
            n1_ref[rows, :] = normed
            cos_t = jnp.concatenate([cos_ref[:, rows]] * heads, axis=0)
            low_t = jnp.concatenate([low_ref[:, rows]] * heads, axis=0)
            high_t = jnp.concatenate([high_ref[:, rows]] * heads, axis=0)
            for c in range(3):
                moved = (mm(normed, w_ref[c], 1, 0) + b_ref[c]).T
                if c < 2:
                    moved = turn(moved, cos_t, low_t, high_t, 1)
                moved = moved.astype(BF16)
                if c == 0:
                    moved = moved * jnp.asarray(SCALE, BF16)
                send_buf[clip, c, :, lanes] = moved

        for step in range(1, ctx):
            outgoing(clip, step).start()
        mine = aligned(me * local, local)
        for c in range(3):
            qkv[clip, c, :, mine] = send_buf[clip, c, aligned(me * HD, HD), :]

    for clip in range(clips):
        for step in range(1, ctx):
            outgoing(clip, step).wait_recv()
        keys[...] = qkv[clip, 1].T

        @pl.loop(0, length // QB)
        def _(block):
            lanes = aligned(block * QB, QB)
            scores = mm(keys[...], qkv[clip, 0, :, lanes], 1, 0)
            largest = jnp.max(scores, axis=0, keepdims=True)
            expon = jnp.exp(scores - largest)
            totals = jnp.sum(expon, axis=0, keepdims=True)
            result = mm(qkv[clip, 2], expon.astype(BF16), 1, 0) / totals
            own_ref[clip, :, lanes] = result
            lse_ref[clip, :, lanes] = largest + jnp.log(totals)
            back_buf[clip, :, lanes] = result.astype(BF16)

        qkv_out[clip] = qkv[clip]
        for step in range(1, ctx):
            returning(clip, step).start()
        att[clip, aligned(me * HD, HD), :] = back_buf[clip, :, aligned(me * local, local)]

    for clip in range(clips):
        for step in range(1, ctx):
            returning(clip, step).wait_recv()
        att_out[clip] = att[clip]
    for clip in range(clips):
        for step in range(1, ctx):
            outgoing(clip, step).wait_send()
            returning(clip, step).wait_send()


def middle_kernel(
    count,
    att_ref, x_ref, g_ref, proj_ref, up_ref, down_ref, bup_ref, gain_ref, shift_ref, outs_ref,
    n2_ref, act_ref, dz_ref, mlp_ref, sum_out, dr_ref, drb_ref, grad_out_ref, stats_ref,
    part_a, land_a, full_a, part_b, land_b, full_b, send_buf, grad_land, sem_a, sem_b, out_sem, in_sem,
):
    n = lax.axis_size("tp")
    ctx, me = lax.axis_size("ctx"), lax.axis_index("ctx")
    clips, local = att_ref.shape[0], att_ref.shape[2]
    rows_all = x_ref.shape[0]
    half = rows_all // 2
    size = half // count
    hops = 2 * (n - 1)
    greet("tp", "ctx")
    stats_ref[...] = jnp.zeros_like(stats_ref)

    for clip in range(clips):
        att = att_ref[clip].T

        for block in range(local // ROWS):
            part_a[pl.ds(clip * local + block * ROWS, ROWS), :] = mm(
                att[block * ROWS : (block + 1) * ROWS], proj_ref[...], 1, 0
            ).astype(BF16)

    def both(ref, first, second):
        return jnp.concatenate([ref[first, :], ref[second, :]], axis=0)

    def put(ref, first, second, value):
        value = value.astype(ref.dtype)
        ref[first, :] = value[:size]
        ref[second, :] = value[size:]

    def residual(first, second):
        return (
            both(x_ref, first, second).astype(F32)
            + both(full_a, first, second).astype(F32)
            + outs_ref[0:1, :]
        )

    @pl.loop(0, count + 2 * hops + 1)
    def _(step):
        chain_step(step, count, size, half, part_a, land_a, full_a, sem_a)
        chain_step(step - hops - 1, count, size, half, part_b, land_b, full_b, sem_b)

        i = step - hops

        @pl.when((i >= 0) & (i < count))
        def _():
            first, second = aligned(i * size, size), aligned(half + i * size, size)
            put(sum_out, first, second, both(full_a, first, second))
            hat, _ = norm_parts(residual(first, second))
            normed = (hat * gain_ref[1:2, :] + shift_ref[1:2, :]).astype(BF16)
            put(n2_ref, first, second, normed)
            pre = mm(normed, up_ref[...], 1, 0) + bup_ref[...]
            cdf = 0.5 + 0.5 * lax.erf(pre * (0.5**0.5))
            act = (pre * cdf).astype(BF16)
            put(act_ref, first, second, act)
            slope = cdf + pre * (jnp.exp(-0.5 * pre * pre) * 0.3989422804014327)
            grad = (mm(both(g_ref, first, second), down_ref[...], 1, 1) * slope).astype(BF16)
            put(dz_ref, first, second, grad)
            put(part_b, first, second, mm(grad, up_ref[...], 1, 1))
            put(mlp_ref, first, second, mm(act, down_ref[...], 1, 0))
            stats_ref[4:5, :] += jnp.sum(grad.astype(F32), axis=0, keepdims=True)

        k = step - 2 * hops - 1

        @pl.when(k >= 0)
        def _():
            first, second = aligned(k * size, size), aligned(half + k * size, size)
            hat, rstd = norm_parts(residual(first, second))
            grad = both(full_b, first, second).astype(F32)
            upstream = both(g_ref, first, second).astype(F32)
            moved = upstream + norm_pull(hat, rstd, gain_ref[1:2, :], grad)
            put(dr_ref, first, second, moved)
            put(drb_ref, first, second, moved)
            stats_ref[0:1, :] += jnp.sum(grad * hat, axis=0, keepdims=True)
            stats_ref[1:2, :] += jnp.sum(grad, axis=0, keepdims=True)
            stats_ref[2:3, :] += jnp.sum(moved, axis=0, keepdims=True)
            stats_ref[3:4, :] += jnp.sum(upstream, axis=0, keepdims=True)

    def outgoing(clip, step):
        peer = lax.rem(me + step, ctx)
        return remote(
            send_buf.at[clip, aligned(peer * HD, HD), :],
            grad_land.at[clip, :, aligned(me * local, local)],
            out_sem.at[clip, step],
            in_sem.at[clip, step],
            "ctx",
            peer,
        )

    for clip in range(clips):

        @pl.loop(0, local // ROWS)
        def _(block):
            send_buf[clip, :, aligned(block * ROWS, ROWS)] = mm(
                proj_ref[...], drb_ref[aligned(clip * local + block * ROWS, ROWS), :], 1, 1
            ).astype(BF16)

        for step in range(1, ctx):
            outgoing(clip, step).start()
        grad_land[clip, :, aligned(me * local, local)] = send_buf[clip, aligned(me * HD, HD), :]

    chain_drain(count, size, half, part_a, land_a, full_a, sem_a)
    chain_drain(count, size, half, part_b, land_b, full_b, sem_b)
    for clip in range(clips):
        for step in range(1, ctx):
            outgoing(clip, step).wait_recv()
            outgoing(clip, step).wait_send()
        grad_out_ref[clip] = grad_land[clip]


def backward_kernel(
    count,
    qkv_ref, own_ref, lse_ref, grad_ref, mlp_ref, x_ref, sum_ref, outs_ref, cos_ref, low_ref, high_ref,
    block_ref, dp_ref, bias_ref,
    part, landed, full, query, keys, vals, grads, acc_k, acc_v, send_buf, moved, sem, out_sem, in_sem,
):
    n = lax.axis_size("tp")
    ctx, me = lax.axis_size("ctx"), lax.axis_index("ctx")
    clips, length = lse_ref.shape[0], lse_ref.shape[2]
    local = length // ctx
    heads = moved.shape[2] // HD
    half = x_ref.shape[0] // 2
    size = half // count
    hops = 2 * (n - 1)
    blocks = length // QB
    greet("tp", "ctx")
    part[...] = mlp_ref[...]

    def outgoing(clip, step):
        peer = lax.rem(me + step, ctx)
        return remote(
            send_buf.at[clip, :, :, aligned(peer * local, local)],
            moved.at[clip, :, aligned(me * HD, HD), :],
            out_sem.at[clip, step],
            in_sem.at[clip, step],
            "ctx",
            peer,
        )

    def finish(i):
        @pl.when((i >= 0) & (i < count))
        def _():
            for way in (0, 1):
                rows = aligned(way * half + i * size, size)
                block_ref[rows, :] = (
                    x_ref[rows, :].astype(F32)
                    + sum_ref[rows, :].astype(F32)
                    + outs_ref[0:1, :]
                    + full[rows, :].astype(F32)
                    + outs_ref[1:2, :]
                ).astype(BF16)

    for clip in range(clips):
        query[...] = qkv_ref[clip, 0].T
        keys[...] = qkv_ref[clip, 1].T
        vals[...] = qkv_ref[clip, 2].T
        grads[...] = grad_ref[clip].T
        acc_k[...] = jnp.zeros_like(acc_k)
        acc_v[...] = jnp.zeros_like(acc_v)

        @pl.loop(0, blocks)
        def _(block):
            at = clip * blocks + block
            chain_step(at, count, size, half, part, landed, full, sem)
            finish(at - hops)
            lanes = aligned(block * QB, QB)
            grad_t = grad_ref[clip, :, lanes]
            scores = mm(keys[...], qkv_ref[clip, 0, :, lanes], 1, 0)
            probs = jnp.exp(scores - lse_ref[clip, :, lanes])
            inner = jnp.sum(grad_t.astype(F32) * own_ref[clip, :, lanes], axis=0, keepdims=True)
            grad_probs = mm(vals[...], grad_t, 1, 0)
            grad_scores = (probs * (grad_probs - inner)).astype(BF16)
            acc_v[...] += mm(probs.astype(BF16), grads[lanes, :], 1, 0)
            acc_k[...] += mm(grad_scores, query[lanes, :], 1, 0)
            send_buf[clip, 0, :, lanes] = (mm(qkv_ref[clip, 1], grad_scores, 1, 0) * SCALE).astype(BF16)

        send_buf[clip, 1] = acc_k[...].T.astype(BF16)
        send_buf[clip, 2] = acc_v[...].T.astype(BF16)
        for step in range(1, ctx):
            outgoing(clip, step).start()
        for c in range(3):
            moved[clip, c, aligned(me * HD, HD), :] = send_buf[clip, c, :, aligned(me * local, local)]

    for extra in range(clips * blocks, count + hops):
        chain_step(extra, count, size, half, part, landed, full, sem)
        finish(extra - hops)

    bias_ref[...] = jnp.zeros_like(bias_ref)
    for clip in range(clips):
        for step in range(1, ctx):
            outgoing(clip, step).wait_recv()

        @pl.loop(0, local // ROWS)
        def _(block):
            lanes = aligned(block * ROWS, ROWS)
            rows = aligned(clip * local + block * ROWS, ROWS)
            cos_t = jnp.concatenate([cos_ref[:, rows]] * heads, axis=0)
            low_t = jnp.concatenate([low_ref[:, rows]] * heads, axis=0)
            high_t = jnp.concatenate([high_ref[:, rows]] * heads, axis=0)
            for c in range(3):
                value = moved[clip, c, :, lanes].astype(F32)
                if c < 2:
                    value = turn(value, cos_t, low_t, high_t, -1)
                value = value.T.astype(BF16)
                dp_ref[c, rows, :] = value
                bias_ref[c : c + 1, :] += jnp.sum(value.astype(F32), axis=0, keepdims=True)

    chain_drain(count, size, half, part, landed, full, sem)
    for clip in range(clips):
        for step in range(1, ctx):
            outgoing(clip, step).wait_send()


def last_kernel(
    count, dp_ref, w_ref, x_ref, dr_ref, gain_ref, grad_in_ref, stats_ref, part, landed, full, sem
):
    n = lax.axis_size("tp")
    rows_all = x_ref.shape[0]
    half = rows_all // 2
    size = half // count
    hops = 2 * (n - 1)
    greet("tp")
    stats_ref[...] = jnp.zeros_like(stats_ref)

    @pl.loop(0, rows_all // ROWS)
    def _(block):
        rows = aligned(block * ROWS, ROWS)
        total = mm(dp_ref[0, rows, :], w_ref[0], 1, 1)
        for c in (1, 2):
            total = total + mm(dp_ref[c, rows, :], w_ref[c], 1, 1)
        part[rows, :] = total.astype(BF16)

    @pl.loop(0, count + hops)
    def _(step):
        chain_step(step, count, size, half, part, landed, full, sem)
        i = step - hops

        @pl.when(i >= 0)
        def _():
            for way in (0, 1):
                rows = aligned(way * half + i * size, size)
                hat, rstd = norm_parts(x_ref[rows, :].astype(F32))
                grad = full[rows, :].astype(F32)
                grad_in_ref[rows, :] = dr_ref[rows, :] + norm_pull(hat, rstd, gain_ref[0:1, :], grad)
                stats_ref[0:1, :] += jnp.sum(grad * hat, axis=0, keepdims=True)
                stats_ref[1:2, :] += jnp.sum(grad, axis=0, keepdims=True)

    chain_drain(count, size, half, part, landed, full, sem)


def contract_rows(left_mat, right_mat):
    return lax.dot_general(
        left_mat, right_mat, (((0,), (0,)), ((), ())), preferred_element_type=jnp.float32
    )


def rotary_tables(positions):
    rows = positions.shape[1]
    half = ROT // 2
    freqs = 10000.0 ** (-2.0 * jnp.arange(half, dtype=F32) / ROT)
    angles = positions.astype(F32)[:, None, :] * freqs[None, :, None]
    cos, sin = jnp.cos(angles), jnp.sin(angles)
    zero = jnp.zeros_like(sin)
    rest = HD - 3 * ROT

    def fill(first, second, value):
        table = jnp.concatenate([first, second], axis=1).reshape(3 * ROT, rows)
        return jnp.concatenate([table, jnp.full((rest, rows), value, F32)], axis=0)

    return fill(cos, cos, 1.0), fill(-sin, zero, 0.0), fill(zero, sin, 0.0)


VMEM = pl.BlockSpec(memory_space=pltpu.VMEM)


def call(kernel, name, number, ins, outs, scratch, flops):
    moved = sum(a.size * a.dtype.itemsize for a in (*ins, *outs))
    return pl.pallas_call(
        kernel,
        name=name,
        out_shape=outs,
        in_specs=[VMEM] * len(ins),
        out_specs=[VMEM] * len(outs),
        scratch_shapes=scratch,
        cost_estimate=pl.CostEstimate(flops=flops, bytes_accessed=moved, transcendentals=0),
        compiler_params=pltpu.CompilerParams(
            collective_id=number, has_side_effects=True, vmem_limit_bytes=60 * 1024 * 1024
        ),
    )(*ins)


def shards(
    block_input, positions, w_qkv, b_qkv, w_proj, w_up, b_up, w_down,
    norm_gains, norm_shifts, out_shifts, grad_out,
):
    clips, local, width = block_input.shape
    rows = clips * local
    ctx, n = lax.axis_size("ctx"), lax.axis_size("tp")
    lane = w_qkv.shape[2]
    hidden = w_up.shape[1]
    length = local * ctx
    assert lane == ctx * HD and clips == 2 and hidden == width
    count = max(1, rows // 2 // 64)
    dma = pltpu.SemaphoreType.DMA
    shape = jax.ShapeDtypeStruct

    full_qkv = lax.all_gather(w_qkv, "fsdp", axis=1, tiled=True)
    full_proj = lax.all_gather(w_proj, "fsdp", axis=1, tiled=True)
    full_up = lax.all_gather(w_up, "fsdp", axis=0, tiled=True)
    full_down = lax.all_gather(w_down, "fsdp", axis=1, tiled=True)

    x = block_input.reshape(rows, width)
    g = grad_out.reshape(rows, width)
    tables = rotary_tables(positions.reshape(3, rows))

    n1, qkv, own, lse, att = call(
        forward_kernel,
        "forward",
        0,
        (x, full_qkv, b_qkv.reshape(3, 1, lane), *tables, norm_gains, norm_shifts),
        (
            shape((rows, width), BF16),
            shape((clips, 3, HD, length), BF16),
            shape((clips, HD, length), F32),
            shape((clips, 1, length), F32),
            shape((clips, lane, local), BF16),
        ),
        [
            pltpu.VMEM((clips, 3, lane, local), BF16),
            pltpu.VMEM((clips, 3, HD, length), BF16),
            pltpu.VMEM((length, HD), BF16),
            pltpu.VMEM((clips, HD, length), BF16),
            pltpu.VMEM((clips, lane, local), BF16),
            dma((clips, ctx)),
            dma((clips, ctx)),
            dma((clips, ctx)),
            dma((clips, ctx)),
        ],
        2 * rows * width * 3 * lane + 4 * clips * length * length * HD,
    )

    wide = shape((rows, width), BF16)
    wide32 = shape((rows, width), F32)
    chain = [pltpu.VMEM((rows, width), BF16)] * 3
    n2, act, dz, mlp, summed, dr, drb, grad_att, stats_two = call(
        functools.partial(middle_kernel, count),
        "middle",
        1,
        (att, x, g, full_proj, full_up, full_down, b_up.reshape(1, hidden), norm_gains, norm_shifts, out_shifts),
        (
            wide, wide, wide, wide, wide, wide32, wide,
            shape((clips, HD, length), BF16),
            shape((8, width), F32),
        ),
        chain
        + chain
        + [
            pltpu.VMEM((clips, lane, local), BF16),
            pltpu.VMEM((clips, HD, length), BF16),
            dma((8, count)),
            dma((8, count)),
            dma((clips, ctx)),
            dma((clips, ctx)),
        ],
        8 * rows * width * hidden,
    )
    grad_down = contract_rows(act, g)
    grad_up = contract_rows(n2, dz)
    grad_proj = mm(att.transpose(1, 0, 2).reshape(lane, rows), drb, 1, 0)

    block_output, dp, bias = call(
        functools.partial(backward_kernel, count),
        "backward",
        2,
        (qkv, own, lse, grad_att, mlp, x, summed, out_shifts, *tables),
        (wide, shape((3, rows, lane), BF16), shape((8, lane), F32)),
        chain
        + [
            pltpu.VMEM((length, HD), BF16),
            pltpu.VMEM((length, HD), BF16),
            pltpu.VMEM((length, HD), BF16),
            pltpu.VMEM((length, HD), BF16),
            pltpu.VMEM((length, HD), F32),
            pltpu.VMEM((length, HD), F32),
            pltpu.VMEM((clips, 3, HD, length), BF16),
            pltpu.VMEM((clips, 3, lane, local), BF16),
            dma((8, count)),
            dma((clips, ctx)),
            dma((clips, ctx)),
        ],
        10 * clips * length * length * HD,
    )
    grad_qkv = jnp.einsum("rd,cre->cde", n1, dp, preferred_element_type=F32)

    grad_input, stats_one = call(
        functools.partial(last_kernel, count),
        "last",
        3,
        (dp, full_qkv, x, dr, norm_gains),
        (wide32, shape((8, width), F32)),
        chain + [dma((8, count))],
        2 * rows * width * 3 * lane,
    )

    def scatter(grad, axis):
        return lax.psum_scatter(grad.astype(BF16), "fsdp", scatter_dimension=axis, tiled=True)

    def total(part):
        return lax.psum(part, "ctx").astype(F32)

    shard_down = total(scatter(grad_down, 1))
    shard_up = total(scatter(grad_up, 0))
    shard_proj = total(scatter(grad_proj, 1))
    shard_qkv = total(scatter(grad_qkv, 1))
    gains, shifts, outs, bqkv, bup = lax.psum(
        (
            jnp.stack([stats_one[0], stats_two[0]]),
            jnp.stack([stats_one[1], stats_two[1]]),
            stats_two[2:4],
            bias[:3],
            stats_two[4],
        ),
        ("fsdp", "ctx"),
    )
    return (
        block_output.reshape(clips, local, width),
        grad_input.reshape(clips, local, width),
        shard_qkv,
        bqkv,
        shard_proj,
        shard_up,
        bup,
        shard_down,
        gains,
        shifts,
        outs,
    )


def solution(mesh):
    rows = P("fsdp", "ctx", None)
    in_specs = (
        rows,
        P(None, "fsdp", "ctx"),
        P(None, "fsdp", "tp"),
        P(None, "tp"),
        P("tp", "fsdp"),
        P("fsdp", "tp"),
        P("tp"),
        P("tp", "fsdp"),
        P(),
        P(),
        P(),
        rows,
    )
    out_specs = (
        rows,
        rows,
        P(None, "fsdp", "tp"),
        P(None, "tp"),
        P("tp", "fsdp"),
        P("fsdp", "tp"),
        P("tp"),
        P("tp", "fsdp"),
        P(),
        P(),
        P(),
    )
    return jax.shard_map(shards, mesh=mesh, in_specs=in_specs, out_specs=out_specs, check_vma=False)
```

time: 888 us -> 557 us (0.63); the launches traced: 875 us -> 556 us
  Pallas kernels: 0 us -> 344 us
  waiting for transfers between devices: 461 us -> 124 us
  local copies, waits for them, and re-layouts: 130 us -> 13 us
  matrix products: 113 us -> 18.7 us
  other arithmetic: 71.1 us -> 6.18 us
  blocking collectives: 60.2 us -> 35.6 us
  starting transfers between devices: 23.8 us -> 0.72 us
    psum x4 -> x1, waiting for transfers between devices: 348 us -> 0.01 us  [total(): return lax.psum(part, 'ctx').astype(F32)]
    pallas_call x0 -> x4, Pallas kernels: none -> 344 us  [call(): pl.pallas_call(kernel, name=name, out_shape=outs, in_specs=[VMEM] * len(i...]
    dot_general x49 -> x2, matrix products: 92.1 us -> 7.5 us  [the longest x1 4.38 us: shards(): grad_qkv = jnp.einsum('rd,cre->cde', n1, dp, preferred_element_type=F32)]
    reduce_scatter x4, waiting for transfers between devices: 12 us -> 80.9 us  [scatter(): lax.psum_scatter(grad.astype(BF16), 'fsdp', scatter_dimension=axis, tiled...]
    dynamic_update_slice x16 -> x0, local copies, waits for them, and re-layouts: 52.4 us -> none  [the longest x4 51.9 us: shards(): lax.map(backward_group, (grouped[0], grouped[1], grouped[2], grad_grouped...]
    all_gather x3, waiting for transfers between devices: 78.1 us -> 40.7 us  [the longest x1 26.2 us: shards(): full_down = lax.all_gather(w_down, 'fsdp', axis=1, tiled=True)]
    reduce_sum x19 -> x0, other arithmetic: 33.6 us -> none  [the longest x4 13 us: layer_norm(): return center * lax.rsqrt(spread + EPSILON) * gain_vec + shift_vec]
    all_to_all x1 -> x0, blocking collectives: 24.7 us -> none  [shards(): lax.all_to_all(grad_heads, 'ctx', split_axis=2, concat_axis=3, tiled=True)]
  transfers between devices with their start and end apart: 14 -> 8, of which waited for: 10 -> 5; matrix products, arithmetic and copies ran while one was open for 24% -> 4% of each run, Pallas kernels for 0% -> 38%
where the time goes in v1:
time: 557 us; the launch traced here: 556 us
  Pallas kernels  344 us (62%)
  waiting for transfers between devices  124 us (22%)
  blocking collectives  35.6 us (6%)
  matrix products  18.7 us (3%)
  between operations  14.4 us (3%)
  local copies, waits for them, and re-layouts  13 us (2%)
  other arithmetic  6.18 us (1%)
    pallas_call x4, Pallas kernels, call(): pl.pallas_call(kernel, name=name, out_shape=outs, in_specs=[VMEM] * len(i...  344 us
    reduce_scatter x4, waiting for transfers between devices, scatter(): lax.psum_scatter(grad.astype(BF16), 'fsdp', scatter_dimension=axis, tiled...  80.9 us
    all_gather x1, waiting for transfers between devices, shards(): full_down = lax.all_gather(w_down, 'fsdp', axis=1, tiled=True)  26.2 us
    psum x1, blocking collectives, shards(): lax.psum((jnp.stack([stats_one[0], stats_two[0]]), jnp.stack([stats_one[1...  23 us
    all_gather x1, waiting for transfers between devices, shards(): full_qkv = lax.all_gather(w_qkv, 'fsdp', axis=1, tiled=True)  14.5 us
    all_gather x1, blocking collectives, shards(): full_proj = lax.all_gather(w_proj, 'fsdp', axis=1, tiled=True)  12.6 us
    dot_general x2, matrix products, contract_rows(): lax.dot_general(left_mat, right_mat, (((0,), (0,)), ((), ())), preferred_...  11.2 us
  transfers between devices with their start and end apart: 8, of which 5 were waited for; matrix products, arithmetic and copies ran while one was open for 4% of the time, Pallas kernels for 38%

profile of v1, /device:TPU:0, one launch (start us, length us, event | category | flops | bytes accessed | tf_op | source)
XLA Modules:
  0.0 556.5 jit_solution(3800352462982913598)
XLA Ops:
  7.2 0.0 copy-start.7
  7.2 0.0 all-gather.4.cloned.1.call-start
  7.2 0.7 all-gather.4.cloned.1.call-update
  7.9 0.0 all-gather.6.cloned.1.call-start
  8.0 0.7 all-gather.6.cloned.1.call-update
  8.7 0.0 all-gather.8.cloned.1.call-start
  8.7 0.7 all-gather.8.cloned.1.call-update
  9.4 0.0 reduce-scatter.7.cloned.1.call-start
  9.5 0.0 copy-done.7
  9.5 0.8 multiply_sine_fusion
  10.3 0.0 copy-start.8
  10.3 0.0 copy-start.4
  10.4 0.7 concatenate.21.low_ref
  11.2 0.7 concatenate.23.high_ref
  11.9 0.0 copy-done.8
  11.9 0.6 reshape.65.b_ref
  12.5 0.7 concatenate.19.cos_ref
  13.2 0.0 copy-done.4
  13.2 12.6 %all_gather.13.proj_ref = bf16[256,1024]{1,0:T(8,128)(2,1)} all-gather(bf16[256,512]{1,0:T(8,128)(2,1)S(1)} %copy-done.4), channel_id=1, replica_groups=mesh['fsdp'=2,'ctx'=4,'tp'=4] {'fsdp'}, dimensions={1}, use_global_device_ids=true | all-gather | bytes 786432 | tf_op jit(solution)/shard_map/all_gather | solution.py:552
  25.8 14.5 %all-gather.4.cloned.1.call-done.w_ref = bf16[3,1024,256]{2,1,0:T(8,128)(2,1)} async-done(((bf16[3,512,256]{2,1,0:T(8,128)(2,1)}), bf16[3,1024,256]{2,1,0:T(8,128)(2,1)}) %all-gather.4.cloned.1.call-update) | async-done | bytes 1572880 | tf_op jit(solution)/shard_map/all_gather | solution.py:551
  40.3 43.3 %forward.1 = (bf16[1024,1024]{1,0:T(8,128)(2,1)}, bf16[2,3,64,2048]{3,2,1,0:T(8,128)(2,1)}, f32[2,64,2048]{2,1,0:T(8,128)}, f32[2,1,2048]{2,1,0:T(1,128)}, bf16[2,256,512]{2,1,0:T(8,128)(2,1)}) custom-call(bf16[1024,1024]{1,0:T(8,128)(2,1)} %bitcast.30, bf16[3,1024,256]{2,1,0:T(8,128)(2,1)} %all-gather.4.cloned.1.call-done.w_ref, ...), custom_call_target="tpu_custom_call" | custom-call | flops 3758096384 | bytes 9735168 | tf_op jit(solution)/shard_map/forward/pallas_call | solution.py:522
  83.6 1.3 copy.26
  84.9 0.0 all-gather.6.cloned.1.call-done.up_ref
  84.9 26.2 %all-gather.8.cloned.1.call-done.down_ref = bf16[1024,1024]{1,0:T(8,128)(2,1)} async-done(((bf16[1024,512]{1,0:T(8,128)(2,1)}), bf16[1024,1024]{1,0:T(8,128)(2,1)}) %all-gather.8.cloned.1.call-update) | async-done | bytes 2097168 | tf_op jit(solution)/shard_map/all_gather | solution.py:554
  111.1 133.7 %middle.1 = (bf16[1024,1024]{1,0:T(8,128)(2,1)}, bf16[1024,1024]{1,0:T(8,128)(2,1)}, bf16[1024,1024]{1,0:T(8,128)(2,1)}, bf16[1024,1024]{1,0:T(8,128)(2,1)}, bf1...) custom-call(bf16[2,256,512]{2,1,0:T(8,128)(2,1)} %get-tuple-element., ...), custom_call_target="tpu_custom_call" | custom-call | flops 8589934592 | bytes 26800128 | tf_op jit(solution)/shard_map/middle/pallas_call | solution.py:522
  244.9 3.1 convolution_convert_fusion.2
  248.0 0.0 reduce-scatter.7.cloned.1.call-update
  248.0 0.2 reduce-scatter.5.cloned.1.call-start
  248.2 0.0 copy-start.11
  248.2 86.1 %backward.1 = (bf16[1024,1024]{1,0:T(8,128)(2,1)}, bf16[3,1024,256]{2,1,0:T(8,128)(2,1)}, f32[8,256]{1,0:T(8,128)}) custom-call(bf16[2,3,64,2048]{3,2,1,0:T(8,128)(2,1)} %get-tuple-element.30.qkv_ref, f32[2,64,2048]{2,1,0:T(8,128)} %get-tuple-element.31.own_ref, f32[2,1,2048]{2,1,0:T(1,128)} %get-tuple-element.32.lse_ref, ...), custom_call_target="tpu_custom_call" | custom-call | flops 5368709120 | bytes 13926400 | tf_op jit(solution)/shard_map/backward/pallas_call | solution.py:522
  334.3 0.0 copy-done.11
  334.3 4.4 fusion.5
  338.7 0.0 reduce-scatter.5.cloned.1.call-update
  338.7 0.0 reduce-scatter.9.cloned.1.call-start
  338.8 5.9 %convolution_convert_fusion.1 = bf16[1024,1024]{1,0:T(8,128)(2,1)} fusion(bf16[1024,1024]{1,0:T(8,128)(2,1)} %get-tuple-element.44, bf16[1024,1024]{1,0:T(8,128)(2,1)} %get-tuple-element.45), kind=kOutput, calls=%fused_computation.3 | convolution fusion | flops 2148532224 | bytes 6291456 | tf_op jit(solution)/shard_map/dot_general | solution.py:496
  344.7 0.0 reduce-scatter.9.cloned.1.call-update
  344.7 0.0 reduce-scatter.11.cloned.1.call-start
  344.8 1.5 copy-done.10
  346.3 5.3 convolution_convert_fusion
  351.6 0.0 reduce-scatter.11.cloned.1.call-update
  351.6 0.0 copy-start.9
  351.6 0.0 copy-start.6
  351.6 0.3 all-reduce.9.cloned.1.call-start
  351.9 0.0 reduce-scatter.7.cloned.1.call-done
  351.9 11.6 %reduce-scatter.5.cloned.1.call-done = bf16[3,512,256]{1,2,0:T(8,128)(2,1)} async-done(((bf16[3,1024,256]{1,2,0:T(8,128)(2,1)}), bf16[3,512,256]{1,2,0:T(8,128)(2,1)}) %reduce-scatter.5.cloned.1.call-update) | async-done | bytes 786448 | tf_op jit(solution)/shard_map/reduce_scatter | solution.py:650
  363.5 34.6 %reduce-scatter.9.cloned.1.call-done = bf16[512,1024]{1,0:T(8,128)(2,1)} async-done(((bf16[1024,1024]{1,0:T(8,128)(2,1)}), bf16[512,1024]{1,0:T(8,128)(2,1)}) %reduce-scatter.9.cloned.1.call-update) | async-done | bytes 1048592 | tf_op jit(solution)/shard_map/reduce_scatter | solution.py:650
  398.1 34.8 %reduce-scatter.11.cloned.1.call-done = bf16[1024,512]{1,0:T(8,128)(2,1)} async-done(((bf16[1024,1024]{1,0:T(8,128)(2,1)}), bf16[1024,512]{1,0:T(8,128)(2,1)}) %reduce-scatter.11.cloned.1.call-update) | async-done | bytes 1048592 | tf_op jit(solution)/shard_map/reduce_scatter | solution.py:650
  432.8 0.0 all-reduce.9.cloned.1.call-update
  432.9 0.0 copy-done.9
  432.9 0.0 copy-done.6
  432.9 81.1 %last.1 = (f32[1024,1024]{1,0:T(8,128)}, f32[8,1024]{1,0:T(8,128)}) custom-call(bf16[3,1024,256]{2,1,0:T(8,128)(2,1)} %get-tuple-element.38.dp_ref, bf16[3,1024,256]{2,1,0:T(8,128)(2,1)} %all-gather.4.cloned.1.call-done.w_ref, bf16[1024,1024]{1,0:T(8,128)(2,1)} %bitcast.33, f32[1024,1024]{1,0:T(8,128)} %get-tuple-element.39.dr_ref, f32[2,1024]{1,0:T(2,128)} %gain_ref.5), custom_call_target="tpu_custom_call" | custom-call | flops 1610612736 | bytes 13672448 | tf_op jit(solution)/shard_map/last/pallas_call | solution.py:522
  514.0 0.8 fusion.9
  514.9 23.0 %all-reduce.5 = (f32[3,256]{1,0:T(4,128)}, f32[1024]{0:T(1024)}, f32[2,1024]{1,0:T(2,128)}, f32[2,1024]{1,0:T(2,128)}, f32[2,1024]{1,0:T(2,128)}) all-reduce(f32[3,256]{1,0:T(4,128)S(1)} %slice.21, f32[1024]{0:T(1024)S(1)} %bitcast.36, f32[2,1024]{1,0:T(2,128)S(1)} %get-tuple-element.88, ...), channel_id=1, replica_groups=mesh['fsdp'=2,'ctx'=4,'tp'=4] {'fsdp','ctx'}, use_global_device_ids=true, to_apply=%region_2.0 | all-reduce | flops 7936 | bytes 63488 | tf_op jit(solution)/shard_map/psum | solution.py:659
  537.9 2.9 convert_element_type.45
  540.8 0.0 copy-done.2
  540.8 1.6 convert_element_type.47
  542.4 0.0 copy-done.3
  542.4 1.4 copy.27
  543.8 0.0 copy-done.5
  543.8 0.9 convert_element_type.43
  544.7 0.0 copy-done.1
  544.7 1.3 copy.36
  546.0 1.6 copy-done
  547.6 2.0 copy.37
  (20 shorter events, 0.2 us)
Async XLA Ops:
  7.2 2.3 copy-start.7
  7.2 33.1 %all-gather.4.cloned.1.call-start = ((), (), s32[]{:S(2)}) async-start(), calls=%async_computation.4 | async-start | bytes 2359296 | tf_op jit(solution)/shard_map/all_gather | solution.py:551
  7.9 77.0 %all-gather.6.cloned.1.call-start = ((), (), s32[]{:S(2)}) async-start(), calls=%async_computation.5 | async-start | bytes 3145728 | tf_op jit(solution)/shard_map/all_gather | solution.py:553
  8.7 102.5 %all-gather.8.cloned.1.call-start = ((), (), s32[]{:S(2)}) async-start(), calls=%async_computation.6 | async-start | bytes 3145728 | tf_op jit(solution)/shard_map/all_gather | solution.py:554
  9.4 342.5 %reduce-scatter.7.cloned.1.call-start = ((), (), s32[]{:S(2)}) async-start(), calls=%async_computation.8 | async-start | bytes 786432 | tf_op jit(solution)/shard_map/reduce_scatter | solution.py:650
  10.3 1.7 copy-start.8
  10.3 2.9 copy-start.4
  248.0 115.5 %reduce-scatter.5.cloned.1.call-start = ((), (), s32[]{:S(2)}) async-start(), calls=%async_computation.7 | async-start | bytes 2359296 | tf_op jit(solution)/shard_map/reduce_scatter | solution.py:650
  248.2 86.1 %copy-start.11 = (bf16[1024,1024]{1,0:T(8,128)(2,1)S(1)}, bf16[1024,1024]{1,0:T(8,128)(2,1)}, u32[]{:S(2)}) copy-start(bf16[1024,1024]{1,0:T(8,128)(2,1)} %get-tuple-element.41) | copy-start | bytes 6291460
  338.7 59.4 %reduce-scatter.9.cloned.1.call-start = ((), (), s32[]{:S(2)}) async-start(), calls=%async_computation.9 | async-start | bytes 3145728 | tf_op jit(solution)/shard_map/reduce_scatter | solution.py:650
  344.7 1.6 copy-start.10
  344.7 88.1 %reduce-scatter.11.cloned.1.call-start = ((), (), s32[]{:S(2)}) async-start(), calls=%async_computation.10 | async-start | bytes 3145728 | tf_op jit(solution)/shard_map/reduce_scatter | solution.py:650
  351.6 81.3 %copy-start.9 = (f32[8,256]{1,0:T(8,128)S(1)}, f32[8,256]{1,0:T(8,128)}, u32[]{:S(2)}) copy-start(f32[8,256]{1,0:T(8,128)} %get-tuple-element.42) | copy-start | bytes 24580
  351.6 81.3 %copy-start.6 = (f32[8,1024]{1,0:T(8,128)S(1)}, f32[8,1024]{1,0:T(8,128)}, u32[]{:S(2)}) copy-start(f32[8,1024]{1,0:T(8,128)} %get-tuple-element.46) | copy-start | bytes 98308
  351.6 186.3 %all-reduce.9.cloned.1.call-start = ((), (), s32[]{:S(2)}) async-start(), calls=%async_computation.11 | async-start | bytes 6291456 | tf_op jit(solution)/shard_map/psum | solution.py:653
  537.9 2.9 copy-start.2
  540.8 1.6 copy-start.3
  540.8 3.0 copy-start.5
  542.4 2.3 copy-start.1
  544.7 2.9 copy-start
Sparse Core Ops, SparseCore 0:
  9.5 30.7 all-gather.3
  41.8 34.5 all-gather.5
  78.0 33.0 all-gather.7
  248.1 12.6 reduce-scatter.6
  338.8 24.6 reduce-scatter.4
  366.2 31.8 reduce-scatter.8
  400.9 31.8 reduce-scatter.10
  435.4 68.4 all-reduce.8

commit v2 on v1

--- a/solution.py
+++ b/solution.py
@@ -12,6 +12,7 @@
 EPSILON = 1e-06
 SCALE = HD ** (-0.5)
 QB = 256
+CHUNK = 64
 ROWS = 128
 MESH = pl.DeviceIdType.MESH
 F32, BF16 = jnp.float32, jnp.bfloat16
@@ -24,12 +25,16 @@
 
 
 def remote(src, dst, send_sem, recv_sem, axis, peer):
+    return remote_at(src, dst, send_sem, recv_sem, {axis: peer})
+
+
+def remote_at(src, dst, send_sem, recv_sem, device):
     return pltpu.make_async_remote_copy(
         src_ref=src,
         dst_ref=dst,
         send_sem=send_sem,
         recv_sem=recv_sem,
-        device_id={axis: peer},
+        device_id=device,
         device_id_type=MESH,
     )
 
@@ -47,6 +52,34 @@
     pl.semaphore_wait(barrier, total)
 
 
+def spot(index):
+    ctx = lax.axis_size("ctx")
+    return {"fsdp": index // ctx, "ctx": lax.rem(index, ctx)}
+
+
+def greet_grid(*axes):
+    barrier = pltpu.get_barrier_semaphore()
+    ctx = lax.axis_size("ctx")
+    size = lax.axis_size("fsdp") * ctx
+    me = lax.axis_index("fsdp") * ctx + lax.axis_index("ctx")
+
+    @pl.loop(1, size)
+    def _(step):
+        pl.semaphore_signal(
+            barrier, inc=1, device_id=spot(lax.rem(me + step, size)), device_id_type=MESH
+        )
+
+    total = size - 1
+    for axis in axes:
+        count, own = lax.axis_size(axis), lax.axis_index(axis)
+        for step in range(1, count):
+            pl.semaphore_signal(
+                barrier, inc=1, device_id={axis: lax.rem(own + step, count)}, device_id_type=MESH
+            )
+            total += 1
+    pl.semaphore_wait(barrier, total)
+
+
 def aligned(start, size):
     return pl.ds(pl.multiple_of(start, size), size)
 
@@ -148,16 +181,182 @@
                 ).wait_send()
 
 
+class GradientSum:
+    def __init__(self, grad, pair, summed, landed, shared, pair_sem, cross_sem, share_sem):
+        self.grad, self.pair, self.summed, self.landed, self.shared = grad, pair, summed, landed, shared
+        self.pair_sem, self.cross_sem, self.share_sem = pair_sem, cross_sem, share_sem
+        self.ctx, self.me = lax.axis_size("ctx"), lax.axis_index("ctx")
+        self.group = self.ctx // 2
+        self.count = grad.shape[0]
+        self.odd = lax.rem(self.me, 2)
+        self.own = lax.axis_index("fsdp") * self.group + self.me // 2
+
+    def pair_copy(self):
+        return remote(
+            self.grad.at[:, 1 - self.odd], self.pair, self.pair_sem.at[0], self.pair_sem.at[1],
+            "ctx", self.me + 1 - 2 * self.odd,
+        )
+
+    def cross_copy(self, step):
+        to = lax.rem(self.own + step, self.count)
+        return remote_at(
+            self.summed.at[to], self.landed.at[self.own],
+            self.cross_sem.at[0, step], self.cross_sem.at[1, step],
+            {"fsdp": to // self.group, "ctx": 2 * lax.rem(to, self.group) + self.odd},
+        )
+
+    def share_copy(self, step):
+        return remote(
+            self.shared.at[self.me], self.shared.at[self.me],
+            self.share_sem.at[0, step], self.share_sem.at[1, step],
+            "ctx", lax.rem(self.me + step, self.ctx),
+        )
+
+    def start_pair(self):
+        self.pair_copy().start()
+
+    def sum_pair(self):
+        self.pair_copy().wait_recv()
+
+        @pl.loop(0, self.count)
+        def _(i):
+            value = (self.grad[i, self.odd].astype(F32) + self.pair[i].astype(F32)).astype(BF16)
+            self.summed[i] = value
+
+        self.landed[self.own] = self.summed[self.own]
+
+    def start_cross(self):
+        @pl.loop(1, self.count)
+        def _(step):
+            self.cross_copy(step).start()
+
+    def sum_cross(self):
+        @pl.loop(1, self.count)
+        def _(step):
+            self.cross_copy(step).wait_recv()
+
+        rows = self.grad.shape[2]
+        part = min(rows, 32)
+
+        @pl.loop(0, rows // part)
+        def _(block):
+            at = aligned(block * part, part)
+            total = self.landed[0, at, :].astype(F32)
+            for i in range(1, self.count):
+                total = total + self.landed[i, at, :].astype(F32)
+            self.shared[self.me, at, :] = total.astype(BF16)
+
+    def start_share(self):
+        @pl.loop(1, self.ctx)
+        def _(step):
+            self.share_copy(step).start()
+
+    def wait_share(self):
+        @pl.loop(1, self.ctx)
+        def _(step):
+            self.share_copy(step).wait_recv()
+
+    def drain(self):
+        self.pair_copy().wait_send()
+
+        @pl.loop(1, self.count)
+        def _(step):
+            self.cross_copy(step).wait_send()
+
+        @pl.loop(1, self.ctx)
+        def _(step):
+            self.share_copy(step).wait_send()
+
+
+def gradient_scratch(pieces, ctx, rows, lanes):
+    half = pieces // 2
+    return [
+        pltpu.VMEM((half, rows, lanes), BF16),
+        pltpu.VMEM((half, rows, lanes), BF16),
+        pltpu.VMEM((half, rows, lanes), BF16),
+        pltpu.VMEM((ctx, rows, lanes), BF16),
+        pltpu.SemaphoreType.DMA((2,)),
+        pltpu.SemaphoreType.DMA((2, half)),
+        pltpu.SemaphoreType.DMA((2, ctx)),
+    ]
+
+
+def put_pieces(grad, unit, lanes, value):
+    value = value.astype(BF16)
+    rows = grad.shape[2]
+    if rows == ROWS:
+        grad[unit // 2, lax.rem(unit, 2), :, lanes] = value
+    else:
+        many = ROWS // (2 * rows)
+        grad[pl.ds(unit * many, many), :, :, lanes] = value.reshape(many, 2, rows, value.shape[1])
+
+
 def forward_kernel(
-    x_ref, w_ref, b_ref, cos_ref, low_ref, high_ref, gain_ref, shift_ref,
-    n1_ref, qkv_out, own_ref, lse_ref, att_out,
-    send_buf, qkv, keys, back_buf, att, out_sem, in_sem, back_out, back_in,
+    x_ref, w_ref, up_ref, down_ref, proj_ref, b_ref, cos_ref, low_ref, high_ref, gain_ref, shift_ref,
+    n1_ref, qkv_out, own_ref, lse_ref, att_out, w_out, up_out, down_out, proj_out,
+    send_buf, qkv, keys, back_buf, att, w_full, up_full, down_full, proj_full, down_t, proj_t,
+    out_sem, in_sem, back_out, back_in, fetch_out, fetch_in, pass_out, pass_in, keep_sem,
 ):
     ctx, me = lax.axis_size("ctx"), lax.axis_index("ctx")
+    fsdp, f = lax.axis_size("fsdp"), lax.axis_index("fsdp")
     clips, length = lse_ref.shape[0], lse_ref.shape[2]
     local = length // ctx
     heads = b_ref.shape[2] // HD
-    greet("ctx")
+    odd = lax.rem(me, 2)
+    span = w_ref.shape[1]
+    part = span // 2
+    pieces = (w_ref, up_ref, down_t, proj_t)
+    wholes = (w_full, up_full, down_full, proj_full)
+    kept = (w_out, up_out, down_out, proj_out)
+    greet("fsdp", "ctx")
+
+    def band(ref, start, size):
+        return ref.at[:, aligned(start, size)] if len(ref.shape) == 3 else ref.at[aligned(start, size)]
+
+    def fetch(k, step):
+        return remote(
+            band(pieces[k], odd * part, part),
+            band(wholes[k], f * span + odd * part, part),
+            fetch_out.at[k, step],
+            fetch_in.at[k, step],
+            "fsdp",
+            lax.rem(f + step, fsdp),
+        )
+
+    def hand(k, step):
+        rows = lax.rem(f + fsdp - step, fsdp) * span + odd * part
+        return remote(
+            band(wholes[k], rows, part),
+            band(wholes[k], rows, part),
+            pass_out.at[k, step],
+            pass_in.at[k, step],
+            "ctx",
+            me + 1 - 2 * odd,
+        )
+
+    def keep(k):
+        return pltpu.make_async_copy(wholes[k], kept[k], keep_sem.at[k])
+
+    def pass_on(k):
+        for step in range(1, fsdp):
+            fetch(k, step).wait_recv()
+            hand(k, step).start()
+
+    for step in range(1, fsdp):
+        fetch(0, step).start()
+    for c in range(3):
+        w_full[c, aligned(f * span, span), :] = w_ref[c]
+    down_t[...] = down_ref[...].T
+    proj_t[...] = proj_ref[...].T
+    for k in (1, 2, 3):
+        for step in range(1, fsdp):
+            fetch(k, step).start()
+
+    @pl.loop(0, clips * local // ROWS)
+    def _(block):
+        rows = aligned(block * ROWS, ROWS)
+        hat, _ = norm_parts(x_ref[rows, :].astype(F32))
+        n1_ref[rows, :] = (hat * gain_ref[0:1, :] + shift_ref[0:1, :]).astype(BF16)
 
     def outgoing(clip, step):
         peer = lax.rem(me + step, ctx)
@@ -181,20 +380,23 @@
             peer,
         )
 
+    pass_on(0)
+    for step in range(1, fsdp):
+        hand(0, step).wait_recv()
+    keep(0).start()
+
     for clip in range(clips):
 
         @pl.loop(0, local // ROWS)
         def _(block):
             rows = aligned(clip * local + block * ROWS, ROWS)
             lanes = aligned(block * ROWS, ROWS)
-            hat, _ = norm_parts(x_ref[rows, :].astype(F32))
-            normed = (hat * gain_ref[0:1, :] + shift_ref[0:1, :]).astype(BF16)
-            n1_ref[rows, :] = normed
+            normed = n1_ref[rows, :]
             cos_t = jnp.concatenate([cos_ref[:, rows]] * heads, axis=0)
             low_t = jnp.concatenate([low_ref[:, rows]] * heads, axis=0)
             high_t = jnp.concatenate([high_ref[:, rows]] * heads, axis=0)
             for c in range(3):
-                moved = (mm(normed, w_ref[c], 1, 0) + b_ref[c]).T
+                moved = (mm(normed, w_full[c], 1, 0) + b_ref[c]).T
                 if c < 2:
                     moved = turn(moved, cos_t, low_t, high_t, 1)
                 moved = moved.astype(BF16)
@@ -207,6 +409,11 @@
         mine = aligned(me * local, local)
         for c in range(3):
             qkv[clip, c, :, mine] = send_buf[clip, c, aligned(me * HD, HD), :]
+
+    own = aligned(f * span, span)
+    up_full[own, :] = up_ref[...]
+    down_full[own, :] = down_t[...]
+    proj_full[own, :] = proj_t[...]
 
     for clip in range(clips):
         for step in range(1, ctx):
@@ -229,6 +436,13 @@
         for step in range(1, ctx):
             returning(clip, step).start()
         att[clip, aligned(me * HD, HD), :] = back_buf[clip, :, aligned(me * local, local)]
+        if clip == 0:
+            for k in (1, 2, 3):
+                pass_on(k)
+    for k in (1, 2, 3):
+        for step in range(1, fsdp):
+            hand(k, step).wait_recv()
+        keep(k).start()
 
     for clip in range(clips):
         for step in range(1, ctx):
@@ -238,31 +452,38 @@
         for step in range(1, ctx):
             outgoing(clip, step).wait_send()
             returning(clip, step).wait_send()
+    for k in range(4):
+        keep(k).wait()
+        for step in range(1, fsdp):
+            fetch(k, step).wait_send()
+            hand(k, step).wait_send()
 
 
 def middle_kernel(
     count,
     att_ref, x_ref, g_ref, proj_ref, up_ref, down_ref, bup_ref, gain_ref, shift_ref, outs_ref,
-    n2_ref, act_ref, dz_ref, mlp_ref, sum_out, dr_ref, drb_ref, grad_out_ref, stats_ref,
-    part_a, land_a, full_a, part_b, land_b, full_b, send_buf, grad_land, sem_a, sem_b, out_sem, in_sem,
+    mlp_ref, sum_out, dr_ref, grads_ref, grad_out_ref, stats_ref,
+    n2_ref, act_ref, dz_ref, drb_ref, att_rows, part_a, land_a, full_a, part_b, land_b, full_b, send_buf, grad_land, sem_a, sem_b, out_sem, in_sem,
 ):
     n = lax.axis_size("tp")
     ctx, me = lax.axis_size("ctx"), lax.axis_index("ctx")
     clips, local = att_ref.shape[0], att_ref.shape[2]
-    rows_all = x_ref.shape[0]
+    rows_all, width = x_ref.shape
+    hidden = act_ref.shape[1]
     half = rows_all // 2
     size = half // count
     hops = 2 * (n - 1)
+    per = 2
     greet("tp", "ctx")
     stats_ref[...] = jnp.zeros_like(stats_ref)
 
     for clip in range(clips):
-        att = att_ref[clip].T
-
-        for block in range(local // ROWS):
-            part_a[pl.ds(clip * local + block * ROWS, ROWS), :] = mm(
-                att[block * ROWS : (block + 1) * ROWS], proj_ref[...], 1, 0
-            ).astype(BF16)
+        att_rows[clip * local : (clip + 1) * local, :] = att_ref[clip].T
+
+    @pl.loop(0, rows_all // ROWS)
+    def _(block):
+        rows = aligned(block * ROWS, ROWS)
+        part_a[rows, :] = mm(att_rows[rows, :], proj_ref[...], 1, 1).astype(BF16)
 
     def both(ref, first, second):
         return jnp.concatenate([ref[first, :], ref[second, :]], axis=0)
@@ -298,11 +519,22 @@
             act = (pre * cdf).astype(BF16)
             put(act_ref, first, second, act)
             slope = cdf + pre * (jnp.exp(-0.5 * pre * pre) * 0.3989422804014327)
-            grad = (mm(both(g_ref, first, second), down_ref[...], 1, 1) * slope).astype(BF16)
+            grad = (mm(both(g_ref, first, second), down_ref[...], 1, 0) * slope).astype(BF16)
             put(dz_ref, first, second, grad)
             put(part_b, first, second, mm(grad, up_ref[...], 1, 1))
-            put(mlp_ref, first, second, mm(act, down_ref[...], 1, 0))
-            stats_ref[4:5, :] += jnp.sum(grad.astype(F32), axis=0, keepdims=True)
+            put(mlp_ref, first, second, mm(act, down_ref[...], 1, 1))
+            stats_ref[6:7, :] += jnp.sum(grad.astype(F32), axis=0, keepdims=True)
+
+        unit = step - hops - count
+
+        @pl.when((unit >= 0) & (unit * per < width // ROWS))
+        def _():
+            @pl.loop(0, per)
+            def _(more):
+                at = unit * per + more
+                lanes = aligned(at * ROWS, ROWS)
+                put_pieces(grads_ref, at, pl.ds(0, hidden), mm(n2_ref[:, lanes], dz_ref[...], 0, 0))
+                put_pieces(grads_ref, at, pl.ds(hidden, hidden), mm(g_ref[:, lanes], act_ref[...], 0, 0))
 
         k = step - 2 * hops - 1
 
@@ -315,10 +547,10 @@
             moved = upstream + norm_pull(hat, rstd, gain_ref[1:2, :], grad)
             put(dr_ref, first, second, moved)
             put(drb_ref, first, second, moved)
-            stats_ref[0:1, :] += jnp.sum(grad * hat, axis=0, keepdims=True)
-            stats_ref[1:2, :] += jnp.sum(grad, axis=0, keepdims=True)
-            stats_ref[2:3, :] += jnp.sum(moved, axis=0, keepdims=True)
-            stats_ref[3:4, :] += jnp.sum(upstream, axis=0, keepdims=True)
+            stats_ref[2:3, :] += jnp.sum(grad * hat, axis=0, keepdims=True)
+            stats_ref[3:4, :] += jnp.sum(grad, axis=0, keepdims=True)
+            stats_ref[4:5, :] += jnp.sum(moved, axis=0, keepdims=True)
+            stats_ref[5:6, :] += jnp.sum(upstream, axis=0, keepdims=True)
 
     def outgoing(clip, step):
         peer = lax.rem(me + step, ctx)
@@ -335,13 +567,17 @@
 
         @pl.loop(0, local // ROWS)
         def _(block):
-            send_buf[clip, :, aligned(block * ROWS, ROWS)] = mm(
-                proj_ref[...], drb_ref[aligned(clip * local + block * ROWS, ROWS), :], 1, 1
-            ).astype(BF16)
+            value = mm(drb_ref[aligned(clip * local + block * ROWS, ROWS), :], proj_ref[...], 1, 0)
+            send_buf[clip, :, aligned(block * ROWS, ROWS)] = value.T.astype(BF16)
 
         for step in range(1, ctx):
             outgoing(clip, step).start()
         grad_land[clip, :, aligned(me * local, local)] = send_buf[clip, aligned(me * HD, HD), :]
+
+    @pl.loop(0, width // ROWS)
+    def _(unit):
+        value = mm(drb_ref[:, aligned(unit * ROWS, ROWS)], att_rows[...], 0, 0)
+        put_pieces(grads_ref, unit, pl.ds(2 * hidden, att_rows.shape[1]), value)
 
     chain_drain(count, size, half, part_a, land_a, full_a, sem_a)
     chain_drain(count, size, half, part_b, land_b, full_b, sem_b)
@@ -354,9 +590,9 @@
 
 def backward_kernel(
     count,
-    qkv_ref, own_ref, lse_ref, grad_ref, mlp_ref, x_ref, sum_ref, outs_ref, cos_ref, low_ref, high_ref,
-    block_ref, dp_ref, bias_ref,
-    part, landed, full, query, keys, vals, grads, acc_k, acc_v, send_buf, moved, sem, out_sem, in_sem,
+    qkv_ref, own_ref, lse_ref, grad_ref, mlp_ref, x_ref, sum_ref, outs_ref, cos_ref, low_ref, high_ref, weights_ref,
+    block_ref, dp_ref, bias_ref, up_ref, down_ref, proj_ref,
+    part, landed, full, query, keys, vals, grads, acc_k, acc_v, send_buf, moved, sem, out_sem, in_sem, *sum_refs,
 ):
     n = lax.axis_size("tp")
     ctx, me = lax.axis_size("ctx"), lax.axis_index("ctx")
@@ -367,7 +603,9 @@
     size = half // count
     hops = 2 * (n - 1)
     blocks = length // QB
-    greet("tp", "ctx")
+    weights = GradientSum(weights_ref, *sum_refs)
+    greet_grid("tp")
+    weights.start_pair()
     part[...] = mlp_ref[...]
 
     def outgoing(clip, step):
@@ -407,6 +645,12 @@
             at = clip * blocks + block
             chain_step(at, count, size, half, part, landed, full, sem)
             finish(at - hops)
+            for place, act in ((1, weights.sum_pair), (2, weights.start_cross)):
+                if clip == 0:
+                    pl.when(block == place)(act)
+            for place, act in ((1, weights.sum_cross), (2, weights.start_share)):
+                if clip == 1:
+                    pl.when(block == place)(act)
             lanes = aligned(block * QB, QB)
             grad_t = grad_ref[clip, :, lanes]
             scores = mm(keys[...], qkv_ref[clip, 0, :, lanes], 1, 0)
@@ -449,22 +693,41 @@
                 dp_ref[c, rows, :] = value
                 bias_ref[c : c + 1, :] += jnp.sum(value.astype(F32), axis=0, keepdims=True)
 
+    weights.wait_share()
+    hidden = up_ref.shape[1]
+    rows = weights_ref.shape[2]
+    for c in range(ctx):
+        at = pl.ds(c * rows, rows)
+        up_ref[at, :] = weights.shared[c, :, 0:hidden].astype(F32)
+        down_ref[at, :] = weights.shared[c, :, hidden : 2 * hidden].astype(F32)
+        proj_ref[at, :] = weights.shared[c, :, 2 * hidden :].astype(F32)
     chain_drain(count, size, half, part, landed, full, sem)
+    weights.drain()
     for clip in range(clips):
         for step in range(1, ctx):
             outgoing(clip, step).wait_send()
 
 
 def last_kernel(
-    count, dp_ref, w_ref, x_ref, dr_ref, gain_ref, grad_in_ref, stats_ref, part, landed, full, sem
+    count, dp_ref, w_ref, x_ref, n1_ref, dr_ref, gain_ref, stats_ref, bias_ref,
+    grad_in_ref, w_out, bqkv_ref, bup_ref, gains_ref, shifts_ref, outs_ref,
+    part, landed, full, sem, grads, small, small_land, small_sem, *sum_refs,
 ):
     n = lax.axis_size("tp")
-    rows_all = x_ref.shape[0]
+    rows_all, width = x_ref.shape
+    lane = dp_ref.shape[2]
     half = rows_all // 2
     size = half // count
     hops = 2 * (n - 1)
-    greet("tp")
-    stats_ref[...] = jnp.zeros_like(stats_ref)
+    units = width // ROWS
+    ctx = lax.axis_size("ctx")
+    pieces = lax.axis_size("fsdp") * ctx
+    me = lax.axis_index("fsdp") * ctx + lax.axis_index("ctx")
+    weights = GradientSum(grads, *sum_refs)
+    greet_grid("tp")
+    small[...] = stats_ref[...]
+    for c in range(3):
+        small[7:8, c * lane : (c + 1) * lane] = bias_ref[c : c + 1, :]
 
     @pl.loop(0, rows_all // ROWS)
     def _(block):
@@ -477,6 +740,24 @@
     @pl.loop(0, count + hops)
     def _(step):
         chain_step(step, count, size, half, part, landed, full, sem)
+
+        @pl.when(step < 4)
+        def _():
+            @pl.loop(0, units // 4)
+            def _(more):
+                unit = step * (units // 4) + more
+                normed = n1_ref[:, aligned(unit * ROWS, ROWS)]
+                for c in range(3):
+                    put_pieces(grads, unit, pl.ds(c * lane, lane), mm(normed, dp_ref[c], 0, 0))
+
+        for place, act in (
+            (4, weights.start_pair),
+            (5, weights.sum_pair),
+            (6, weights.start_cross),
+            (9, weights.sum_cross),
+            (10, weights.start_share),
+        ):
+            pl.when(step == place)(act)
         i = step - hops
 
         @pl.when(i >= 0)
@@ -486,16 +767,47 @@
                 hat, rstd = norm_parts(x_ref[rows, :].astype(F32))
                 grad = full[rows, :].astype(F32)
                 grad_in_ref[rows, :] = dr_ref[rows, :] + norm_pull(hat, rstd, gain_ref[0:1, :], grad)
-                stats_ref[0:1, :] += jnp.sum(grad * hat, axis=0, keepdims=True)
-                stats_ref[1:2, :] += jnp.sum(grad, axis=0, keepdims=True)
-
+                small[0:1, :] += jnp.sum(grad * hat, axis=0, keepdims=True)
+                small[1:2, :] += jnp.sum(grad, axis=0, keepdims=True)
+
+    def spread(step):
+        to = lax.rem(me + step, pieces)
+        return remote_at(
+            small, small_land.at[me], small_sem.at[0, step], small_sem.at[1, step], spot(to)
+        )
+
+    @pl.loop(1, pieces)
+    def _(step):
+        spread(step).start()
+
+    small_land[me] = small[...]
+    weights.wait_share()
+    rows = grads.shape[2]
+    for c in range(3):
+        for i in range(ctx):
+            w_out[c, i * rows : (i + 1) * rows, :] = weights.shared[i, :, c * lane : (c + 1) * lane].astype(F32)
     chain_drain(count, size, half, part, landed, full, sem)
-
-
-def contract_rows(left_mat, right_mat):
-    return lax.dot_general(
-        left_mat, right_mat, (((0,), (0,)), ((), ())), preferred_element_type=jnp.float32
-    )
+    weights.drain()
+
+    @pl.loop(1, pieces)
+    def _(step):
+        spread(step).wait_recv()
+
+    total = small_land[0]
+    for i in range(1, pieces):
+        total = total + small_land[i]
+    gains_ref[0:1, :] = total[0:1]
+    gains_ref[1:2, :] = total[2:3]
+    shifts_ref[0:1, :] = total[1:2]
+    shifts_ref[1:2, :] = total[3:4]
+    outs_ref[...] = total[4:6]
+    bup_ref[...] = total[6:7]
+    for c in range(3):
+        bqkv_ref[c : c + 1, :] = total[7:8, c * lane : (c + 1) * lane]
+
+    @pl.loop(1, pieces)
+    def _(step):
+        spread(step).wait_send()
 
 
 def rotary_tables(positions):
@@ -515,16 +827,17 @@
 
 
 VMEM = pl.BlockSpec(memory_space=pltpu.VMEM)
-
-
-def call(kernel, name, number, ins, outs, scratch, flops):
+ANY = pl.BlockSpec(memory_space=pl.ANY)
+
+
+def call(kernel, name, number, ins, outs, scratch, flops, kept=0):
     moved = sum(a.size * a.dtype.itemsize for a in (*ins, *outs))
     return pl.pallas_call(
         kernel,
         name=name,
         out_shape=outs,
         in_specs=[VMEM] * len(ins),
-        out_specs=[VMEM] * len(outs),
+        out_specs=[VMEM] * (len(outs) - kept) + [ANY] * kept,
         scratch_shapes=scratch,
         cost_estimate=pl.CostEstimate(flops=flops, bytes_accessed=moved, transcendentals=0),
         compiler_params=pltpu.CompilerParams(
@@ -544,137 +857,155 @@
     hidden = w_up.shape[1]
     length = local * ctx
     assert lane == ctx * HD and clips == 2 and hidden == width
-    count = max(1, rows // 2 // 64)
+    assert width == w_down.shape[0]
+    fsdp = lax.axis_size("fsdp")
+    pieces = fsdp * ctx
+    span = width // fsdp
+    piece = span // ctx
+    count = max(1, rows // 2 // CHUNK)
     dma = pltpu.SemaphoreType.DMA
     shape = jax.ShapeDtypeStruct
-
-    full_qkv = lax.all_gather(w_qkv, "fsdp", axis=1, tiled=True)
-    full_proj = lax.all_gather(w_proj, "fsdp", axis=1, tiled=True)
-    full_up = lax.all_gather(w_up, "fsdp", axis=0, tiled=True)
-    full_down = lax.all_gather(w_down, "fsdp", axis=1, tiled=True)
+    vmem = pltpu.VMEM
 
     x = block_input.reshape(rows, width)
     g = grad_out.reshape(rows, width)
     tables = rotary_tables(positions.reshape(3, rows))
-
-    n1, qkv, own, lse, att = call(
+    wide = shape((rows, width), BF16)
+    wide32 = shape((rows, width), F32)
+    square = shape((width, hidden), BF16)
+
+    n1, qkv, own, lse, att, full_qkv, full_up, full_down, full_proj = call(
         forward_kernel,
         "forward",
         0,
-        (x, full_qkv, b_qkv.reshape(3, 1, lane), *tables, norm_gains, norm_shifts),
+        (x, w_qkv, w_up, w_down, w_proj, b_qkv.reshape(3, 1, lane), *tables, norm_gains, norm_shifts),
         (
-            shape((rows, width), BF16),
+            wide,
             shape((clips, 3, HD, length), BF16),
             shape((clips, HD, length), F32),
             shape((clips, 1, length), F32),
             shape((clips, lane, local), BF16),
+            shape((3, width, lane), BF16),
+            square,
+            square,
+            shape((width, lane), BF16),
         ),
         [
-            pltpu.VMEM((clips, 3, lane, local), BF16),
-            pltpu.VMEM((clips, 3, HD, length), BF16),
-            pltpu.VMEM((length, HD), BF16),
-            pltpu.VMEM((clips, HD, length), BF16),
-            pltpu.VMEM((clips, lane, local), BF16),
-            dma((clips, ctx)),
-            dma((clips, ctx)),
-            dma((clips, ctx)),
-            dma((clips, ctx)),
-        ],
+            vmem((clips, 3, lane, local), BF16),
+            vmem((clips, 3, HD, length), BF16),
+            vmem((length, HD), BF16),
+            vmem((clips, HD, length), BF16),
+            vmem((clips, lane, local), BF16),
+            vmem((3, width, lane), BF16),
+            vmem((width, hidden), BF16),
+            vmem((width, hidden), BF16),
+            vmem((width, lane), BF16),
+            vmem((span, hidden), BF16),
+            vmem((span, lane), BF16),
+        ]
+        + [dma((clips, ctx))] * 4
+        + [dma((4, fsdp))] * 4
+        + [dma((4,))],
         2 * rows * width * 3 * lane + 4 * clips * length * length * HD,
+        kept=4,
     )
 
-    wide = shape((rows, width), BF16)
-    wide32 = shape((rows, width), F32)
-    chain = [pltpu.VMEM((rows, width), BF16)] * 3
-    n2, act, dz, mlp, summed, dr, drb, grad_att, stats_two = call(
+    chain = [vmem((rows, width), BF16)] * 3
+    lanes = 2 * hidden + lane
+    mlp, summed, dr, grads, grad_att, stats = call(
         functools.partial(middle_kernel, count),
         "middle",
         1,
         (att, x, g, full_proj, full_up, full_down, b_up.reshape(1, hidden), norm_gains, norm_shifts, out_shifts),
         (
-            wide, wide, wide, wide, wide, wide32, wide,
+            wide,
+            wide,
+            wide32,
+            shape((pieces // 2, 2, piece, lanes), BF16),
             shape((clips, HD, length), BF16),
             shape((8, width), F32),
         ),
-        chain
+        [
+            vmem((rows, width), BF16),
+            vmem((rows, hidden), BF16),
+            vmem((rows, hidden), BF16),
+            vmem((rows, width), BF16),
+            vmem((rows, lane), BF16),
+        ]
+        + chain
         + chain
         + [
-            pltpu.VMEM((clips, lane, local), BF16),
-            pltpu.VMEM((clips, HD, length), BF16),
+            vmem((clips, lane, local), BF16),
+            vmem((clips, HD, length), BF16),
             dma((8, count)),
             dma((8, count)),
             dma((clips, ctx)),
             dma((clips, ctx)),
         ],
-        8 * rows * width * hidden,
+        12 * rows * width * hidden,
     )
-    grad_down = contract_rows(act, g)
-    grad_up = contract_rows(n2, dz)
-    grad_proj = mm(att.transpose(1, 0, 2).reshape(lane, rows), drb, 1, 0)
-
-    block_output, dp, bias = call(
+
+    block_output, dp, bias, shard_up, shard_down, shard_proj = call(
         functools.partial(backward_kernel, count),
         "backward",
         2,
-        (qkv, own, lse, grad_att, mlp, x, summed, out_shifts, *tables),
-        (wide, shape((3, rows, lane), BF16), shape((8, lane), F32)),
+        (qkv, own, lse, grad_att, mlp, x, summed, out_shifts, *tables, grads),
+        (
+            wide,
+            shape((3, rows, lane), BF16),
+            shape((8, lane), F32),
+            shape((span, hidden), F32),
+            shape((span, hidden), F32),
+            shape((span, lane), F32),
+        ),
         chain
+        + [vmem((length, HD), BF16)] * 4
+        + [vmem((length, HD), F32)] * 2
         + [
-            pltpu.VMEM((length, HD), BF16),
-            pltpu.VMEM((length, HD), BF16),
-            pltpu.VMEM((length, HD), BF16),
-            pltpu.VMEM((length, HD), BF16),
-            pltpu.VMEM((length, HD), F32),
-            pltpu.VMEM((length, HD), F32),
-            pltpu.VMEM((clips, 3, HD, length), BF16),
-            pltpu.VMEM((clips, 3, lane, local), BF16),
+            vmem((clips, 3, HD, length), BF16),
+            vmem((clips, 3, lane, local), BF16),
             dma((8, count)),
             dma((clips, ctx)),
             dma((clips, ctx)),
-        ],
+        ]
+        + gradient_scratch(pieces, ctx, piece, lanes),
         10 * clips * length * length * HD,
     )
-    grad_qkv = jnp.einsum("rd,cre->cde", n1, dp, preferred_element_type=F32)
-
-    grad_input, stats_one = call(
+
+    grad_input, shard_qkv, bqkv, bup, gains, shifts, outs = call(
         functools.partial(last_kernel, count),
         "last",
         3,
-        (dp, full_qkv, x, dr, norm_gains),
-        (wide32, shape((8, width), F32)),
-        chain + [dma((8, count))],
-        2 * rows * width * 3 * lane,
-    )
-
-    def scatter(grad, axis):
-        return lax.psum_scatter(grad.astype(BF16), "fsdp", scatter_dimension=axis, tiled=True)
-
-    def total(part):
-        return lax.psum(part, "ctx").astype(F32)
-
-    shard_down = total(scatter(grad_down, 1))
-    shard_up = total(scatter(grad_up, 0))
-    shard_proj = total(scatter(grad_proj, 1))
-    shard_qkv = total(scatter(grad_qkv, 1))
-    gains, shifts, outs, bqkv, bup = lax.psum(
+        (dp, full_qkv, x, n1, dr, norm_gains, stats, bias),
         (
-            jnp.stack([stats_one[0], stats_two[0]]),
-            jnp.stack([stats_one[1], stats_two[1]]),
-            stats_two[2:4],
-            bias[:3],
-            stats_two[4],
+            wide32,
+            shape((3, span, lane), F32),
+            shape((3, lane), F32),
+            shape((1, hidden), F32),
+            shape((2, width), F32),
+            shape((2, width), F32),
+            shape((2, width), F32),
         ),
-        ("fsdp", "ctx"),
+        chain
+        + [
+            dma((8, count)),
+            vmem((pieces // 2, 2, piece, 3 * lane), BF16),
+            vmem((8, width), F32),
+            vmem((pieces, 8, width), F32),
+            dma((2, pieces)),
+        ]
+        + gradient_scratch(pieces, ctx, piece, 3 * lane),
+        4 * rows * width * 3 * lane,
     )
     return (
         block_output.reshape(clips, local, width),
         grad_input.reshape(clips, local, width),
         shard_qkv,
         bqkv,
-        shard_proj,
+        shard_proj.T,
         shard_up,
-        bup,
-        shard_down,
+        bup.reshape(hidden),
+        shard_down.T,
         gains,
         shifts,
         outs,

time: 557 us -> 398 us (0.71)
  waiting for transfers between devices: 124 us -> 0 us
  blocking collectives: 35.6 us -> 0 us
  Pallas kernels: 344 us -> 376 us
  matrix products: 18.7 us -> 0 us
  between operations: 14.4 us -> 0.76 us
  local copies, waits for them, and re-layouts: 13 us -> 19 us
    reduce_scatter x4 -> x0, waiting for transfers between devices: 80.9 us -> none  [scatter(): lax.psum_scatter(grad.astype(BF16), 'fsdp', scatter_dimension=axis, tiled...]
    all_gather x3 -> x0, waiting for transfers between devices: 40.7 us -> none  [the longest x1 26.2 us: shards(): full_down = lax.all_gather(w_down, 'fsdp', axis=1, tiled=True)]
    pallas_call x4, Pallas kernels: 344 us -> 376 us  [call(): pl.pallas_call(kernel, name=name, out_shape=outs, in_specs=[VMEM] * len(i...]
    psum x1 -> x0, blocking collectives: 23 us -> none  [shards(): lax.psum((jnp.stack([stats_one[0], stats_two[0]]), jnp.stack([stats_one[1...]
    dot_general x4 -> x0, matrix products: 18.7 us -> none  [the longest x2 11.2 us: contract_rows(): lax.dot_general(left_mat, right_mat, (((0,), (0,)), ((), ())), preferred_...]
    all_gather x1 -> x0, blocking collectives: 12.6 us -> none  [shards(): full_proj = lax.all_gather(w_proj, 'fsdp', axis=1, tiled=True)]
    unnamed x28 -> x32, local copies, waits for them, and re-layouts: 7.94 us -> 15.4 us
  transfers between devices with their start and end apart: 8 -> 0, of which waited for: 5 -> 0; matrix products, arithmetic and copies ran while one was open for 4% -> 0% of each run, Pallas kernels for 38% -> 0%
where the time goes in v2:
time: 398 us; the launch traced here: 397 us
  Pallas kernels  376 us (94%)
  local copies, waits for them, and re-layouts  19 us (5%)
    pallas_call x4, Pallas kernels, call(): pl.pallas_call(kernel, name=name, out_shape=outs, in_specs=[VMEM] * len(i...  376 us
    unnamed x32, local copies, waits for them, and re-layouts  15.4 us

profile of v2, /device:TPU:0, one launch (start us, length us, event | category | flops | bytes accessed | tf_op | source)
XLA Modules:
  0.0 397.4 jit_solution(16148988865475453101)
XLA Ops:
  0.7 1.3 reshape.65.b_ref
  1.9 0.7 convert_bitcast_fusion
  2.6 0.8 multiply_sine_fusion
  3.5 0.7 concatenate.23.high_ref
  4.3 0.7 concatenate.21.low_ref
  5.1 0.7 concatenate.19.cos_ref
  5.8 58.6 %forward.1 = (bf16[1024,1024]{1,0:T(8,128)(2,1)}, bf16[2,3,64,2048]{3,2,1,0:T(8,128)(2,1)}, f32[2,64,2048]{2,1,0:T(8,128)}, f32[2,1,2048]{2,1,0:T(1,128)}, bf16[...) custom-call(bf16[1024,1024]{1,0:T(8,128)(2,1)} %bitcast.18, ...), custom_call_target="tpu_custom_call" | custom-call | flops 3758096384 | bytes 17599488 | tf_op jit(solution)/shard_map/forward/pallas_call | solution.py:835
  64.4 134.9 %middle.1 = (bf16[1024,1024]{1,0:T(8,128)(2,1)}, bf16[1024,1024]{1,0:T(8,128)(2,1)}, f32[1024,1024]{1,0:T(8,128)}, bf16[4,2,128,2304]{3,2,1,0:T(8,128)(2,1)}, bf...) custom-call(bf16[2,256,512]{2,1,0:T(8,128)(2,1)} %get-tuple-element.42.att_ref, bf16[1024,1024]{1,0:T(8,128)(2,1)} %bitcast.19, ...), custom_call_target="tpu_custom_call" | custom-call | flops 12884901888 | bytes 23130112 | tf_op jit(solution)/shard_map/middle/pallas_call | solution.py:835
  199.3 96.8 %backward.1 = (bf16[1024,1024]{1,0:T(8,128)(2,1)}, bf16[3,1024,256]{2,1,0:T(8,128)(2,1)}, f32[8,256]{1,0:T(8,128)}, f32[512,1024]{1,0:T(8,128)}, f32[512,1024]{1,0:T(8,128)}, /*index=5*/f32[512,256]{1,0:T(8,128)}) custom-call(bf16[2,3,64,2048]{3,2,1,0:T(8,128)(2,1)} %get-tuple-element.39.qkv_ref, f32[2,64,2048]{2,1,0:T(8,128)} %get-tuple-element.40.own_ref, ...), custom_call_target="tpu_custom_call" | custom-call | flops 5368709120 | bytes 23363584 | tf_op jit(solution)/shard_map/backward/pallas_call | solution.py:835
  296.1 0.0 copy-start.4
  296.1 85.9 %last.1 = (f32[1024,1024]{1,0:T(8,128)}, f32[3,512,256]{2,1,0:T(8,128)}, f32[3,256]{1,0:T(4,128)}, f32[1,1024]{1,0:T(1,128)}, f32[2,1024]{1,0:T(2,128)}, /*index=5*/f32[2,1024]{1,0:T(2,128)}, f32[2,1024]{1,0:T(2,128)}) custom-call(bf16[3,1024,256]{2,1,0:T(8,128)(2,1)} %get-tuple-element.51.dp_ref, bf16[3,1024,256]{2,1,0:T(8,128)(2,1)} %get-tuple-element.52.w_ref, ...), custom_call_target="tpu_custom_call" | custom-call | flops 3221225472 | bytes 17382400 | tf_op jit(solution)/shard_map/last/pallas_call | solution.py:835
  382.0 0.0 copy-done.4
  382.0 1.0 copy.23
  383.0 0.0 copy-start.2
  383.0 3.0 copy.24
  386.0 0.0 copy-done.2
  386.0 0.0 copy-start
  386.0 1.3 copy.35
  387.3 1.6 copy-done
  389.0 0.0 copy-start.3
  389.0 2.0 copy.36
  391.0 0.5 copy-done.3
  391.5 0.0 copy-start.9
  391.5 0.0 copy-start.1
  391.5 1.1 copy.37
  392.6 0.0 copy-done.9
  392.7 0.6 copy.38
  393.2 0.4 copy-done.1
  393.7 0.0 copy-start.8
  393.7 0.0 copy-start.7
  393.7 0.0 copy-start.6
  393.7 0.0 copy-start.5
  393.7 1.3 copy.39
  395.0 0.0 copy-done.8
  395.0 0.6 copy.40
  395.6 0.0 copy-done.7
  395.6 0.6 copy.41
  396.2 0.0 copy-done.6
  396.2 0.6 copy.42
  396.8 0.0 copy-done.5
  396.8 0.6 copy.43
  (8 shorter events, 0.2 us)
Async XLA Ops:
  296.1 85.9 %copy-start.4 = (f32[512,256]{1,0:T(8,128)S(1)}, f32[512,256]{1,0:T(8,128)}, u32[]{:S(2)}) copy-start(f32[512,256]{1,0:T(8,128)} %get-tuple-element.60) | copy-start | bytes 1572868
  383.0 3.0 copy-start.2
  386.0 2.9 copy-start
  389.0 2.5 copy-start.3
  391.5 1.1 copy-start.9
  391.5 2.2 copy-start.1
  393.7 1.3 copy-start.8
  393.7 1.9 copy-start.7
  393.7 2.5 copy-start.6
  393.7 3.1 copy-start.5

commit v3 on v2

v3 whole, which is shorter than its diff:
```python
import functools

import jax
import jax.numpy as jnp
from jax import lax
from jax.experimental import pallas as pl
from jax.experimental.pallas import tpu as pltpu
from jax.sharding import PartitionSpec as P

HD = 64
ROT = 20
EPSILON = 1e-06
SCALE = HD ** (-0.5)
QB = 256
CHUNK = 32
ROWS = 128
MESH = pl.DeviceIdType.MESH
F32, BF16 = jnp.float32, jnp.bfloat16


def mm(left, right, left_dim, right_dim):
    return lax.dot_general(
        left, right, (((left_dim,), (right_dim,)), ((), ())), preferred_element_type=F32
    )


def remote(src, dst, send_sem, recv_sem, axis, peer):
    return remote_at(src, dst, send_sem, recv_sem, {axis: peer})


def remote_at(src, dst, send_sem, recv_sem, device):
    return pltpu.make_async_remote_copy(
        src_ref=src,
        dst_ref=dst,
        send_sem=send_sem,
        recv_sem=recv_sem,
        device_id=device,
        device_id_type=MESH,
    )


def greet(*axes):
    barrier = pltpu.get_barrier_semaphore()
    total = 0
    for axis in axes:
        size, me = lax.axis_size(axis), lax.axis_index(axis)
        for step in range(1, size):
            pl.semaphore_signal(
                barrier, inc=1, device_id={axis: lax.rem(me + step, size)}, device_id_type=MESH
            )
            total += 1
    pl.semaphore_wait(barrier, total)


def spot(index):
    ctx = lax.axis_size("ctx")
    return {"fsdp": index // ctx, "ctx": lax.rem(index, ctx)}


def greet_grid(*axes):
    barrier = pltpu.get_barrier_semaphore()
    ctx = lax.axis_size("ctx")
    size = lax.axis_size("fsdp") * ctx
    me = lax.axis_index("fsdp") * ctx + lax.axis_index("ctx")

    @pl.loop(1, size)
    def _(step):
        pl.semaphore_signal(
            barrier, inc=1, device_id=spot(lax.rem(me + step, size)), device_id_type=MESH
        )

    total = size - 1
    for axis in axes:
        count, own = lax.axis_size(axis), lax.axis_index(axis)
        for step in range(1, count):
            pl.semaphore_signal(
                barrier, inc=1, device_id={axis: lax.rem(own + step, count)}, device_id_type=MESH
            )
            total += 1
    pl.semaphore_wait(barrier, total)


def aligned(start, size):
    return pl.ds(pl.multiple_of(start, size), size)


def norm_parts(values):
    center = values - jnp.mean(values, axis=-1, keepdims=True)
    rstd = lax.rsqrt(jnp.mean(center * center, axis=-1, keepdims=True) + EPSILON)
    return center * rstd, rstd


def norm_pull(hat, rstd, gain, grad):
    scaled = grad * gain
    return rstd * (
        scaled
        - jnp.mean(scaled, axis=-1, keepdims=True)
        - hat * jnp.mean(scaled * hat, axis=-1, keepdims=True)
    )


def turn(values, cos_t, low_t, high_t, sign):
    half = ROT // 2
    up = jnp.concatenate([values[half:], values[:half]], axis=0)
    down = jnp.concatenate([values[-half:], values[:-half]], axis=0)
    if sign > 0:
        return values * cos_t + (up * low_t + down * high_t)
    return values * cos_t - (up * low_t + down * high_t)


def chain_rows(way, i):
    many = ROWS // 2 // CHUNK
    return aligned((i // many) * ROWS + way * (ROWS // 2) + lax.rem(i, many) * CHUNK, CHUNK)


class Chain:
    def __init__(self, part, landed, full, sems):
        self.part, self.landed, self.full, self.sems = part, landed, full, sems
        self.n, self.j = lax.axis_size("tp"), lax.axis_index("tp")
        self.count = part.shape[0] // 2 // CHUNK
        self.hops = 2 * (self.n - 1)

    def pos(self, way):
        return (self.n - 1 - self.j) if way == 0 else self.j

    def sums(self, way, i):
        rows = chain_rows(way, i)
        return remote(
            self.part.at[rows], self.landed.at[rows],
            self.sems.at[4 * way, i], self.sems.at[4 * way + 1, i],
            "tp", self.j - 1 if way == 0 else self.j + 1,
        )

    def totals(self, way, i):
        rows = chain_rows(way, i)
        return remote(
            self.full.at[rows], self.full.at[rows],
            self.sems.at[4 * way + 2, i], self.sems.at[4 * way + 3, i],
            "tp", self.j + 1 if way == 0 else self.j - 1,
        )

    def added(self, way, i):
        rows = chain_rows(way, i)
        return (self.part[rows, :].astype(F32) + self.landed[rows, :].astype(F32)).astype(BF16)

    def step(self, step):
        n, count = self.n, self.count
        for way in (0, 1):
            pos = self.pos(way)
            i = step - pos

            @pl.when((i >= 0) & (i < count))
            def _():
                @pl.when(pos == 0)
                def _():
                    self.sums(way, i).start()

                @pl.when((pos > 0) & (pos < n - 1))
                def _():
                    self.sums(way, i).wait_recv()
                    self.part[chain_rows(way, i), :] = self.added(way, i)
                    self.sums(way, i).start()

                @pl.when(pos == n - 1)
                def _():
                    self.sums(way, i).wait_recv()
                    self.full[chain_rows(way, i), :] = self.added(way, i)
                    self.totals(way, i).start()

            k = step - (n - 1) - (n - 1 - pos)

            @pl.when((k >= 0) & (k < count) & (pos < n - 1))
            def _():
                self.totals(way, k).wait_recv()

                @pl.when(pos > 0)
                def _():
                    self.totals(way, k).start()

    def drain(self):
        for way in (0, 1):
            pos = self.pos(way)

            @pl.loop(0, self.count)
            def _(i):
                @pl.when(pos < self.n - 1)
                def _():
                    self.sums(way, i).wait_send()

                @pl.when(pos > 0)
                def _():
                    self.totals(way, i).wait_send()


def chain_scratch(rows, width):
    return [pltpu.VMEM((rows, width), BF16)] * 3 + [pltpu.SemaphoreType.DMA((8, rows // 2 // CHUNK))]


class GradientSum:
    def __init__(self, grad, pair, summed, landed, shared, pair_sem, cross_sem, share_sem):
        self.grad, self.pair, self.summed, self.landed, self.shared = grad, pair, summed, landed, shared
        self.pair_sem, self.cross_sem, self.share_sem = pair_sem, cross_sem, share_sem
        self.ctx, self.me = lax.axis_size("ctx"), lax.axis_index("ctx")
        self.group = self.ctx // 2
        self.count = grad.shape[0]
        self.odd = lax.rem(self.me, 2)
        self.own = lax.axis_index("fsdp") * self.group + self.me // 2

    def pair_copy(self):
        return remote(
            self.grad.at[:, 1 - self.odd], self.pair, self.pair_sem.at[0], self.pair_sem.at[1],
            "ctx", self.me + 1 - 2 * self.odd,
        )

    def cross_copy(self, step):
        to = lax.rem(self.own + step, self.count)
        return remote_at(
            self.summed.at[to], self.landed.at[self.own],
            self.cross_sem.at[0, step], self.cross_sem.at[1, step],
            {"fsdp": to // self.group, "ctx": 2 * lax.rem(to, self.group) + self.odd},
        )

    def share_copy(self, step):
        return remote(
            self.shared.at[self.me], self.shared.at[self.me],
            self.share_sem.at[0, step], self.share_sem.at[1, step],
            "ctx", lax.rem(self.me + step, self.ctx),
        )

    def start_pair(self):
        self.pair_copy().start()

    def sum_pair(self):
        self.pair_copy().wait_recv()

        @pl.loop(0, self.count)
        def _(i):
            value = (self.grad[i, self.odd].astype(F32) + self.pair[i].astype(F32)).astype(BF16)
            self.summed[i] = value

        self.landed[self.own] = self.summed[self.own]

    def start_cross(self):
        @pl.loop(1, self.count)
        def _(step):
            self.cross_copy(step).start()

    def sum_cross(self):
        @pl.loop(1, self.count)
        def _(step):
            self.cross_copy(step).wait_recv()

        rows = self.grad.shape[2]
        part = min(rows, 32)

        @pl.loop(0, rows // part)
        def _(block):
            at = aligned(block * part, part)
            total = self.landed[0, at, :].astype(F32)
            for i in range(1, self.count):
                total = total + self.landed[i, at, :].astype(F32)
            self.shared[self.me, at, :] = total.astype(BF16)

    def start_share(self):
        @pl.loop(1, self.ctx)
        def _(step):
            self.share_copy(step).start()

    def wait_share(self):
        @pl.loop(1, self.ctx)
        def _(step):
            self.share_copy(step).wait_recv()

    def drain(self):
        self.pair_copy().wait_send()

        @pl.loop(1, self.count)
        def _(step):
            self.cross_copy(step).wait_send()

        @pl.loop(1, self.ctx)
        def _(step):
            self.share_copy(step).wait_send()


def gradient_scratch(pieces, ctx, rows, lanes):
    half = pieces // 2
    return [
        pltpu.VMEM((half, rows, lanes), BF16),
        pltpu.VMEM((half, rows, lanes), BF16),
        pltpu.VMEM((half, rows, lanes), BF16),
        pltpu.VMEM((ctx, rows, lanes), BF16),
        pltpu.SemaphoreType.DMA((2,)),
        pltpu.SemaphoreType.DMA((2, half)),
        pltpu.SemaphoreType.DMA((2, ctx)),
    ]


def put_pieces(grad, unit, lanes, value):
    value = value.astype(BF16)
    rows = grad.shape[2]
    if rows == ROWS:
        grad[unit // 2, lax.rem(unit, 2), :, lanes] = value
    else:
        many = ROWS // (2 * rows)
        grad[pl.ds(unit * many, many), :, :, lanes] = value.reshape(many, 2, rows, value.shape[1])


def first_kernel(
    x_ref, w_ref, up_ref, down_ref, proj_ref, b_ref, cos_ref, low_ref, high_ref, g_ref, bup_ref,
    gain_ref, shift_ref, outs_ref,
    stats_ref, n1_out, qkv_out, own_out, lse_out, w_out, mlp_out, sum_out, dr_out, grads_out, grad_out,
    n1, qkv, own, lse, w_full, mlp, summed, dr, grads, grad_land,
    send_buf, keys, back_buf, att, up_full, down_full, proj_full, down_t, proj_t,
    n2, act, dz, drb, slope_buf, grad_send, part, landed, full, chain_sem,
    out_sem, in_sem, back_sem, fetch_sem, hand_sem, row_sem, gather_sem, grad_sem, keep_sem,
):
    ctx, me = lax.axis_size("ctx"), lax.axis_index("ctx")
    fsdp, f = lax.axis_size("fsdp"), lax.axis_index("fsdp")
    n, j = lax.axis_size("tp"), lax.axis_index("tp")
    clips, length = lse.shape[0], lse.shape[2]
    local = length // ctx
    lane = b_ref.shape[2]
    heads = lane // HD
    rows_all, width = x_ref.shape
    hidden = act.shape[1]
    odd = lax.rem(me, 2)
    mate = me + 1 - 2 * odd
    span = w_ref.shape[1]
    half = span // 2
    blocks = local // ROWS
    chunks = clips * blocks
    chain = Chain(part, landed, full, chain_sem)
    many = chain.count // chunks
    greet("fsdp", "ctx", "tp")
    stats_ref[...] = jnp.zeros_like(stats_ref)

    def keep(k, source, target):
        return pltpu.make_async_copy(source, target, keep_sem.at[k])

    pieces = (w_ref, up_ref, proj_t, down_t)
    wholes = (w_full, up_full, proj_full, down_full)

    def band(ref, start, size):
        return ref.at[:, aligned(start, size)] if len(ref.shape) == 3 else ref.at[aligned(start, size)]

    def fetch(k, step):
        return remote(
            band(pieces[k], odd * half, half),
            band(wholes[k], f * span + odd * half, half),
            fetch_sem.at[0, k, step],
            fetch_sem.at[1, k, step],
            "fsdp",
            lax.rem(f + step, fsdp),
        )

    def hand(k, step):
        rows = lax.rem(f + fsdp - step, fsdp) * span + odd * half
        return remote(
            band(wholes[k], rows, half),
            band(wholes[k], rows, half),
            hand_sem.at[0, k, step],
            hand_sem.at[1, k, step],
            "ctx",
            mate,
        )

    def fetch_all(k):
        for step in range(1, fsdp):
            fetch(k, step).start()

    def pass_on(k):
        for step in range(1, fsdp):
            fetch(k, step).wait_recv()
            hand(k, step).start()

    def handed(k):
        for step in range(1, fsdp):
            hand(k, step).wait_recv()

    def row(way, block):
        view = proj_t.at[aligned(odd * half, half), aligned(block * lane, lane)]
        return remote(
            view, view, row_sem.at[0, way, block], row_sem.at[1, way, block],
            "tp", j + 1 if way == 0 else j - 1,
        )

    def other_half(step):
        view = proj_t.at[aligned(odd * half, half)]
        return remote(view, view, row_sem.at[0, 2, 0], row_sem.at[1, 2, 0], "ctx", mate)

    def ring(link, step):
        for way in (0, 1):
            block = j - step if way == 0 else j + step
            onward = (j < n - 1) if way == 0 else (j > 0)

            @pl.when((block >= 0) & (block < n))
            def _():
                if step > 0:
                    link(way, block).wait_recv()

                @pl.when(onward)
                def _():
                    link(way, block).start()

    def ring_drain(link):
        for way in (0, 1):
            onward = (j < n - 1) if way == 0 else (j > 0)
            for step in range(n):
                block = j - step if way == 0 else j + step

                @pl.when((block >= 0) & (block < n) & onward)
                def _():
                    link(way, block).wait_send()

    fetch_all(0)
    n2[0:span, 0:lane] = proj_ref[...].T
    proj_t[aligned(odd * half, half), aligned(j * lane, lane)] = n2[aligned(odd * half, half), 0:lane]
    down_t[...] = down_ref[...].T
    ring(row, 0)
    fetch_all(1)
    for c in range(3):
        w_full[c, aligned(f * span, span), :] = w_ref[c]

    @pl.loop(0, chunks)
    def _(block):
        rows = aligned(block * ROWS, ROWS)
        hat, _ = norm_parts(x_ref[rows, :].astype(F32))
        n1[rows, :] = (hat * gain_ref[0:1, :] + shift_ref[0:1, :]).astype(BF16)

    for step in range(1, n - 1):
        ring(row, step)
    pass_on(0)
    for step in range(n - 1, n):
        ring(row, step)
    fetch_all(2)
    fetch_all(3)
    other_half(0).start()
    handed(0)
    keep(0, w_full, w_out).start()
    keep(1, n1, n1_out).start()

    def outgoing(clip, step):
        peer = lax.rem(me + step, ctx)
        return remote(
            send_buf.at[clip, :, aligned(peer * HD, HD), :],
            qkv.at[clip, :, :, aligned(me * local, local)],
            out_sem.at[clip, step],
            in_sem.at[clip, step],
            "ctx",
            peer,
        )

    def returning(clip, step):
        peer = lax.rem(me + step, ctx)
        return remote(
            back_buf.at[clip, :, aligned(peer * local, local)],
            att.at[clip, aligned(j * lane + me * HD, HD), :],
            back_sem.at[0, clip, step],
            back_sem.at[1, clip, step],
            "ctx",
            peer,
        )

    for clip in range(clips):

        @pl.loop(0, blocks)
        def _(block):
            rows = aligned(clip * local + block * ROWS, ROWS)
            lanes = aligned(block * ROWS, ROWS)
            normed = n1[rows, :]
            cos_t = jnp.concatenate([cos_ref[:, rows]] * heads, axis=0)
            low_t = jnp.concatenate([low_ref[:, rows]] * heads, axis=0)
            high_t = jnp.concatenate([high_ref[:, rows]] * heads, axis=0)
            for c in range(3):
                moved = (mm(normed, w_full[c], 1, 0) + b_ref[c]).T
                if c < 2:
                    moved = turn(moved, cos_t, low_t, high_t, 1)
                moved = moved.astype(BF16)
                if c == 0:
                    moved = moved * jnp.asarray(SCALE, BF16)
                send_buf[clip, c, :, lanes] = moved

        for step in range(1, ctx):
            outgoing(clip, step).start()
        mine = aligned(me * local, local)
        for c in range(3):
            qkv[clip, c, :, mine] = send_buf[clip, c, aligned(me * HD, HD), :]

    def heads_link(chunk):
        def link(way, block):
            view = att.at[chunk // blocks, aligned(block * lane, lane), aligned(lax.rem(chunk, blocks) * ROWS, ROWS)]
            return remote(
                view, view, gather_sem.at[0, way, block, chunk], gather_sem.at[1, way, block, chunk],
                "tp", j + 1 if way == 0 else j - 1,
            )

        return link

    def send_heads(clip):
        for step in range(1, ctx):
            returning(clip, step).wait_recv()
        for chunk in range(clip * blocks, (clip + 1) * blocks):
            ring(heads_link(chunk), 0)

    own_rows = aligned(f * span, span)
    up_full[own_rows, :] = up_ref[...]
    down_full[own_rows, :] = down_t[...]

    for clip in range(clips):
        for step in range(1, ctx):
            outgoing(clip, step).wait_recv()
        keys[...] = qkv[clip, 1].T
        if clip == 1:
            pass_on(1)
            other_half(0).wait_recv()
            proj_full[own_rows, :] = proj_t[...]
            pass_on(2)

        @pl.loop(0, length // QB)
        def _(block):
            if clip == 1:

                @pl.when(block == length // QB // 2)
                def _():
                    send_heads(0)

            lanes = aligned(block * QB, QB)
            scores = mm(keys[...], qkv[clip, 0, :, lanes], 1, 0)
            largest = jnp.max(scores, axis=0, keepdims=True)
            expon = jnp.exp(scores - largest)
            totals = jnp.sum(expon, axis=0, keepdims=True)
            result = mm(qkv[clip, 2], expon.astype(BF16), 1, 0) / totals
            own[clip, :, lanes] = result
            lse[clip, :, lanes] = largest + jnp.log(totals)
            back_buf[clip, :, lanes] = result.astype(BF16)

        for step in range(1, ctx):
            returning(clip, step).start()
        att[clip, aligned(j * lane + me * HD, HD), :] = back_buf[clip, :, aligned(me * local, local)]
    pass_on(3)
    keep(2, qkv, qkv_out).start()
    keep(3, own, own_out).start()
    keep(4, lse, lse_out).start()

    def residual(rows):
        return x_ref[rows, :].astype(F32) + summed[rows, :].astype(F32) + outs_ref[0:1, :]

    def give(clip, step):
        peer = lax.rem(me + step, ctx)
        return remote(
            grad_send.at[clip, aligned(peer * HD, HD), :],
            grad_land.at[clip, :, aligned(me * local, local)],
            grad_sem.at[0, clip, step],
            grad_sem.at[1, clip, step],
            "ctx",
            peer,
        )

    def give_all(clip):
        @pl.loop(0, blocks)
        def _(block):
            value = mm(drb[aligned(clip * local + block * ROWS, ROWS), :], proj_full[:, aligned(j * lane, lane)], 1, 0)
            grad_send[clip, :, aligned(block * ROWS, ROWS)] = value.T.astype(BF16)

        for step in range(1, ctx):
            give(clip, step).start()
        grad_land[clip, :, aligned(me * local, local)] = grad_send[clip, aligned(me * HD, HD), :]
        keep(7 + clip, dr.at[pl.ds(clip * local, local)], dr_out.at[pl.ds(clip * local, local)]).start()

    ahead = n - 1
    lag = ahead + 1 + chain.hops // many

    @pl.loop(1, chunks + lag)
    def _(step):
        for hop in range(1, n):
            chunk = step - hop

            @pl.when((chunk >= 0) & (chunk < chunks))
            def _():
                ring(heads_link(chunk), hop)

        @pl.when(step == 1)
        def _():
            send_heads(1)

        @pl.when(step == ahead - 1)
        def _():
            for k in (1, 2, 3):
                handed(k)

        k = step - ahead
        rows = aligned(k * ROWS, ROWS)
        busy = (k >= 0) & (k < chunks)
        at = (step - ahead - 1) * many
        chain.step(at)

        @pl.when(busy)
        def _():
            heads_in = att[k // blocks, :, aligned(lax.rem(k, blocks) * ROWS, ROWS)].T
            summed[rows, :] = mm(heads_in, proj_full[...], 1, 1).astype(BF16)
            hat, _ = norm_parts(residual(rows))
            normed = (hat * gain_ref[1:2, :] + shift_ref[1:2, :]).astype(BF16)
            n2[rows, :] = normed
            pre = mm(normed, up_full[...], 1, 0) + bup_ref[...]
            cdf = 0.5 + 0.5 * lax.erf(pre * (0.5**0.5))
            act[rows, :] = (pre * cdf).astype(BF16)
            slope_buf[...] = cdf + pre * (jnp.exp(-0.5 * pre * pre) * 0.3989422804014327)

        for more in range(1, many):
            chain.step(at + more)

        @pl.when(busy)
        def _():
            grad = (mm(g_ref[rows, :], down_full[...], 1, 0) * slope_buf[...]).astype(BF16)
            dz[rows, :] = grad
            part[rows, :] = mm(grad, up_full[...], 1, 1).astype(BF16)
            mlp[rows, :] = mm(act[rows, :], down_full[...], 1, 1).astype(BF16)
            stats_ref[6:7, :] += jnp.sum(grad.astype(F32), axis=0, keepdims=True)

        done = step - lag

        @pl.when((done >= 0) & (done < chunks))
        def _():
            rows = aligned(done * ROWS, ROWS)
            hat, rstd = norm_parts(residual(rows))
            grad = full[rows, :].astype(F32)
            upstream = g_ref[rows, :].astype(F32)
            moved = upstream + norm_pull(hat, rstd, gain_ref[1:2, :], grad)
            dr[rows, :] = moved
            drb[rows, :] = moved.astype(BF16)
            stats_ref[2:3, :] += jnp.sum(grad * hat, axis=0, keepdims=True)
            stats_ref[3:4, :] += jnp.sum(grad, axis=0, keepdims=True)
            stats_ref[4:5, :] += jnp.sum(moved, axis=0, keepdims=True)
            stats_ref[5:6, :] += jnp.sum(upstream, axis=0, keepdims=True)

        @pl.when(done == blocks - 1)
        def _():
            give_all(0)

        @pl.when(step == chunks + ahead)
        def _():
            keep(5, mlp, mlp_out).start()
            keep(6, summed, sum_out).start()

        unit = step - ahead - chunks

        @pl.when((unit >= 0) & (unit * 2 < width // ROWS))
        def _():
            @pl.loop(0, 2)
            def _(more):
                u = unit * 2 + more
                lanes = aligned(u * ROWS, ROWS)
                put_pieces(grads, u, pl.ds(0, hidden), mm(n2[:, lanes], dz[...], 0, 0))
                put_pieces(grads, u, pl.ds(hidden, hidden), mm(g_ref[:, lanes], act[...], 0, 0))

    give_all(1)

    @pl.loop(0, width // ROWS)
    def _(unit):
        lanes = aligned(unit * ROWS, ROWS)
        value = jnp.zeros((ROWS, lane), F32)
        for clip in range(clips):
            value = value + mm(
                drb[clip * local : (clip + 1) * local, lanes], att[clip, aligned(j * lane, lane), :], 0, 1
            )
        put_pieces(grads, unit, pl.ds(2 * hidden, lane), value)

    keep(9, grads, grads_out).start()
    for clip in range(clips):
        for step in range(1, ctx):
            give(clip, step).wait_recv()
    keep(10, grad_land, grad_out).start()

    chain.drain()
    ring_drain(row)
    other_half(0).wait_send()

    @pl.loop(0, chunks)
    def _(chunk):
        ring_drain(heads_link(chunk))

    for clip in range(clips):
        for step in range(1, ctx):
            outgoing(clip, step).wait_send()
            returning(clip, step).wait_send()
            give(clip, step).wait_send()
    for k in range(4):
        for step in range(1, fsdp):
            fetch(k, step).wait_send()
            hand(k, step).wait_send()
    for k, (source, target) in enumerate(
        ((w_full, w_out), (n1, n1_out), (qkv, qkv_out), (own, own_out), (lse, lse_out), (mlp, mlp_out), (summed, sum_out))
    ):
        keep(k, source, target).wait()
    for clip in range(clips):
        keep(7 + clip, dr.at[pl.ds(clip * local, local)], dr_out.at[pl.ds(clip * local, local)]).wait()
    keep(9, grads, grads_out).wait()
    keep(10, grad_land, grad_out).wait()


def second_kernel(
    cos_ref, low_ref, high_ref, gain_ref, outs_ref, stats_ref,
    qkv_any, own_any, lse_any, grad_any, mlp_any, weights_any, x_any, sum_any, w_any, dr_any, n1_any,
    small_ref, block_out, grad_in_out, shared_out, shared_qkv_out,
    qkv_ref, own_ref, lse_ref, grad_ref, part, weights_ref, x_ref, sum_ref, w_ref, dr_ref, n1_ref,
    landed, full, sem, part_b, landed_b, full_b, sem_b,
    query, keys, vals, grads, acc_k, acc_v, send_buf, moved, dp_ref, grads_qkv, small, small_land,
    load_sem, keep_sem, out_sem, in_sem, small_sem, *sum_refs,
):
    n = lax.axis_size("tp")
    ctx, me = lax.axis_size("ctx"), lax.axis_index("ctx")
    clips, length = lse_ref.shape[0], lse_ref.shape[2]
    local = length // ctx
    lane = dp_ref.shape[2]
    heads = lane // HD
    width = x_ref.shape[1]
    blocks = length // QB
    pieces = lax.axis_size("fsdp") * ctx
    rank = lax.axis_index("fsdp") * ctx + me
    loads = [
        pltpu.make_async_copy(source, target, load_sem.at[k])
        for k, (source, target) in enumerate(
            (
                (qkv_any, qkv_ref), (own_any, own_ref), (lse_any, lse_ref), (grad_any, grad_ref),
                (mlp_any, part), (weights_any, weights_ref), (x_any, x_ref), (sum_any, sum_ref),
                (w_any, w_ref), (dr_any, dr_ref), (n1_any, n1_ref),
            )
        )
    ]
    for load in loads:
        load.start()
    weights = GradientSum(weights_ref, *sum_refs[:7])
    weights_qkv = GradientSum(grads_qkv, *sum_refs[7:])
    first = Chain(part, landed, full, sem)
    last = Chain(part_b, landed_b, full_b, sem_b)
    count, hops = first.count, first.hops
    greet_grid("tp")
    for k in range(5):
        loads[k].wait()
    small[...] = stats_ref[...]

    def outgoing(clip, step):
        peer = lax.rem(me + step, ctx)
        return remote(
            send_buf.at[clip, :, :, aligned(peer * local, local)],
            moved.at[clip, :, aligned(me * HD, HD), :],
            out_sem.at[clip, step],
            in_sem.at[clip, step],
            "ctx",
            peer,
        )

    def finish(i):
        @pl.when((i >= 0) & (i < count))
        def _():
            for way in (0, 1):
                rows = chain_rows(way, i)
                sum_ref[rows, :] = (
                    x_ref[rows, :].astype(F32)
                    + sum_ref[rows, :].astype(F32)
                    + outs_ref[0:1, :]
                    + full[rows, :].astype(F32)
                    + outs_ref[1:2, :]
                ).astype(BF16)

    def close(i):
        @pl.when((i >= 0) & (i < count))
        def _():
            for way in (0, 1):
                rows = chain_rows(way, i)
                hat, rstd = norm_parts(x_ref[rows, :].astype(F32))
                grad = full_b[rows, :].astype(F32)
                dr_ref[rows, :] += norm_pull(hat, rstd, gain_ref[0:1, :], grad)
                small[0:1, :] += jnp.sum(grad * hat, axis=0, keepdims=True)
                small[1:2, :] += jnp.sum(grad, axis=0, keepdims=True)

    def unturn(clip):
        for step in range(1, ctx):
            outgoing(clip, step).wait_recv()

        @pl.loop(0, local // ROWS)
        def _(block):
            lanes = aligned(block * ROWS, ROWS)
            rows = aligned(clip * local + block * ROWS, ROWS)
            cos_t = jnp.concatenate([cos_ref[:, rows]] * heads, axis=0)
            low_t = jnp.concatenate([low_ref[:, rows]] * heads, axis=0)
            high_t = jnp.concatenate([high_ref[:, rows]] * heads, axis=0)
            total = jnp.zeros((ROWS, width), F32)
            for c in range(3):
                value = moved[clip, c, :, lanes].astype(F32)
                if c < 2:
                    value = turn(value, cos_t, low_t, high_t, -1)
                value = value.T.astype(BF16)
                dp_ref[c, rows, :] = value
                small[7:8, c * lane : (c + 1) * lane] += jnp.sum(value.astype(F32), axis=0, keepdims=True)
                total = total + mm(value, w_ref[c], 1, 1)
            part_b[rows, :] = total.astype(BF16)

    half = blocks // 2
    for clip in range(clips):
        query[...] = qkv_ref[clip, 0].T
        keys[...] = qkv_ref[clip, 1].T
        vals[...] = qkv_ref[clip, 2].T
        grads[...] = grad_ref[clip].T
        acc_k[...] = jnp.zeros_like(acc_k)
        acc_v[...] = jnp.zeros_like(acc_v)
        if clip == 0:
            loads[5].wait()
            weights.start_pair()
            for k in range(6, len(loads)):
                loads[k].wait()

        @pl.loop(0, blocks)
        def _(block):
            at = clip * blocks + block
            first.step(at)
            finish(at - hops)
            if clip == 0:
                plan = ((1, weights.sum_pair), (2, weights.start_cross))
            else:
                plan = ((half - 1, lambda: unturn(0)), (half, weights.sum_cross), (half + 1, weights.start_share))

                @pl.when(block >= half)
                def _():
                    last.step(block - half)

            for place, act in plan:
                pl.when(block == place)(act)
            lanes = aligned(block * QB, QB)
            grad_t = grad_ref[clip, :, lanes]
            scores = mm(keys[...], qkv_ref[clip, 0, :, lanes], 1, 0)
            probs = jnp.exp(scores - lse_ref[clip, :, lanes])
            inner = jnp.sum(grad_t.astype(F32) * own_ref[clip, :, lanes], axis=0, keepdims=True)
            grad_probs = mm(vals[...], grad_t, 1, 0)
            grad_scores = (probs * (grad_probs - inner)).astype(BF16)
            acc_v[...] += mm(probs.astype(BF16), grads[lanes, :], 1, 0)
            acc_k[...] += mm(grad_scores, query[lanes, :], 1, 0)
            send_buf[clip, 0, :, lanes] = (mm(qkv_ref[clip, 1], grad_scores, 1, 0) * SCALE).astype(BF16)

        send_buf[clip, 1] = acc_k[...].T.astype(BF16)
        send_buf[clip, 2] = acc_v[...].T.astype(BF16)
        for step in range(1, ctx):
            outgoing(clip, step).start()
        for c in range(3):
            moved[clip, c, aligned(me * HD, HD), :] = send_buf[clip, c, :, aligned(me * local, local)]

    split = count // clips

    def both(step):
        last.step(step)
        close(step - hops)
        other = step - half + clips * blocks
        first.step(other)
        finish(other - hops)

    @pl.loop(half, split)
    def _(step):
        both(step)

    unturn(1)
    units = width // ROWS

    @pl.loop(split, count + hops)
    def _(step):
        both(step)

        @pl.when(step - split < 4)
        def _():
            @pl.loop(0, units // 4)
            def _(more):
                unit = (step - split) * (units // 4) + more
                normed = n1_ref[:, aligned(unit * ROWS, ROWS)]
                for c in range(3):
                    put_pieces(grads_qkv, unit, pl.ds(c * lane, lane), mm(normed, dp_ref[c], 0, 0))

        for place, act in (
            (4, weights_qkv.start_pair),
            (5, weights_qkv.sum_pair),
            (6, weights_qkv.start_cross),
            (9, weights_qkv.sum_cross),
            (10, weights_qkv.start_share),
        ):
            pl.when(step == split + place)(act)

    def spread(step):
        return remote_at(
            small, small_land.at[rank], small_sem.at[0, step], small_sem.at[1, step],
            spot(lax.rem(rank + step, pieces)),
        )

    @pl.loop(1, pieces)
    def _(step):
        spread(step).start()

    keeps = [
        pltpu.make_async_copy(source, target, keep_sem.at[k])
        for k, (source, target) in enumerate(
            (
                (dr_ref, grad_in_out),
                (sum_ref, block_out),
                (weights.shared, shared_out),
                (weights_qkv.shared, shared_qkv_out),
            )
        )
    ]
    keeps[0].start()
    keeps[1].start()
    small_land[rank] = small[...]
    weights.wait_share()
    keeps[2].start()
    weights_qkv.wait_share()
    keeps[3].start()
    first.drain()
    last.drain()
    weights.drain()
    weights_qkv.drain()
    for clip in range(clips):
        for step in range(1, ctx):
            outgoing(clip, step).wait_send()

    @pl.loop(1, pieces)
    def _(step):
        spread(step).wait_recv()

    total = small_land[0]
    for i in range(1, pieces):
        total = total + small_land[i]
    small_ref[...] = total

    @pl.loop(1, pieces)
    def _(step):
        spread(step).wait_send()

    for copy in keeps:
        copy.wait()


def rotary_tables(positions):
    rows = positions.shape[1]
    half = ROT // 2
    freqs = 10000.0 ** (-2.0 * jnp.arange(half, dtype=F32) / ROT)
    angles = positions.astype(F32)[:, None, :] * freqs[None, :, None]
    cos, sin = jnp.cos(angles), jnp.sin(angles)
    zero = jnp.zeros_like(sin)
    rest = HD - 3 * ROT

    def fill(first, second, value):
        table = jnp.concatenate([first, second], axis=1).reshape(3 * ROT, rows)
        return jnp.concatenate([table, jnp.full((rest, rows), value, F32)], axis=0)

    return fill(cos, cos, 1.0), fill(-sin, zero, 0.0), fill(zero, sin, 0.0)


VMEM = pl.BlockSpec(memory_space=pltpu.VMEM)
ANY = pl.BlockSpec(memory_space=pl.ANY)


def call(kernel, name, number, ins, outs, scratch, flops, held=0, kept=0):
    moved = sum(a.size * a.dtype.itemsize for a in (*ins, *outs))
    return pl.pallas_call(
        kernel,
        name=name,
        out_shape=outs,
        in_specs=[VMEM] * (len(ins) - held) + [ANY] * held,
        out_specs=[VMEM] * (len(outs) - kept) + [ANY] * kept,
        scratch_shapes=scratch,
        cost_estimate=pl.CostEstimate(flops=flops, bytes_accessed=moved, transcendentals=0),
        compiler_params=pltpu.CompilerParams(
            collective_id=number, has_side_effects=True, vmem_limit_bytes=63 * 1024 * 1024
        ),
    )(*ins)


def shards(
    block_input, positions, w_qkv, b_qkv, w_proj, w_up, b_up, w_down,
    norm_gains, norm_shifts, out_shifts, grad_out,
):
    clips, local, width = block_input.shape
    rows = clips * local
    ctx, n = lax.axis_size("ctx"), lax.axis_size("tp")
    lane = w_qkv.shape[2]
    hidden = w_up.shape[1]
    length = local * ctx
    assert lane == ctx * HD and clips == 2 and hidden == width
    assert width == w_down.shape[0]
    fsdp = lax.axis_size("fsdp")
    pieces = fsdp * ctx
    span = width // fsdp
    piece = span // ctx
    dma = pltpu.SemaphoreType.DMA
    shape = jax.ShapeDtypeStruct
    vmem = pltpu.VMEM
    chunks = rows // ROWS

    x = block_input.reshape(rows, width)
    g = grad_out.reshape(rows, width)
    tables = rotary_tables(positions.reshape(3, rows))
    lanes = 2 * hidden + lane
    carried = (
        ((rows, width), BF16),
        ((clips, 3, HD, length), BF16),
        ((clips, HD, length), F32),
        ((clips, 1, length), F32),
        ((3, width, lane), BF16),
        ((rows, width), BF16),
        ((rows, width), BF16),
        ((rows, width), F32),
        ((pieces // 2, 2, piece, lanes), BF16),
        ((clips, HD, length), BF16),
    )
    stats, n1, qkv, own, lse, full_qkv, mlp, summed, dr, grads, grad_att = call(
        first_kernel,
        "first",
        0,
        (
            x, w_qkv, w_up, w_down, w_proj, b_qkv.reshape(3, 1, lane), *tables, g,
            b_up.reshape(1, hidden), norm_gains, norm_shifts, out_shifts,
        ),
        (shape((8, width), F32), *(shape(*item) for item in carried)),
        [vmem(*item) for item in carried]
        + [
            vmem((clips, 3, lane, local), BF16),
            vmem((length, HD), BF16),
            vmem((clips, HD, length), BF16),
            vmem((clips, n * lane, local), BF16),
            vmem((width, hidden), BF16),
            vmem((width, hidden), BF16),
            vmem((width, n * lane), BF16),
            vmem((span, hidden), BF16),
            vmem((span, n * lane), BF16),
            vmem((rows, width), BF16),
            vmem((rows, hidden), BF16),
            vmem((rows, hidden), BF16),
            vmem((rows, width), BF16),
            vmem((ROWS, hidden), F32),
            vmem((clips, lane, local), BF16),
        ]
        + chain_scratch(rows, width)
        + [
            dma((clips, ctx)),
            dma((clips, ctx)),
            dma((2, clips, ctx)),
            dma((2, 4, fsdp)),
            dma((2, 4, fsdp)),
            dma((2, 3, n)),
            dma((2, 2, n, chunks)),
            dma((2, clips, ctx)),
            dma((11,)),
        ],
        2 * rows * width * (3 * lane + n * lane + 6 * hidden) + 4 * clips * length * length * HD,
        kept=10,
    )

    held = (qkv, own, lse, grad_att, mlp, grads, x, summed, full_qkv, dr, n1)
    chain = chain_scratch(rows, width)
    small, block_output, grad_input, shared, shared_qkv = call(
        second_kernel,
        "second",
        1,
        (*tables, norm_gains, out_shifts, stats, *held),
        (
            shape((8, width), F32),
            shape((rows, width), BF16),
            shape((rows, width), F32),
            shape((ctx, piece, lanes), BF16),
            shape((ctx, piece, 3 * lane), BF16),
        ),
        [vmem(item.shape, item.dtype) for item in held]
        + chain[1:]
        + chain
        + [vmem((length, HD), BF16)] * 4
        + [vmem((length, HD), F32)] * 2
        + [
            vmem((clips, 3, HD, length), BF16),
            vmem((clips, 3, lane, local), BF16),
            vmem((3, rows, lane), BF16),
            vmem((pieces // 2, 2, piece, 3 * lane), BF16),
            vmem((8, width), F32),
            vmem((pieces, 8, width), F32),
            dma((len(held),)),
            dma((4,)),
            dma((clips, ctx)),
            dma((clips, ctx)),
            dma((2, pieces)),
        ]
        + gradient_scratch(pieces, ctx, piece, lanes)
        + gradient_scratch(pieces, ctx, piece, 3 * lane),
        4 * rows * width * 3 * lane + 10 * clips * length * length * HD,
        held=len(held),
        kept=4,
    )
    shared = shared.reshape(span, lanes)
    shared_qkv = shared_qkv.reshape(span, 3, lane)
    return (
        block_output.reshape(clips, local, width),
        grad_input.reshape(clips, local, width),
        shared_qkv.transpose(1, 0, 2).astype(F32),
        small[7, : 3 * lane].reshape(3, lane),
        shared[:, 2 * hidden :].T.astype(F32),
        shared[:, :hidden].astype(F32),
        small[6],
        shared[:, hidden : 2 * hidden].T.astype(F32),
        small[0:4:2],
        small[1:4:2],
        small[4:6],
    )


def solution(mesh):
    rows = P("fsdp", "ctx", None)
    in_specs = (
        rows,
        P(None, "fsdp", "ctx"),
        P(None, "fsdp", "tp"),
        P(None, "tp"),
        P("tp", "fsdp"),
        P("fsdp", "tp"),
        P("tp"),
        P("tp", "fsdp"),
        P(),
        P(),
        P(),
        rows,
    )
    out_specs = (
        rows,
        rows,
        P(None, "fsdp", "tp"),
        P(None, "tp"),
        P("tp", "fsdp"),
        P("fsdp", "tp"),
        P("tp"),
        P("tp", "fsdp"),
        P(),
        P(),
        P(),
    )
    return jax.shard_map(shards, mesh=mesh, in_specs=in_specs, out_specs=out_specs, check_vma=False)
```

time: 398 us -> 339 us (0.85)
  Pallas kernels: 376 us -> 310 us
  other arithmetic: 1.52 us -> 7.29 us
    pallas_call x4 -> x2, Pallas kernels: 376 us -> 310 us  [call(): pl.pallas_call(kernel, name=name, out_shape=outs, in_specs=[VMEM] * (len(...]
    unnamed x32 -> x10, local copies, waits for them, and re-layouts: 15.4 us -> 8.41 us
    slice x0 -> x5, local copies, waits for them, and re-layouts: none -> 6.2 us  [the longest x1 1.37 us: shards(): small[1:4:2]]
where the time goes in v3:
time: 339 us; the launch traced here: 338 us
  Pallas kernels  310 us (91%)
  local copies, waits for them, and re-layouts  20 us (6%)
  other arithmetic  7.29 us (2%)
    pallas_call x2, Pallas kernels, call(): pl.pallas_call(kernel, name=name, out_shape=outs, in_specs=[VMEM] * (len(...  310 us
    unnamed x10, local copies, waits for them, and re-layouts  8.41 us

profile of v3, /device:TPU:0, one launch (start us, length us, event | category | flops | bytes accessed | tf_op | source)
XLA Modules:
  0.0 338.4 jit_solution(18249116806865673112)
XLA Ops:
  0.7 1.3 reshape.71.b_ref
  1.9 0.7 convert_bitcast_fusion.2
  2.6 0.8 multiply_sine_fusion
  3.5 0.7 concatenate.23.high_ref
  4.3 0.7 concatenate.21.low_ref
  5.1 0.7 concatenate.19.cos_ref
  5.8 163.2 %first.1 = (f32[8,1024]{1,0:T(8,128)}, bf16[1024,1024]{1,0:T(8,128)(2,1)}, bf16[2,3,64,2048]{3,2,1,0:T(8,128)(2,1)}, f32[2,64,2048]{2,1,0:T(8,128)}, f32[2,1,204...) custom-call(bf16[1024,1024]{1,0:T(8,128)(2,1)} %bitcast.25, ...), custom_call_target="tpu_custom_call" | custom-call | flops 18790481920 | bytes 28130304 | tf_op jit(solution)/shard_map/first/pallas_call | solution.py:961
  169.0 147.2 %second.1 = (f32[8,1024]{1,0:T(8,128)}, bf16[1024,1024]{1,0:T(8,128)(2,1)}, f32[1024,1024]{1,0:T(8,128)}, bf16[4,128,2304]{2,1,0:T(8,128)(2,1)}, bf16[4,128,768]{2,1,0:T(8,128)(2,1)}) custom-call(f32[64,1024]{1,0:T(8,128)} %concatenate.19.cos_ref, f32[64,1024]{1,0:T(8,128)} %concatenate.21.low_ref, f32[64,1024]{1,0:T(8,128)} %concatenate.23.high_ref, ...), custom_call_target="tpu_custom_call" | custom-call | flops 8589934592 | bytes 32342016 | tf_op jit(solution)/shard_map/second/pallas_call | solution.py:961
  316.2 1.4 slice.27
  317.6 0.8 slice_reduce_fusion
  318.3 0.6 reshape_squeeze.3
  318.9 1.4 slice.31
  320.3 1.4 slice.30
  321.6 1.4 slice.29
  323.0 1.0 convert_bitcast_fusion.1
  324.0 1.0 copy.29
  325.0 3.2 fusion.1
  328.2 0.5 copy.30
  328.7 0.0 copy-start.1
  328.7 1.6 convert_bitcast_fusion
  330.3 0.0 copy-done.1
  330.3 0.6 copy.26
  330.9 0.6 reshape.77
  331.6 1.6 copy.28
  333.2 0.0 copy-start
  333.2 3.2 copy.34
  336.4 0.0 copy-done
  336.4 2.0 copy.35
  (8 shorter events, 0.2 us)
Async XLA Ops:
  328.7 1.6 copy-start.1
  333.2 3.2 copy-start

commit v4 on v3

--- a/solution.py
+++ b/solution.py
@@ -12,6 +12,7 @@
 EPSILON = 1e-06
 SCALE = HD ** (-0.5)
 QB = 256
+LAG = 2
 CHUNK = 32
 ROWS = 128
 MESH = pl.DeviceIdType.MESH
@@ -108,6 +109,26 @@
     return values * cos_t - (up * low_t + down * high_t)
 
 
+def fill_tables(pos_ref, cos_t, low_t, high_t):
+    half = ROT // 2
+    local = pos_ref.shape[2]
+    channel = lax.broadcasted_iota(jnp.int32, (HD, 1), 0)
+    place = lax.rem(channel, ROT)
+    index = lax.rem(place, half)
+    freq = jnp.zeros((HD, 1), F32)
+    for i in range(half):
+        freq = jnp.where(index == i, 10000.0 ** (-2.0 * i / ROT), freq)
+    turned = channel < 3 * ROT
+    for clip in range(pos_ref.shape[1]):
+        pos = [pos_ref[a, clip : clip + 1, :].astype(F32) for a in range(3)]
+        angle = freq * jnp.where(channel < ROT, pos[0], jnp.where(channel < 2 * ROT, pos[1], pos[2]))
+        sine = jnp.sin(angle)
+        lanes = pl.ds(clip * local, local)
+        cos_t[:, lanes] = jnp.where(turned, jnp.cos(angle), 1.0)
+        low_t[:, lanes] = jnp.where(turned & (place < half), -sine, 0.0)
+        high_t[:, lanes] = jnp.where(turned & (place >= half), sine, 0.0)
+
+
 def chain_rows(way, i):
     many = ROWS // 2 // CHUNK
     return aligned((i // many) * ROWS + way * (ROWS // 2) + lax.rem(i, many) * CHUNK, CHUNK)
@@ -118,7 +139,7 @@
         self.part, self.landed, self.full, self.sems = part, landed, full, sems
         self.n, self.j = lax.axis_size("tp"), lax.axis_index("tp")
         self.count = part.shape[0] // 2 // CHUNK
-        self.hops = 2 * (self.n - 1)
+        self.hops = 2 * (self.n - 1) * LAG
 
     def pos(self, way):
         return (self.n - 1 - self.j) if way == 0 else self.j
@@ -147,7 +168,7 @@
         n, count = self.n, self.count
         for way in (0, 1):
             pos = self.pos(way)
-            i = step - pos
+            i = step - pos * LAG
 
             @pl.when((i >= 0) & (i < count))
             def _():
@@ -167,7 +188,7 @@
                     self.full[chain_rows(way, i), :] = self.added(way, i)
                     self.totals(way, i).start()
 
-            k = step - (n - 1) - (n - 1 - pos)
+            k = step - (2 * (n - 1) - pos) * LAG
 
             @pl.when((k >= 0) & (k < count) & (pos < n - 1))
             def _():
@@ -221,10 +242,18 @@
         )
 
     def share_copy(self, step):
+        to = self.me + 1 - 2 * self.odd if step == 0 else lax.rem(self.me + 2 * step, self.ctx)
         return remote(
             self.shared.at[self.me], self.shared.at[self.me],
-            self.share_sem.at[0, step], self.share_sem.at[1, step],
-            "ctx", lax.rem(self.me + step, self.ctx),
+            self.share_sem.at[0, step], self.share_sem.at[1, step], "ctx", to,
+        )
+
+    def pass_copy(self, step):
+        slot = lax.rem(self.me + self.ctx - 2 * step, self.ctx)
+        return remote(
+            self.shared.at[slot], self.shared.at[slot],
+            self.share_sem.at[2, step], self.share_sem.at[3, step],
+            "ctx", self.me + 1 - 2 * self.odd,
         )
 
     def start_pair(self):
@@ -262,14 +291,18 @@
             self.shared[self.me, at, :] = total.astype(BF16)
 
     def start_share(self):
-        @pl.loop(1, self.ctx)
-        def _(step):
+        for step in range(self.group):
             self.share_copy(step).start()
 
+    def pass_share(self):
+        for step in range(1, self.group):
+            self.share_copy(step).wait_recv()
+            self.pass_copy(step).start()
+
     def wait_share(self):
-        @pl.loop(1, self.ctx)
-        def _(step):
-            self.share_copy(step).wait_recv()
+        self.share_copy(0).wait_recv()
+        for step in range(1, self.group):
+            self.pass_copy(step).wait_recv()
 
     def drain(self):
         self.pair_copy().wait_send()
@@ -278,9 +311,10 @@
         def _(step):
             self.cross_copy(step).wait_send()
 
-        @pl.loop(1, self.ctx)
-        def _(step):
+        for step in range(self.group):
             self.share_copy(step).wait_send()
+            if step > 0:
+                self.pass_copy(step).wait_send()
 
 
 def gradient_scratch(pieces, ctx, rows, lanes):
@@ -292,7 +326,7 @@
         pltpu.VMEM((ctx, rows, lanes), BF16),
         pltpu.SemaphoreType.DMA((2,)),
         pltpu.SemaphoreType.DMA((2, half)),
-        pltpu.SemaphoreType.DMA((2, ctx)),
+        pltpu.SemaphoreType.DMA((4, ctx)),
     ]
 
 
@@ -307,12 +341,13 @@
 
 
 def first_kernel(
-    x_ref, w_ref, up_ref, down_ref, proj_ref, b_ref, cos_ref, low_ref, high_ref, g_ref, bup_ref,
-    gain_ref, shift_ref, outs_ref,
+    b_ref, pos_ref, bup_ref, gain_ref, shift_ref, outs_ref,
+    x_any, w_any, up_any, down_any, proj_any, g_any,
     stats_ref, n1_out, qkv_out, own_out, lse_out, w_out, mlp_out, sum_out, dr_out, grads_out, grad_out,
     n1, qkv, own, lse, w_full, mlp, summed, dr, grads, grad_land,
     send_buf, keys, back_buf, att, up_full, down_full, proj_full, down_t, proj_t,
     n2, act, dz, drb, slope_buf, grad_send, part, landed, full, chain_sem,
+    cos_ref, low_ref, high_ref, x_ref, down_ref, proj_ref, g_ref, load_sem,
     out_sem, in_sem, back_sem, fetch_sem, hand_sem, row_sem, gather_sem, grad_sem, keep_sem,
 ):
     ctx, me = lax.axis_size("ctx"), lax.axis_index("ctx")
@@ -320,25 +355,41 @@
     n, j = lax.axis_size("tp"), lax.axis_index("tp")
     clips, length = lse.shape[0], lse.shape[2]
     local = length // ctx
-    lane = b_ref.shape[2]
+    lane = b_ref.shape[1]
     heads = lane // HD
     rows_all, width = x_ref.shape
     hidden = act.shape[1]
     odd = lax.rem(me, 2)
     mate = me + 1 - 2 * odd
-    span = w_ref.shape[1]
+    span = w_any.shape[1]
     half = span // 2
     blocks = local // ROWS
     chunks = clips * blocks
     chain = Chain(part, landed, full, chain_sem)
     many = chain.count // chunks
+    own_rows = aligned(f * span, span)
+    load_x, load_w, load_up, load_down, load_proj, load_g = (
+        pltpu.make_async_copy(source, target, load_sem.at[k])
+        for k, (source, target) in enumerate(
+            (
+                (x_any, x_ref),
+                (w_any, w_full.at[:, own_rows]),
+                (up_any, up_full.at[own_rows]),
+                (down_any, down_ref),
+                (proj_any, proj_ref),
+                (g_any, g_ref),
+            )
+        )
+    )
+    for load in (load_proj, load_x, load_w, load_down, load_up, load_g):
+        load.start()
     greet("fsdp", "ctx", "tp")
     stats_ref[...] = jnp.zeros_like(stats_ref)
 
     def keep(k, source, target):
         return pltpu.make_async_copy(source, target, keep_sem.at[k])
 
-    pieces = (w_ref, up_ref, proj_t, down_t)
+    pieces = (w_any, up_any, proj_t, down_t)
     wholes = (w_full, up_full, proj_full, down_full)
 
     def band(ref, start, size):
@@ -414,13 +465,15 @@
                     link(way, block).wait_send()
 
     fetch_all(0)
+    fetch_all(1)
+    load_proj.wait()
     n2[0:span, 0:lane] = proj_ref[...].T
     proj_t[aligned(odd * half, half), aligned(j * lane, lane)] = n2[aligned(odd * half, half), 0:lane]
+    ring(row, 0)
+    load_down.wait()
     down_t[...] = down_ref[...].T
-    ring(row, 0)
-    fetch_all(1)
-    for c in range(3):
-        w_full[c, aligned(f * span, span), :] = w_ref[c]
+    load_x.wait()
+    fill_tables(pos_ref, cos_ref, low_ref, high_ref)
 
     @pl.loop(0, chunks)
     def _(block):
@@ -437,6 +490,7 @@
     fetch_all(3)
     other_half(0).start()
     handed(0)
+    load_w.wait()
     keep(0, w_full, w_out).start()
     keep(1, n1, n1_out).start()
 
@@ -473,7 +527,7 @@
             low_t = jnp.concatenate([low_ref[:, rows]] * heads, axis=0)
             high_t = jnp.concatenate([high_ref[:, rows]] * heads, axis=0)
             for c in range(3):
-                moved = (mm(normed, w_full[c], 1, 0) + b_ref[c]).T
+                moved = (mm(normed, w_full[c], 1, 0) + b_ref[c : c + 1, :]).T
                 if c < 2:
                     moved = turn(moved, cos_t, low_t, high_t, 1)
                 moved = moved.astype(BF16)
@@ -503,8 +557,20 @@
         for chunk in range(clip * blocks, (clip + 1) * blocks):
             ring(heads_link(chunk), 0)
 
-    own_rows = aligned(f * span, span)
-    up_full[own_rows, :] = up_ref[...]
+    def ring_step(step):
+        for hop in range(1, n):
+            chunk = step + 2 * (n - 1 - hop)
+            if isinstance(step, int):
+                if 0 <= chunk < chunks:
+                    ring(heads_link(chunk), hop)
+            else:
+
+                @pl.when(chunk < chunks)
+                def _():
+                    ring(heads_link(chunk), hop)
+
+    load_up.wait()
+    load_g.wait()
     down_full[own_rows, :] = down_t[...]
 
     for clip in range(clips):
@@ -525,6 +591,12 @@
                 def _():
                     send_heads(0)
 
+                for early in range(-2 * (n - 2), -2):
+
+                    @pl.when(block == length // QB - 1)
+                    def _():
+                        ring_step(early)
+
             lanes = aligned(block * QB, QB)
             scores = mm(keys[...], qkv[clip, 0, :, lanes], 1, 0)
             largest = jnp.max(scores, axis=0, keepdims=True)
@@ -538,7 +610,12 @@
         for step in range(1, ctx):
             returning(clip, step).start()
         att[clip, aligned(j * lane + me * HD, HD), :] = back_buf[clip, :, aligned(me * local, local)]
+    ring_step(-2)
+    send_heads(1)
     pass_on(3)
+    ring_step(-1)
+    for k in (1, 2, 3):
+        handed(k)
     keep(2, qkv, qkv_out).start()
     keep(3, own, own_out).start()
     keep(4, lse, lse_out).start()
@@ -568,31 +645,15 @@
         grad_land[clip, :, aligned(me * local, local)] = grad_send[clip, aligned(me * HD, HD), :]
         keep(7 + clip, dr.at[pl.ds(clip * local, local)], dr_out.at[pl.ds(clip * local, local)]).start()
 
-    ahead = n - 1
-    lag = ahead + 1 + chain.hops // many
-
-    @pl.loop(1, chunks + lag)
+    lag = 1 + pl.cdiv(chain.hops, many)
+
+    @pl.loop(0, chunks + lag)
     def _(step):
-        for hop in range(1, n):
-            chunk = step - hop
-
-            @pl.when((chunk >= 0) & (chunk < chunks))
-            def _():
-                ring(heads_link(chunk), hop)
-
-        @pl.when(step == 1)
-        def _():
-            send_heads(1)
-
-        @pl.when(step == ahead - 1)
-        def _():
-            for k in (1, 2, 3):
-                handed(k)
-
-        k = step - ahead
+        k = step
         rows = aligned(k * ROWS, ROWS)
-        busy = (k >= 0) & (k < chunks)
-        at = (step - ahead - 1) * many
+        busy = k < chunks
+        pl.when(busy)(lambda: ring_step(step))
+        at = (step - 1) * many
         chain.step(at)
 
         @pl.when(busy)
@@ -638,12 +699,12 @@
         def _():
             give_all(0)
 
-        @pl.when(step == chunks + ahead)
+        @pl.when(step == chunks)
         def _():
             keep(5, mlp, mlp_out).start()
             keep(6, summed, sum_out).start()
 
-        unit = step - ahead - chunks
+        unit = step - chunks
 
         @pl.when((unit >= 0) & (unit * 2 < width // ROWS))
         def _():
@@ -700,13 +761,13 @@
 
 
 def second_kernel(
-    cos_ref, low_ref, high_ref, gain_ref, outs_ref, stats_ref,
+    pos_ref, gain_ref, outs_ref, stats_ref,
     qkv_any, own_any, lse_any, grad_any, mlp_any, weights_any, x_any, sum_any, w_any, dr_any, n1_any,
-    small_ref, block_out, grad_in_out, shared_out, shared_qkv_out,
+    bqkv_ref, bup_ref, gains_ref, shifts_ref, sums_ref, w_out, proj_out, up_out, down_out, block_out, grad_in_out,
     qkv_ref, own_ref, lse_ref, grad_ref, part, weights_ref, x_ref, sum_ref, w_ref, dr_ref, n1_ref,
     landed, full, sem, part_b, landed_b, full_b, sem_b,
     query, keys, vals, grads, acc_k, acc_v, send_buf, moved, dp_ref, grads_qkv, small, small_land,
-    load_sem, keep_sem, out_sem, in_sem, small_sem, *sum_refs,
+    cos_ref, low_ref, high_ref, load_sem, keep_sem, out_sem, in_sem, small_sem, *sum_refs,
 ):
     n = lax.axis_size("tp")
     ctx, me = lax.axis_size("ctx"), lax.axis_index("ctx")
@@ -735,6 +796,7 @@
     first = Chain(part, landed, full, sem)
     last = Chain(part_b, landed_b, full_b, sem_b)
     count, hops = first.count, first.hops
+    fill_tables(pos_ref, cos_ref, low_ref, high_ref)
     greet_grid("tp")
     for k in range(5):
         loads[k].wait()
@@ -797,7 +859,6 @@
                 total = total + mm(value, w_ref[c], 1, 1)
             part_b[rows, :] = total.astype(BF16)
 
-    half = blocks // 2
     for clip in range(clips):
         query[...] = qkv_ref[clip, 0].T
         keys[...] = qkv_ref[clip, 1].T
@@ -814,19 +875,15 @@
         @pl.loop(0, blocks)
         def _(block):
             at = clip * blocks + block
-            first.step(at)
-            finish(at - hops)
+
+            @pl.when(lax.rem(at, 2) == 0)
+            def _():
+                first.step(at // 2)
+                finish(at // 2 - hops)
+
             if clip == 0:
-                plan = ((1, weights.sum_pair), (2, weights.start_cross))
-            else:
-                plan = ((half - 1, lambda: unturn(0)), (half, weights.sum_cross), (half + 1, weights.start_share))
-
-                @pl.when(block >= half)
-                def _():
-                    last.step(block - half)
-
-            for place, act in plan:
-                pl.when(block == place)(act)
+                pl.when(block == 1)(weights.sum_pair)
+                pl.when(block == 2)(weights.start_cross)
             lanes = aligned(block * QB, QB)
             grad_t = grad_ref[clip, :, lanes]
             scores = mm(keys[...], qkv_ref[clip, 0, :, lanes], 1, 0)
@@ -845,23 +902,38 @@
         for c in range(3):
             moved[clip, c, aligned(me * HD, HD), :] = send_buf[clip, c, :, aligned(me * local, local)]
 
-    split = count // clips
+    done = clips * blocks // 2
+    early = done + 3
+    total = count + hops
+    split = count // clips // 2
+    units = width // ROWS
+
+    @pl.loop(done, early)
+    def _(step):
+        first.step(step)
+        finish(step - hops)
+
+    unturn(0)
 
     def both(step):
         last.step(step)
         close(step - hops)
-        other = step - half + clips * blocks
-        first.step(other)
-        finish(other - hops)
-
-    @pl.loop(half, split)
+        other = (step * (total - early)) // total
+
+        @pl.when(other != ((step - 1 + total) * (total - early)) // total - (total - early))
+        def _():
+            first.step(early + other)
+            finish(early + other - hops)
+
+    @pl.loop(0, split)
     def _(step):
         both(step)
+        pl.when(step == 1)(weights.sum_cross)
+        pl.when(step == 2)(weights.start_share)
 
     unturn(1)
-    units = width // ROWS
-
-    @pl.loop(split, count + hops)
+
+    @pl.loop(split, total)
     def _(step):
         both(step)
 
@@ -875,11 +947,13 @@
                     put_pieces(grads_qkv, unit, pl.ds(c * lane, lane), mm(normed, dp_ref[c], 0, 0))
 
         for place, act in (
+            (2, weights.pass_share),
             (4, weights_qkv.start_pair),
             (5, weights_qkv.sum_pair),
             (6, weights_qkv.start_cross),
             (9, weights_qkv.sum_cross),
             (10, weights_qkv.start_share),
+            (13, weights_qkv.pass_share),
         ):
             pl.when(step == split + place)(act)
 
@@ -899,18 +973,25 @@
             (
                 (dr_ref, grad_in_out),
                 (sum_ref, block_out),
-                (weights.shared, shared_out),
-                (weights_qkv.shared, shared_qkv_out),
             )
         )
     ]
     keeps[0].start()
     keeps[1].start()
     small_land[rank] = small[...]
+    rows = weights.shared.shape[1]
+    hidden = up_out.shape[1]
     weights.wait_share()
-    keeps[2].start()
+    for c in range(ctx):
+        at = pl.ds(c * rows, rows)
+        up_out[at, :] = weights.shared[c, :, 0:hidden]
+    down_out[...] = weights.shared[:, :, hidden : 2 * hidden].reshape(ctx * rows, hidden).T
+    proj_out[...] = weights.shared[:, :, 2 * hidden :].reshape(ctx * rows, lane).T
     weights_qkv.wait_share()
-    keeps[3].start()
+    for i in range(ctx):
+        at = pl.ds(i * rows, rows)
+        for c in range(3):
+            w_out[c, at, :] = weights_qkv.shared[i, :, c * lane : (c + 1) * lane]
     first.drain()
     last.drain()
     weights.drain()
@@ -923,10 +1004,17 @@
     def _(step):
         spread(step).wait_recv()
 
-    total = small_land[0]
+    sums = small_land[0]
     for i in range(1, pieces):
-        total = total + small_land[i]
-    small_ref[...] = total
+        sums = sums + small_land[i]
+    gains_ref[0:1, :] = sums[0:1]
+    gains_ref[1:2, :] = sums[2:3]
+    shifts_ref[0:1, :] = sums[1:2]
+    shifts_ref[1:2, :] = sums[3:4]
+    sums_ref[...] = sums[4:6]
+    bup_ref[...] = sums[6:7]
+    for c in range(3):
+        bqkv_ref[c : c + 1, :] = sums[7:8, c * lane : (c + 1) * lane]
 
     @pl.loop(1, pieces)
     def _(step):
@@ -934,22 +1022,6 @@
 
     for copy in keeps:
         copy.wait()
-
-
-def rotary_tables(positions):
-    rows = positions.shape[1]
-    half = ROT // 2
-    freqs = 10000.0 ** (-2.0 * jnp.arange(half, dtype=F32) / ROT)
-    angles = positions.astype(F32)[:, None, :] * freqs[None, :, None]
-    cos, sin = jnp.cos(angles), jnp.sin(angles)
-    zero = jnp.zeros_like(sin)
-    rest = HD - 3 * ROT
-
-    def fill(first, second, value):
-        table = jnp.concatenate([first, second], axis=1).reshape(3 * ROT, rows)
-        return jnp.concatenate([table, jnp.full((rest, rows), value, F32)], axis=0)
-
-    return fill(cos, cos, 1.0), fill(-sin, zero, 0.0), fill(zero, sin, 0.0)
 
 
 VMEM = pl.BlockSpec(memory_space=pltpu.VMEM)
@@ -995,7 +1067,6 @@
 
     x = block_input.reshape(rows, width)
     g = grad_out.reshape(rows, width)
-    tables = rotary_tables(positions.reshape(3, rows))
     lanes = 2 * hidden + lane
     carried = (
         ((rows, width), BF16),
@@ -1014,8 +1085,8 @@
         "first",
         0,
         (
-            x, w_qkv, w_up, w_down, w_proj, b_qkv.reshape(3, 1, lane), *tables, g,
-            b_up.reshape(1, hidden), norm_gains, norm_shifts, out_shifts,
+            b_qkv, positions, b_up.reshape(1, hidden), norm_gains, norm_shifts, out_shifts,
+            x, w_qkv, w_up, w_down, w_proj, g,
         ),
         (shape((8, width), F32), *(shape(*item) for item in carried)),
         [vmem(*item) for item in carried]
@@ -1037,7 +1108,13 @@
             vmem((clips, lane, local), BF16),
         ]
         + chain_scratch(rows, width)
+        + [vmem((HD, rows), F32)] * 3
         + [
+            vmem((rows, width), BF16),
+            vmem((hidden, span), BF16),
+            vmem((lane, span), BF16),
+            vmem((rows, width), BF16),
+            dma((6,)),
             dma((clips, ctx)),
             dma((clips, ctx)),
             dma((2, clips, ctx)),
@@ -1049,22 +1126,29 @@
             dma((11,)),
         ],
         2 * rows * width * (3 * lane + n * lane + 6 * hidden) + 4 * clips * length * length * HD,
+        held=6,
         kept=10,
     )
 
     held = (qkv, own, lse, grad_att, mlp, grads, x, summed, full_qkv, dr, n1)
     chain = chain_scratch(rows, width)
-    small, block_output, grad_input, shared, shared_qkv = call(
+    bqkv, bup, gains, shifts, sums, shard_qkv, shard_proj, shard_up, shard_down, block_output, grad_input = call(
         second_kernel,
         "second",
         1,
-        (*tables, norm_gains, out_shifts, stats, *held),
+        (positions, norm_gains, out_shifts, stats, *held),
         (
-            shape((8, width), F32),
+            shape((3, lane), F32),
+            shape((1, hidden), F32),
+            shape((2, width), F32),
+            shape((2, width), F32),
+            shape((2, width), F32),
+            shape((3, span, lane), BF16),
+            shape((lane, span), BF16),
+            shape((span, hidden), BF16),
+            shape((hidden, span), BF16),
             shape((rows, width), BF16),
             shape((rows, width), F32),
-            shape((ctx, piece, lanes), BF16),
-            shape((ctx, piece, 3 * lane), BF16),
         ),
         [vmem(item.shape, item.dtype) for item in held]
         + chain[1:]
@@ -1078,8 +1162,11 @@
             vmem((pieces // 2, 2, piece, 3 * lane), BF16),
             vmem((8, width), F32),
             vmem((pieces, 8, width), F32),
+            vmem((HD, rows), F32),
+            vmem((HD, rows), F32),
+            vmem((HD, rows), F32),
             dma((len(held),)),
-            dma((4,)),
+            dma((2,)),
             dma((clips, ctx)),
             dma((clips, ctx)),
             dma((2, pieces)),
@@ -1088,22 +1175,20 @@
         + gradient_scratch(pieces, ctx, piece, 3 * lane),
         4 * rows * width * 3 * lane + 10 * clips * length * length * HD,
         held=len(held),
-        kept=4,
+        kept=2,
     )
-    shared = shared.reshape(span, lanes)
-    shared_qkv = shared_qkv.reshape(span, 3, lane)
     return (
         block_output.reshape(clips, local, width),
         grad_input.reshape(clips, local, width),
-        shared_qkv.transpose(1, 0, 2).astype(F32),
-        small[7, : 3 * lane].reshape(3, lane),
-        shared[:, 2 * hidden :].T.astype(F32),
-        shared[:, :hidden].astype(F32),
-        small[6],
-        shared[:, hidden : 2 * hidden].T.astype(F32),
-        small[0:4:2],
-        small[1:4:2],
-        small[4:6],
+        shard_qkv.astype(F32),
+        bqkv,
+        shard_proj.astype(F32),
+        shard_up.astype(F32),
+        bup.reshape(hidden),
+        shard_down.astype(F32),
+        gains,
+        shifts,
+        sums,
     )
 
 

time: 339 us -> 301 us (0.89)
  Pallas kernels: 310 us -> 284 us
  local copies, waits for them, and re-layouts: 20 us -> 8.7 us
    pallas_call x2, Pallas kernels: 310 us -> 284 us  [call(): pl.pallas_call(kernel, name=name, out_shape=outs, in_specs=[VMEM] * (len(...]
    slice x5 -> x0, local copies, waits for them, and re-layouts: 6.2 us -> none  [the longest x1 1.37 us: shards(): small[1:4:2]]
    convert_element_type x2 -> x4, other arithmetic: 2.6 us -> 7.48 us  [the longest x1 2.41 us: shards(): shard_qkv.astype(F32)]
    unnamed x10 -> x25, local copies, waits for them, and re-layouts: 8.41 us -> 8.7 us
where the time goes in v4:
time: 301 us; the launch traced here: 300 us
  Pallas kernels  284 us (94%)
  local copies, waits for them, and re-layouts  8.7 us (3%)
  other arithmetic  7.48 us (2%)
    pallas_call x2, Pallas kernels, call(): pl.pallas_call(kernel, name=name, out_shape=outs, in_specs=[VMEM] * (len(...  284 us
    unnamed x25, local copies, waits for them, and re-layouts  8.7 us

profile of v4, /device:TPU:0, one launch (start us, length us, event | category | flops | bytes accessed | tf_op | source)
XLA Modules:
  0.0 300.4 jit_solution(7259847697108127370)
XLA Ops:
  0.6 140.3 %first.1 = (f32[8,1024]{1,0:T(8,128)}, bf16[1024,1024]{1,0:T(8,128)(2,1)}, bf16[2,3,64,2048]{3,2,1,0:T(8,128)(2,1)}, f32[2,64,2048]{2,1,0:T(8,128)}, f32[2,1,204...) custom-call(f32[3,256]{1,0:T(4,128)} %b_ref.1, ...), custom_call_target="tpu_custom_call" | custom-call | flops 18790481920 | bytes 27356160 | tf_op jit(solution)/shard_map/first/pallas_call | solution.py:1033
  140.9 143.2 %second.1 = (f32[3,256]{1,0:T(4,128)}, f32[1,1024]{1,0:T(1,128)}, f32[2,1024]{1,0:T(2,128)}, f32[2,1024]{1,0:T(2,128)}, f32[2,1024]{1,0:T(2,128)}, /*index=5*/bf...) custom-call(s32[3,2,512]{2,1,0:T(2,128)} %pos_ref.3, ...), custom_call_target="tpu_custom_call" | custom-call | flops 8589934592 | bytes 31566848 | tf_op jit(solution)/shard_map/second/pallas_call | solution.py:1033
  284.2 0.0 copy-start.3
  284.2 1.9 convert_element_type.13
  286.1 2.4 convert_element_type.12
  288.5 0.0 copy-done.3
  288.5 0.0 copy-start.2
  288.5 1.6 convert_element_type.14
  290.0 0.0 copy-done.2
  290.0 0.0 copy-start.1
  290.0 1.6 convert_element_type.15
  291.7 0.7 copy-done.1
  292.4 0.0 copy-start
  292.4 1.3 copy.30
  293.7 1.6 copy-done
  295.3 0.0 copy-start.8
  295.3 0.0 copy-start.7
  295.3 0.0 copy-start.6
  295.3 0.0 copy-start.5
  295.4 0.0 copy-start.4
  295.4 2.0 copy.31
  297.4 0.0 copy-done.8
  297.4 0.6 copy.32
  298.0 0.0 copy-done.7
  298.0 0.6 copy.33
  298.6 0.0 copy-done.6
  298.6 0.6 copy.34
  299.2 0.0 copy-done.5
  299.2 0.6 copy.35
  299.8 0.0 copy-done.4
  299.8 0.6 copy.36
Async XLA Ops:
  284.2 4.3 %copy-start.3 = (bf16[512,1024]{1,0:T(8,128)(2,1)S(1)}, bf16[512,1024]{1,0:T(8,128)(2,1)}, u32[]{:S(2)}) copy-start(bf16[512,1024]{1,0:T(8,128)(2,1)} %get-tuple-element.49) | copy-start | bytes 3145732
  288.5 1.6 copy-start.2
  290.0 2.3 copy-start.1
  292.4 2.9 copy-start
  295.3 2.0 copy-start.8
  295.3 2.6 copy-start.7
  295.3 3.2 %copy-start.6 = (f32[2,1024]{1,0:T(2,128)S(1)}, f32[2,1024]{1,0:T(2,128)}, u32[]{:S(2)}) copy-start(f32[2,1024]{1,0:T(2,128)} %get-tuple-element.74) | copy-start | bytes 24580
  295.3 3.8 %copy-start.5 = (f32[2,1024]{1,0:T(2,128)S(1)}, f32[2,1024]{1,0:T(2,128)}, u32[]{:S(2)}) copy-start(f32[2,1024]{1,0:T(2,128)} %get-tuple-element.75) | copy-start | bytes 24580
  295.4 4.4 %copy-start.4 = (f32[2,1024]{1,0:T(2,128)S(1)}, f32[2,1024]{1,0:T(2,128)}, u32[]{:S(2)}) copy-start(f32[2,1024]{1,0:T(2,128)} %get-tuple-element.76) | copy-start | bytes 24580

commit v5 on v4

--- a/solution.py
+++ b/solution.py
@@ -12,6 +12,7 @@
 EPSILON = 1e-06
 SCALE = HD ** (-0.5)
 QB = 256
+FINISH = 4
 LAG = 2
 CHUNK = 32
 ROWS = 128
@@ -389,11 +390,11 @@
     def keep(k, source, target):
         return pltpu.make_async_copy(source, target, keep_sem.at[k])
 
-    pieces = (w_any, up_any, proj_t, down_t)
-    wholes = (w_full, up_full, proj_full, down_full)
+    pieces = (*(w_any.at[c] for c in range(3)), up_any, proj_t, down_t)
+    wholes = (*(w_full.at[c] for c in range(3)), up_full, proj_full, down_full)
 
     def band(ref, start, size):
-        return ref.at[:, aligned(start, size)] if len(ref.shape) == 3 else ref.at[aligned(start, size)]
+        return ref.at[aligned(start, size)]
 
     def fetch(k, step):
         return remote(
@@ -464,8 +465,8 @@
                 def _():
                     link(way, block).wait_send()
 
-    fetch_all(0)
-    fetch_all(1)
+    for k in range(4):
+        fetch_all(k)
     load_proj.wait()
     n2[0:span, 0:lane] = proj_ref[...].T
     proj_t[aligned(odd * half, half), aligned(j * lane, lane)] = n2[aligned(odd * half, half), 0:lane]
@@ -481,26 +482,13 @@
         hat, _ = norm_parts(x_ref[rows, :].astype(F32))
         n1[rows, :] = (hat * gain_ref[0:1, :] + shift_ref[0:1, :]).astype(BF16)
 
-    for step in range(1, n - 1):
-        ring(row, step)
-    pass_on(0)
-    for step in range(n - 1, n):
-        ring(row, step)
-    fetch_all(2)
-    fetch_all(3)
-    other_half(0).start()
-    handed(0)
-    load_w.wait()
-    keep(0, w_full, w_out).start()
-    keep(1, n1, n1_out).start()
-
-    def outgoing(clip, step):
+    def outgoing(clip, c, step):
         peer = lax.rem(me + step, ctx)
         return remote(
-            send_buf.at[clip, :, aligned(peer * HD, HD), :],
-            qkv.at[clip, :, :, aligned(me * local, local)],
-            out_sem.at[clip, step],
-            in_sem.at[clip, step],
+            send_buf.at[clip, c, aligned(peer * HD, HD), :],
+            qkv.at[clip, c, :, aligned(me * local, local)],
+            out_sem.at[clip, c, step],
+            in_sem.at[clip, c, step],
             "ctx",
             peer,
         )
@@ -516,30 +504,41 @@
             peer,
         )
 
-    for clip in range(clips):
-
+    def project(clip, c):
         @pl.loop(0, blocks)
         def _(block):
             rows = aligned(clip * local + block * ROWS, ROWS)
-            lanes = aligned(block * ROWS, ROWS)
-            normed = n1[rows, :]
-            cos_t = jnp.concatenate([cos_ref[:, rows]] * heads, axis=0)
-            low_t = jnp.concatenate([low_ref[:, rows]] * heads, axis=0)
-            high_t = jnp.concatenate([high_ref[:, rows]] * heads, axis=0)
-            for c in range(3):
-                moved = (mm(normed, w_full[c], 1, 0) + b_ref[c : c + 1, :]).T
-                if c < 2:
-                    moved = turn(moved, cos_t, low_t, high_t, 1)
-                moved = moved.astype(BF16)
-                if c == 0:
-                    moved = moved * jnp.asarray(SCALE, BF16)
-                send_buf[clip, c, :, lanes] = moved
+            moved = (mm(n1[rows, :], w_full[c], 1, 0) + b_ref[c : c + 1, :]).T
+            if c < 2:
+                cos_t = jnp.concatenate([cos_ref[:, rows]] * heads, axis=0)
+                low_t = jnp.concatenate([low_ref[:, rows]] * heads, axis=0)
+                high_t = jnp.concatenate([high_ref[:, rows]] * heads, axis=0)
+                moved = turn(moved, cos_t, low_t, high_t, 1)
+            moved = moved.astype(BF16)
+            if c == 0:
+                moved = moved * jnp.asarray(SCALE, BF16)
+            send_buf[clip, c, :, aligned(block * ROWS, ROWS)] = moved
 
         for step in range(1, ctx):
-            outgoing(clip, step).start()
-        mine = aligned(me * local, local)
-        for c in range(3):
-            qkv[clip, c, :, mine] = send_buf[clip, c, aligned(me * HD, HD), :]
+            outgoing(clip, c, step).start()
+        qkv[clip, c, :, aligned(me * local, local)] = send_buf[clip, c, aligned(me * HD, HD), :]
+
+    load_w.wait()
+    for c in range(3):
+        pass_on(c)
+        handed(c)
+        project(0, c)
+        if c + 1 < n:
+            ring(row, c + 1)
+    for step in range(4, n):
+        ring(row, step)
+    fetch_all(4)
+    fetch_all(5)
+    other_half(0).start()
+    for c in range(3):
+        project(1, c)
+    keep(0, w_full, w_out).start()
+    keep(1, n1, n1_out).start()
 
     def heads_link(chunk):
         def link(way, block):
@@ -574,14 +573,14 @@
     down_full[own_rows, :] = down_t[...]
 
     for clip in range(clips):
-        for step in range(1, ctx):
-            outgoing(clip, step).wait_recv()
+        for c in range(3):
+            for step in range(1, ctx):
+                outgoing(clip, c, step).wait_recv()
         keys[...] = qkv[clip, 1].T
         if clip == 1:
-            pass_on(1)
             other_half(0).wait_recv()
             proj_full[own_rows, :] = proj_t[...]
-            pass_on(2)
+            pass_on(3)
 
         @pl.loop(0, length // QB)
         def _(block):
@@ -611,11 +610,11 @@
             returning(clip, step).start()
         att[clip, aligned(j * lane + me * HD, HD), :] = back_buf[clip, :, aligned(me * local, local)]
     ring_step(-2)
+    pass_on(4)
     send_heads(1)
-    pass_on(3)
     ring_step(-1)
-    for k in (1, 2, 3):
-        handed(k)
+    handed(3)
+    handed(4)
     keep(2, qkv, qkv_out).start()
     keep(3, own, own_out).start()
     keep(4, lse, lse_out).start()
@@ -645,7 +644,8 @@
         grad_land[clip, :, aligned(me * local, local)] = grad_send[clip, aligned(me * HD, HD), :]
         keep(7 + clip, dr.at[pl.ds(clip * local, local)], dr_out.at[pl.ds(clip * local, local)]).start()
 
-    lag = 1 + pl.cdiv(chain.hops, many)
+    late = slope_buf.shape[0] - 1
+    lag = late + 1 + pl.cdiv(chain.hops, many)
 
     @pl.loop(0, chunks + lag)
     def _(step):
@@ -653,8 +653,16 @@
         rows = aligned(k * ROWS, ROWS)
         busy = k < chunks
         pl.when(busy)(lambda: ring_step(step))
-        at = (step - 1) * many
+        at = (step - late - 1) * many
         chain.step(at)
+
+        @pl.when(step == late - 1)
+        def _():
+            pass_on(5)
+
+        @pl.when(step == late)
+        def _():
+            handed(5)
 
         @pl.when(busy)
         def _():
@@ -666,14 +674,18 @@
             pre = mm(normed, up_full[...], 1, 0) + bup_ref[...]
             cdf = 0.5 + 0.5 * lax.erf(pre * (0.5**0.5))
             act[rows, :] = (pre * cdf).astype(BF16)
-            slope_buf[...] = cdf + pre * (jnp.exp(-0.5 * pre * pre) * 0.3989422804014327)
+            slope_buf[lax.rem(k, late + 1)] = cdf + pre * (jnp.exp(-0.5 * pre * pre) * 0.3989422804014327)
 
         for more in range(1, many):
             chain.step(at + more)
 
-        @pl.when(busy)
+        back = step - late
+
+        @pl.when((back >= 0) & (back < chunks))
         def _():
-            grad = (mm(g_ref[rows, :], down_full[...], 1, 0) * slope_buf[...]).astype(BF16)
+            rows = aligned(back * ROWS, ROWS)
+            slope = slope_buf[lax.rem(back, late + 1)]
+            grad = (mm(g_ref[rows, :], down_full[...], 1, 0) * slope).astype(BF16)
             dz[rows, :] = grad
             part[rows, :] = mm(grad, up_full[...], 1, 1).astype(BF16)
             mlp[rows, :] = mm(act[rows, :], down_full[...], 1, 1).astype(BF16)
@@ -699,12 +711,12 @@
         def _():
             give_all(0)
 
-        @pl.when(step == chunks)
+        @pl.when(step == chunks + late)
         def _():
             keep(5, mlp, mlp_out).start()
             keep(6, summed, sum_out).start()
 
-        unit = step - chunks
+        unit = step - chunks - late
 
         @pl.when((unit >= 0) & (unit * 2 < width // ROWS))
         def _():
@@ -743,10 +755,11 @@
 
     for clip in range(clips):
         for step in range(1, ctx):
-            outgoing(clip, step).wait_send()
+            for c in range(3):
+                outgoing(clip, c, step).wait_send()
             returning(clip, step).wait_send()
             give(clip, step).wait_send()
-    for k in range(4):
+    for k in range(6):
         for step in range(1, fsdp):
             fetch(k, step).wait_send()
             hand(k, step).wait_send()
@@ -789,7 +802,7 @@
             )
         )
     ]
-    for load in loads:
+    for load in loads[:5]:
         load.start()
     weights = GradientSum(weights_ref, *sum_refs[:7])
     weights_qkv = GradientSum(grads_qkv, *sum_refs[7:])
@@ -800,6 +813,8 @@
     greet_grid("tp")
     for k in range(5):
         loads[k].wait()
+    for load in loads[5:]:
+        load.start()
     small[...] = stats_ref[...]
 
     def outgoing(clip, step):
@@ -876,10 +891,8 @@
         def _(block):
             at = clip * blocks + block
 
-            @pl.when(lax.rem(at, 2) == 0)
-            def _():
-                first.step(at // 2)
-                finish(at // 2 - hops)
+            first.step(at)
+            finish(at - hops)
 
             if clip == 0:
                 pl.when(block == 1)(weights.sum_pair)
@@ -902,8 +915,8 @@
         for c in range(3):
             moved[clip, c, aligned(me * HD, HD), :] = send_buf[clip, c, :, aligned(me * local, local)]
 
-    done = clips * blocks // 2
-    early = done + 3
+    done = clips * blocks
+    early = done + 1
     total = count + hops
     split = count // clips // 2
     units = width // ROWS
@@ -914,6 +927,16 @@
         finish(step - hops)
 
     unturn(0)
+
+    def write_shards():
+        rows = weights.shared.shape[1]
+        hidden = up_out.shape[1]
+        weights.wait_share()
+        for c in range(ctx):
+            at = pl.ds(c * rows, rows)
+            up_out[at, :] = weights.shared[c, :, 0:hidden]
+        down_out[...] = weights.shared[:, :, hidden : 2 * hidden].reshape(ctx * rows, hidden).T
+        proj_out[...] = weights.shared[:, :, 2 * hidden :].reshape(ctx * rows, lane).T
 
     def both(step):
         last.step(step)
@@ -948,6 +971,7 @@
 
         for place, act in (
             (2, weights.pass_share),
+            (8, write_shards),
             (4, weights_qkv.start_pair),
             (5, weights_qkv.sum_pair),
             (6, weights_qkv.start_cross),
@@ -979,15 +1003,8 @@
     keeps[0].start()
     keeps[1].start()
     small_land[rank] = small[...]
-    rows = weights.shared.shape[1]
-    hidden = up_out.shape[1]
-    weights.wait_share()
-    for c in range(ctx):
-        at = pl.ds(c * rows, rows)
-        up_out[at, :] = weights.shared[c, :, 0:hidden]
-    down_out[...] = weights.shared[:, :, hidden : 2 * hidden].reshape(ctx * rows, hidden).T
-    proj_out[...] = weights.shared[:, :, 2 * hidden :].reshape(ctx * rows, lane).T
     weights_qkv.wait_share()
+    rows = weights_qkv.shared.shape[1]
     for i in range(ctx):
         at = pl.ds(i * rows, rows)
         for c in range(3):
@@ -1042,6 +1059,30 @@
             collective_id=number, has_side_effects=True, vmem_limit_bytes=63 * 1024 * 1024
         ),
     )(*ins)
+
+
+def finish_kernel(*refs):
+    half = len(refs) // 2
+    for source, target in zip(refs[:half], refs[half:]):
+        target[...] = source[...].astype(target.dtype)
+
+
+def finish(results, dtypes, cuts, steps):
+    def spec(shape, cut):
+        if cut is None:
+            return pl.BlockSpec(shape, lambda i: (0,) * len(shape))
+        block = tuple(size // steps if axis == cut else size for axis, size in enumerate(shape))
+        return pl.BlockSpec(block, lambda i: tuple(i if axis == cut else 0 for axis in range(len(shape))))
+
+    specs = [spec(item.shape, cut) for item, cut in zip(results, cuts)]
+    return pl.pallas_call(
+        finish_kernel,
+        name="finish",
+        grid=(steps,),
+        in_specs=specs,
+        out_specs=specs,
+        out_shape=[jax.ShapeDtypeStruct(item.shape, kind) for item, kind in zip(results, dtypes)],
+    )(*results)
 
 
 def shards(
@@ -1104,7 +1145,7 @@
             vmem((rows, hidden), BF16),
             vmem((rows, hidden), BF16),
             vmem((rows, width), BF16),
-            vmem((ROWS, hidden), F32),
+            vmem((2, ROWS, hidden), F32),
             vmem((clips, lane, local), BF16),
         ]
         + chain_scratch(rows, width)
@@ -1115,11 +1156,11 @@
             vmem((lane, span), BF16),
             vmem((rows, width), BF16),
             dma((6,)),
-            dma((clips, ctx)),
-            dma((clips, ctx)),
+            dma((clips, 3, ctx)),
+            dma((clips, 3, ctx)),
             dma((2, clips, ctx)),
-            dma((2, 4, fsdp)),
-            dma((2, 4, fsdp)),
+            dma((2, 6, fsdp)),
+            dma((2, 6, fsdp)),
             dma((2, 3, n)),
             dma((2, 2, n, chunks)),
             dma((2, clips, ctx)),
@@ -1132,7 +1173,7 @@
 
     held = (qkv, own, lse, grad_att, mlp, grads, x, summed, full_qkv, dr, n1)
     chain = chain_scratch(rows, width)
-    bqkv, bup, gains, shifts, sums, shard_qkv, shard_proj, shard_up, shard_down, block_output, grad_input = call(
+    results = call(
         second_kernel,
         "second",
         1,
@@ -1177,15 +1218,18 @@
         held=len(held),
         kept=2,
     )
+    bqkv, bup, gains, shifts, sums, shard_qkv, shard_proj, shard_up, shard_down, block_output, grad_input = finish(
+        results, (F32,) * 9 + (BF16, F32), (None,) * 5 + (1, 0, 0, 0, 0, 0), FINISH
+    )
     return (
         block_output.reshape(clips, local, width),
         grad_input.reshape(clips, local, width),
-        shard_qkv.astype(F32),
+        shard_qkv,
         bqkv,
-        shard_proj.astype(F32),
-        shard_up.astype(F32),
+        shard_proj,
+        shard_up,
         bup.reshape(hidden),
-        shard_down.astype(F32),
+        shard_down,
         gains,
         shifts,
         sums,

time: 301 us -> 281 us (0.934)
  local copies, waits for them, and re-layouts: 8.7 us -> 0 us
  other arithmetic: 7.48 us -> 0 us
  Pallas kernels: 284 us -> 280 us
    pallas_call x2, Pallas kernels: 284 us -> 272 us  [call(): pl.pallas_call(kernel, name=name, out_shape=outs, in_specs=[VMEM] * (len(...]
    unnamed x25 -> x0, local copies, waits for them, and re-layouts: 8.7 us -> none
    pallas_call x0 -> x1, Pallas kernels: none -> 8.4 us  [finish(): pl.pallas_call(finish_kernel, name='finish', grid=(steps,), in_specs=spec...]
    convert_element_type x4 -> x0, other arithmetic: 7.48 us -> none  [the longest x1 2.41 us: shards(): shard_qkv.astype(F32)]
where the time goes in v5:
time: 281 us
  Pallas kernels  280 us (100%)
    pallas_call x2, Pallas kernels, call(): pl.pallas_call(kernel, name=name, out_shape=outs, in_specs=[VMEM] * (len(...  272 us
    pallas_call x1, Pallas kernels, finish(): pl.pallas_call(finish_kernel, name='finish', grid=(steps,), in_specs=spec...  8.4 us

profile of v5, /device:TPU:0, one launch (start us, length us, event | category | flops | bytes accessed | tf_op | source)
XLA Modules:
  0.0 280.9 jit_solution(8410534289703624987)
XLA Ops:
  0.6 139.8 %first.1 = (f32[8,1024]{1,0:T(8,128)}, bf16[1024,1024]{1,0:T(8,128)(2,1)}, bf16[2,3,64,2048]{3,2,1,0:T(8,128)(2,1)}, f32[2,64,2048]{2,1,0:T(8,128)}, f32[2,1,204...) custom-call(f32[3,256]{1,0:T(4,128)} %b_ref.1, ...), custom_call_target="tpu_custom_call" | custom-call | flops 18790481920 | bytes 27356160 | tf_op jit(solution)/shard_map/first/pallas_call | solution.py:1050
  140.5 131.9 %second.1 = (f32[3,256]{1,0:T(4,128)}, f32[1,1024]{1,0:T(1,128)}, f32[2,1024]{1,0:T(2,128)}, f32[2,1024]{1,0:T(2,128)}, f32[2,1024]{1,0:T(2,128)}, /*index=5*/bf...) custom-call(s32[3,2,512]{2,1,0:T(2,128)} %pos_ref.3, ...), custom_call_target="tpu_custom_call" | custom-call | flops 8589934592 | bytes 31566848 | tf_op jit(solution)/shard_map/second/pallas_call | solution.py:1050
  272.3 8.4 %finish.1 = (f32[3,256]{1,0:T(4,128)}, f32[1,1024]{1,0:T(1,128)}, f32[2,1024]{1,0:T(2,128)}, f32[2,1024]{1,0:T(2,128)}, f32[2,1024]{1,0:T(2,128)}, /*index=5*/f3...) custom-call(f32[3,256]{1,0:T(4,128)} %get-tuple-element.55.refs_0_, ...), custom_call_target="tpu_custom_call" | custom-call | tf_op jit(solution)/shard_map/finish/pallas_call | solution.py:1078

commit v6 on v5

--- a/solution.py
+++ b/solution.py
@@ -139,83 +139,110 @@
     def __init__(self, part, landed, full, sems):
         self.part, self.landed, self.full, self.sems = part, landed, full, sems
         self.n, self.j = lax.axis_size("tp"), lax.axis_index("tp")
+        self.root = self.n - 2
         self.count = part.shape[0] // 2 // CHUNK
-        self.hops = 2 * (self.n - 1) * LAG
+        self.hops = 2 * self.root * LAG
 
     def pos(self, way):
         return (self.n - 1 - self.j) if way == 0 else self.j
 
+    def link(self, way, i, kind, source, target, onward):
+        rows = chain_rows(way, i)
+        up = onward if way == 1 else not onward
+        return remote(
+            source.at[rows], target.at[rows],
+            self.sems.at[8 * way + 2 * kind, i], self.sems.at[8 * way + 2 * kind + 1, i],
+            "tp", self.j + 1 if up else self.j - 1,
+        )
+
     def sums(self, way, i):
-        rows = chain_rows(way, i)
-        return remote(
-            self.part.at[rows], self.landed.at[rows],
-            self.sems.at[4 * way, i], self.sems.at[4 * way + 1, i],
-            "tp", self.j - 1 if way == 0 else self.j + 1,
-        )
+        return self.link(way, i, 0, self.part, self.landed, True)
 
     def totals(self, way, i):
-        rows = chain_rows(way, i)
-        return remote(
-            self.full.at[rows], self.full.at[rows],
-            self.sems.at[4 * way + 2, i], self.sems.at[4 * way + 3, i],
-            "tp", self.j + 1 if way == 0 else self.j - 1,
-        )
-
-    def added(self, way, i):
-        rows = chain_rows(way, i)
-        return (self.part[rows, :].astype(F32) + self.landed[rows, :].astype(F32)).astype(BF16)
+        return self.link(way, i, 1, self.full, self.full, False)
+
+    def near(self, way, i):
+        return self.link(way, i, 2, self.part, self.full, False)
+
+    def near_totals(self, way, i):
+        return self.link(way, i, 3, self.full, self.full, True)
 
     def step(self, step):
-        n, count = self.n, self.count
+        root, count = self.root, self.count
         for way in (0, 1):
             pos = self.pos(way)
-            i = step - pos * LAG
+            i = step - jnp.where(pos > root, root - 1, pos) * LAG
 
             @pl.when((i >= 0) & (i < count))
             def _():
+                rows = chain_rows(way, i)
+
                 @pl.when(pos == 0)
                 def _():
                     self.sums(way, i).start()
 
-                @pl.when((pos > 0) & (pos < n - 1))
+                @pl.when((pos > 0) & (pos < root))
                 def _():
                     self.sums(way, i).wait_recv()
-                    self.part[chain_rows(way, i), :] = self.added(way, i)
+                    value = self.part[rows, :].astype(F32) + self.landed[rows, :].astype(F32)
+                    self.part[rows, :] = value.astype(BF16)
                     self.sums(way, i).start()
 
-                @pl.when(pos == n - 1)
-                def _():
+                @pl.when(pos == root + 1)
+                def _():
+                    self.near(way, i).start()
+
+                @pl.when(pos == root)
+                def _():
+                    self.near(way, i).wait_recv()
                     self.sums(way, i).wait_recv()
-                    self.full[chain_rows(way, i), :] = self.added(way, i)
+                    value = self.part[rows, :].astype(F32) + self.landed[rows, :].astype(F32)
+                    self.full[rows, :] = (value + self.full[rows, :].astype(F32)).astype(BF16)
                     self.totals(way, i).start()
-
-            k = step - (2 * (n - 1) - pos) * LAG
-
-            @pl.when((k >= 0) & (k < count) & (pos < n - 1))
+                    self.near_totals(way, i).start()
+
+            k = step - jnp.where(pos > root, root + 1, 2 * root - pos) * LAG
+
+            @pl.when((k >= 0) & (k < count))
             def _():
-                self.totals(way, k).wait_recv()
-
-                @pl.when(pos > 0)
+                @pl.when(pos < root)
+                def _():
+                    self.totals(way, k).wait_recv()
+
+                @pl.when((pos > 0) & (pos < root))
                 def _():
                     self.totals(way, k).start()
 
+                @pl.when(pos == root + 1)
+                def _():
+                    self.near_totals(way, k).wait_recv()
+
     def drain(self):
+        root = self.root
         for way in (0, 1):
             pos = self.pos(way)
 
             @pl.loop(0, self.count)
             def _(i):
-                @pl.when(pos < self.n - 1)
+                @pl.when(pos < root)
                 def _():
                     self.sums(way, i).wait_send()
 
-                @pl.when(pos > 0)
+                @pl.when((pos > 0) & (pos <= root))
                 def _():
                     self.totals(way, i).wait_send()
 
+                @pl.when(pos == root + 1)
+                def _():
+                    self.near(way, i).wait_send()
+
+                @pl.when(pos == root)
+                def _():
+                    self.near_totals(way, i).wait_send()
+
 
 def chain_scratch(rows, width):
-    return [pltpu.VMEM((rows, width), BF16)] * 3 + [pltpu.SemaphoreType.DMA((8, rows // 2 // CHUNK))]
+    return [pltpu.VMEM((rows, width), BF16)] * 3 + [pltpu.SemaphoreType.DMA((16, rows // 2 // CHUNK))]
 
 
 class GradientSum:
@@ -792,6 +819,8 @@
     blocks = length // QB
     pieces = lax.axis_size("fsdp") * ctx
     rank = lax.axis_index("fsdp") * ctx + me
+    former = pl.ds(0, x_ref.shape[0] // 2)
+    latter = pl.ds(x_ref.shape[0] // 2, x_ref.shape[0] // 2)
     loads = [
         pltpu.make_async_copy(source, target, load_sem.at[k])
         for k, (source, target) in enumerate(
@@ -802,19 +831,24 @@
             )
         )
     ]
-    for load in loads[:5]:
-        load.start()
+    for k in (4, 5, 0, 3, 1, 2):
+        loads[k].start()
     weights = GradientSum(weights_ref, *sum_refs[:7])
     weights_qkv = GradientSum(grads_qkv, *sum_refs[7:])
     first = Chain(part, landed, full, sem)
     last = Chain(part_b, landed_b, full_b, sem_b)
     count, hops = first.count, first.hops
-    fill_tables(pos_ref, cos_ref, low_ref, high_ref)
     greet_grid("tp")
-    for k in range(5):
+    loads[4].wait()
+    first.step(0)
+    loads[5].wait()
+    weights.start_pair()
+    for k in range(4):
         loads[k].wait()
-    for load in loads[5:]:
+    for load in loads[6:]:
         load.start()
+    first.step(1)
+    ahead = 2
     small[...] = stats_ref[...]
 
     def outgoing(clip, step):
@@ -881,18 +915,22 @@
         grads[...] = grad_ref[clip].T
         acc_k[...] = jnp.zeros_like(acc_k)
         acc_v[...] = jnp.zeros_like(acc_v)
-        if clip == 0:
-            loads[5].wait()
-            weights.start_pair()
-            for k in range(6, len(loads)):
-                loads[k].wait()
+        if clip == 1:
+            fill_tables(pos_ref, cos_ref, low_ref, high_ref)
 
         @pl.loop(0, blocks)
         def _(block):
             at = clip * blocks + block
 
-            first.step(at)
-            finish(at - hops)
+            first.step(at + ahead)
+            if clip == 0:
+
+                @pl.when(block == 3)
+                def _():
+                    for load in loads[6:]:
+                        load.wait()
+
+            finish(at + ahead - hops)
 
             if clip == 0:
                 pl.when(block == 1)(weights.sum_pair)
@@ -915,7 +953,7 @@
         for c in range(3):
             moved[clip, c, aligned(me * HD, HD), :] = send_buf[clip, c, :, aligned(me * local, local)]
 
-    done = clips * blocks
+    done = clips * blocks + ahead
     early = done + 1
     total = count + hops
     split = count // clips // 2
@@ -938,7 +976,19 @@
         down_out[...] = weights.shared[:, :, hidden : 2 * hidden].reshape(ctx * rows, hidden).T
         proj_out[...] = weights.shared[:, :, 2 * hidden :].reshape(ctx * rows, lane).T
 
+    keeps = [
+        pltpu.make_async_copy(source, target, keep_sem.at[k])
+        for k, (source, target) in enumerate(
+            (
+                (dr_ref.at[former], grad_in_out.at[former]),
+                (dr_ref.at[latter], grad_in_out.at[latter]),
+                (sum_ref, block_out),
+            )
+        )
+    ]
+
     def both(step):
+        pl.when(step == hops + count // 2)(keeps[0].start)
         last.step(step)
         close(step - hops)
         other = (step * (total - early)) // total
@@ -960,11 +1010,11 @@
     def _(step):
         both(step)
 
-        @pl.when(step - split < 4)
+        @pl.when(step - split < 2)
         def _():
-            @pl.loop(0, units // 4)
+            @pl.loop(0, units // 2)
             def _(more):
-                unit = (step - split) * (units // 4) + more
+                unit = (step - split) * (units // 2) + more
                 normed = n1_ref[:, aligned(unit * ROWS, ROWS)]
                 for c in range(3):
                     put_pieces(grads_qkv, unit, pl.ds(c * lane, lane), mm(normed, dp_ref[c], 0, 0))
@@ -972,12 +1022,12 @@
         for place, act in (
             (2, weights.pass_share),
             (8, write_shards),
-            (4, weights_qkv.start_pair),
-            (5, weights_qkv.sum_pair),
-            (6, weights_qkv.start_cross),
-            (9, weights_qkv.sum_cross),
-            (10, weights_qkv.start_share),
-            (13, weights_qkv.pass_share),
+            (2, weights_qkv.start_pair),
+            (4, weights_qkv.sum_pair),
+            (4, weights_qkv.start_cross),
+            (7, weights_qkv.sum_cross),
+            (7, weights_qkv.start_share),
+            (10, weights_qkv.pass_share),
         ):
             pl.when(step == split + place)(act)
 
@@ -991,17 +1041,8 @@
     def _(step):
         spread(step).start()
 
-    keeps = [
-        pltpu.make_async_copy(source, target, keep_sem.at[k])
-        for k, (source, target) in enumerate(
-            (
-                (dr_ref, grad_in_out),
-                (sum_ref, block_out),
-            )
-        )
-    ]
-    keeps[0].start()
     keeps[1].start()
+    keeps[2].start()
     small_land[rank] = small[...]
     weights_qkv.wait_share()
     rows = weights_qkv.shared.shape[1]
@@ -1207,7 +1248,7 @@
             vmem((HD, rows), F32),
             vmem((HD, rows), F32),
             dma((len(held),)),
-            dma((2,)),
+            dma((3,)),
             dma((clips, ctx)),
             dma((clips, ctx)),
             dma((2, pieces)),

time: 281 us -> 272 us (0.968)
  Pallas kernels: 280 us -> 271 us
    pallas_call x2, Pallas kernels: 272 us -> 263 us  [call(): pl.pallas_call(kernel, name=name, out_shape=outs, in_specs=[VMEM] * (len(...]
where the time goes in v6:
time: 272 us
  Pallas kernels  271 us (100%)
    pallas_call x2, Pallas kernels, call(): pl.pallas_call(kernel, name=name, out_shape=outs, in_specs=[VMEM] * (len(...  263 us
    pallas_call x1, Pallas kernels, finish(): pl.pallas_call(finish_kernel, name='finish', grid=(steps,), in_specs=spec...  8.4 us

profile of v6, /device:TPU:0, one launch (start us, length us, event | category | flops | bytes accessed | tf_op | source)
XLA Modules:
  0.0 272.1 jit_solution(16026214190247953320)
XLA Ops:
  0.6 137.9 %first.1 = (f32[8,1024]{1,0:T(8,128)}, bf16[1024,1024]{1,0:T(8,128)(2,1)}, bf16[2,3,64,2048]{3,2,1,0:T(8,128)(2,1)}, f32[2,64,2048]{2,1,0:T(8,128)}, f32[2,1,204...) custom-call(f32[3,256]{1,0:T(4,128)} %b_ref.1, ...), custom_call_target="tpu_custom_call" | custom-call | flops 18790481920 | bytes 27356160 | tf_op jit(solution)/shard_map/first/pallas_call | solution.py:1091
  138.6 124.9 %second.1 = (f32[3,256]{1,0:T(4,128)}, f32[1,1024]{1,0:T(1,128)}, f32[2,1024]{1,0:T(2,128)}, f32[2,1024]{1,0:T(2,128)}, f32[2,1024]{1,0:T(2,128)}, /*index=5*/bf...) custom-call(s32[3,2,512]{2,1,0:T(2,128)} %pos_ref.3, ...), custom_call_target="tpu_custom_call" | custom-call | flops 8589934592 | bytes 31566848 | tf_op jit(solution)/shard_map/second/pallas_call | solution.py:1091
  263.5 8.4 %finish.1 = (f32[3,256]{1,0:T(4,128)}, f32[1,1024]{1,0:T(1,128)}, f32[2,1024]{1,0:T(2,128)}, f32[2,1024]{1,0:T(2,128)}, f32[2,1024]{1,0:T(2,128)}, /*index=5*/f3...) custom-call(f32[3,256]{1,0:T(4,128)} %get-tuple-element.55.refs_0_, ...), custom_call_target="tpu_custom_call" | custom-call | tf_op jit(solution)/shard_map/finish/pallas_call | solution.py:1119

commit v7 on v6

--- a/solution.py
+++ b/solution.py
@@ -12,7 +12,7 @@
 EPSILON = 1e-06
 SCALE = HD ** (-0.5)
 QB = 256
-FINISH = 4
+FINISH = 2
 LAG = 2
 CHUNK = 32
 ROWS = 128
@@ -661,11 +661,6 @@
         )
 
     def give_all(clip):
-        @pl.loop(0, blocks)
-        def _(block):
-            value = mm(drb[aligned(clip * local + block * ROWS, ROWS), :], proj_full[:, aligned(j * lane, lane)], 1, 0)
-            grad_send[clip, :, aligned(block * ROWS, ROWS)] = value.T.astype(BF16)
-
         for step in range(1, ctx):
             give(clip, step).start()
         grad_land[clip, :, aligned(me * local, local)] = grad_send[clip, aligned(me * HD, HD), :]
@@ -728,7 +723,10 @@
             upstream = g_ref[rows, :].astype(F32)
             moved = upstream + norm_pull(hat, rstd, gain_ref[1:2, :], grad)
             dr[rows, :] = moved
-            drb[rows, :] = moved.astype(BF16)
+            low = moved.astype(BF16)
+            drb[rows, :] = low
+            value = mm(low, proj_full[:, aligned(j * lane, lane)], 1, 0)
+            grad_send[done // blocks, :, aligned(lax.rem(done, blocks) * ROWS, ROWS)] = value.T.astype(BF16)
             stats_ref[2:3, :] += jnp.sum(grad * hat, axis=0, keepdims=True)
             stats_ref[3:4, :] += jnp.sum(grad, axis=0, keepdims=True)
             stats_ref[4:5, :] += jnp.sum(moved, axis=0, keepdims=True)
@@ -956,7 +954,7 @@
     done = clips * blocks + ahead
     early = done + 1
     total = count + hops
-    split = count // clips // 2
+    split = count // clips
     units = width // ROWS
 
     @pl.loop(done, early)

time: 272 us -> 266 us (0.978)
  Pallas kernels: 271 us -> 265 us
    pallas_call x2, Pallas kernels: 263 us -> 257 us  [call(): pl.pallas_call(kernel, name=name, out_shape=outs, in_specs=[VMEM] * (len(...]
where the time goes in v7:
time: 266 us
  Pallas kernels  265 us (100%)
    pallas_call x2, Pallas kernels, call(): pl.pallas_call(kernel, name=name, out_shape=outs, in_specs=[VMEM] * (len(...  257 us
    pallas_call x1, Pallas kernels, finish(): pl.pallas_call(finish_kernel, name='finish', grid=(steps,), in_specs=spec...  7.51 us

profile of v7, /device:TPU:0, one launch (start us, length us, event | category | flops | bytes accessed | tf_op | source)
XLA Modules:
  0.0 265.7 jit_solution(15510928154895243248)
XLA Ops:
  0.6 136.7 %first.1 = (f32[8,1024]{1,0:T(8,128)}, bf16[1024,1024]{1,0:T(8,128)(2,1)}, bf16[2,3,64,2048]{3,2,1,0:T(8,128)(2,1)}, f32[2,64,2048]{2,1,0:T(8,128)}, f32[2,1,204...) custom-call(f32[3,256]{1,0:T(4,128)} %b_ref.1, ...), custom_call_target="tpu_custom_call" | custom-call | flops 18790481920 | bytes 27356160 | tf_op jit(solution)/shard_map/first/pallas_call | solution.py:1089
  137.3 120.7 %second.1 = (f32[3,256]{1,0:T(4,128)}, f32[1,1024]{1,0:T(1,128)}, f32[2,1024]{1,0:T(2,128)}, f32[2,1024]{1,0:T(2,128)}, f32[2,1024]{1,0:T(2,128)}, /*index=5*/bf...) custom-call(s32[3,2,512]{2,1,0:T(2,128)} %pos_ref.3, ...), custom_call_target="tpu_custom_call" | custom-call | flops 8589934592 | bytes 31566848 | tf_op jit(solution)/shard_map/second/pallas_call | solution.py:1089
  258.0 7.5 %finish.1 = (f32[3,256]{1,0:T(4,128)}, f32[1,1024]{1,0:T(1,128)}, f32[2,1024]{1,0:T(2,128)}, f32[2,1024]{1,0:T(2,128)}, f32[2,1024]{1,0:T(2,128)}, /*index=5*/f3...) custom-call(f32[3,256]{1,0:T(4,128)} %get-tuple-element.55.refs_0_, ...), custom_call_target="tpu_custom_call" | custom-call | tf_op jit(solution)/shard_map/finish/pallas_call | solution.py:1117

commit v8 on v7

--- a/solution.py
+++ b/solution.py
@@ -152,7 +152,7 @@
         return remote(
             source.at[rows], target.at[rows],
             self.sems.at[8 * way + 2 * kind, i], self.sems.at[8 * way + 2 * kind + 1, i],
-            "tp", self.j + 1 if up else self.j - 1,
+            "tp", lax.rem(self.j + (1 if up else self.n - 1), self.n),
         )
 
     def sums(self, way, i):
@@ -461,7 +461,7 @@
         view = proj_t.at[aligned(odd * half, half), aligned(block * lane, lane)]
         return remote(
             view, view, row_sem.at[0, way, block], row_sem.at[1, way, block],
-            "tp", j + 1 if way == 0 else j - 1,
+            "tp", lax.rem(j + (1 if way == 0 else n - 1), n),
         )
 
     def other_half(step):
@@ -572,7 +572,7 @@
             view = att.at[chunk // blocks, aligned(block * lane, lane), aligned(lax.rem(chunk, blocks) * ROWS, ROWS)]
             return remote(
                 view, view, gather_sem.at[0, way, block, chunk], gather_sem.at[1, way, block, chunk],
-                "tp", j + 1 if way == 0 else j - 1,
+                "tp", lax.rem(j + (1 if way == 0 else n - 1), n),
             )
 
         return link
@@ -999,8 +999,8 @@
     @pl.loop(0, split)
     def _(step):
         both(step)
-        pl.when(step == 1)(weights.sum_cross)
-        pl.when(step == 2)(weights.start_share)
+        pl.when(step == 3)(weights.sum_cross)
+        pl.when(step == 4)(weights.start_share)
 
     unturn(1)
 

time: 266 us -> 266 us (level)
  no operation moved by 1% of the time
where the time goes in v8:
time: 266 us
  Pallas kernels  265 us (100%)
    pallas_call x2, Pallas kernels, call(): pl.pallas_call(kernel, name=name, out_shape=outs, in_specs=[VMEM] * (len(...  257 us
    pallas_call x1, Pallas kernels, finish(): pl.pallas_call(finish_kernel, name='finish', grid=(steps,), in_specs=spec...  7.51 us

profile of v8, /device:TPU:0, one launch (start us, length us, event | category | flops | bytes accessed | tf_op | source)
XLA Modules:
  0.0 265.8 jit_solution(2469329877728747687)
XLA Ops:
  0.6 136.7 %first.1 = (f32[8,1024]{1,0:T(8,128)}, bf16[1024,1024]{1,0:T(8,128)(2,1)}, bf16[2,3,64,2048]{3,2,1,0:T(8,128)(2,1)}, f32[2,64,2048]{2,1,0:T(8,128)}, f32[2,1,204...) custom-call(f32[3,256]{1,0:T(4,128)} %b_ref.1, ...), custom_call_target="tpu_custom_call" | custom-call | flops 18790481920 | bytes 27356160 | tf_op jit(solution)/shard_map/first/pallas_call | solution.py:1089
  137.3 120.8 %second.1 = (f32[3,256]{1,0:T(4,128)}, f32[1,1024]{1,0:T(1,128)}, f32[2,1024]{1,0:T(2,128)}, f32[2,1024]{1,0:T(2,128)}, f32[2,1024]{1,0:T(2,128)}, /*index=5*/bf...) custom-call(s32[3,2,512]{2,1,0:T(2,128)} %pos_ref.3, ...), custom_call_target="tpu_custom_call" | custom-call | flops 8589934592 | bytes 31566848 | tf_op jit(solution)/shard_map/second/pallas_call | solution.py:1089
  258.1 7.5 %finish.1 = (f32[3,256]{1,0:T(4,128)}, f32[1,1024]{1,0:T(1,128)}, f32[2,1024]{1,0:T(2,128)}, f32[2,1024]{1,0:T(2,128)}, f32[2,1024]{1,0:T(2,128)}, /*index=5*/f3...) custom-call(f32[3,256]{1,0:T(4,128)} %get-tuple-element.55.refs_0_, ...), custom_call_target="tpu_custom_call" | custom-call | tf_op jit(solution)/shard_map/finish/pallas_call | solution.py:1117

commit v9 on v8

--- a/solution.py
+++ b/solution.py
@@ -952,7 +952,7 @@
             moved[clip, c, aligned(me * HD, HD), :] = send_buf[clip, c, :, aligned(me * local, local)]
 
     done = clips * blocks + ahead
-    early = done + 1
+    early = done
     total = count + hops
     split = count // clips
     units = width // ROWS

time: 266 us -> 266 us (level)
  no operation moved by 1% of the time
where the time goes in v9:
time: 266 us
  Pallas kernels  265 us (100%)
    pallas_call x2, Pallas kernels, call(): pl.pallas_call(kernel, name=name, out_shape=outs, in_specs=[VMEM] * (len(...  258 us
    pallas_call x1, Pallas kernels, finish(): pl.pallas_call(finish_kernel, name='finish', grid=(steps,), in_specs=spec...  7.51 us

profile of v9, /device:TPU:0, one launch (start us, length us, event | category | flops | bytes accessed | tf_op | source)
XLA Modules:
  0.0 265.9 jit_solution(13426399212875500626)
XLA Ops:
  0.6 136.7 %first.1 = (f32[8,1024]{1,0:T(8,128)}, bf16[1024,1024]{1,0:T(8,128)(2,1)}, bf16[2,3,64,2048]{3,2,1,0:T(8,128)(2,1)}, f32[2,64,2048]{2,1,0:T(8,128)}, f32[2,1,204...) custom-call(f32[3,256]{1,0:T(4,128)} %b_ref.1, ...), custom_call_target="tpu_custom_call" | custom-call | flops 18790481920 | bytes 27356160 | tf_op jit(solution)/shard_map/first/pallas_call | solution.py:1089
  137.3 120.9 %second.1 = (f32[3,256]{1,0:T(4,128)}, f32[1,1024]{1,0:T(1,128)}, f32[2,1024]{1,0:T(2,128)}, f32[2,1024]{1,0:T(2,128)}, f32[2,1024]{1,0:T(2,128)}, /*index=5*/bf...) custom-call(s32[3,2,512]{2,1,0:T(2,128)} %pos_ref.3, ...), custom_call_target="tpu_custom_call" | custom-call | flops 8589934592 | bytes 31566848 | tf_op jit(solution)/shard_map/second/pallas_call | solution.py:1089
  258.2 7.5 %finish.1 = (f32[3,256]{1,0:T(4,128)}, f32[1,1024]{1,0:T(1,128)}, f32[2,1024]{1,0:T(2,128)}, f32[2,1024]{1,0:T(2,128)}, f32[2,1024]{1,0:T(2,128)}, /*index=5*/f3...) custom-call(f32[3,256]{1,0:T(4,128)} %get-tuple-element.55.refs_0_, ...), custom_call_target="tpu_custom_call" | custom-call | tf_op jit(solution)/shard_map/finish/pallas_call | solution.py:1117
